TPU v7x, 512 devices: a whole 4x8x8 slice. The times are simulated.
512 devices in a mesh: chain: 64 (over x, z, core), rep: 8 (over y).
Axes of the slice: x: 4, y: 8, z: 8, core: 2. Of those that a mesh axis runs over, the one named last changes fastest.
Arguments:
- spins: bfloat16 [98304, 256], P('chain'), may hold values from -1 to 1, as said below
- energies: bfloat16 [98304], P('chain'), may hold values from -150 to -70
- counts: int32 [64], P('chain'), may hold values from 1 to 1536, 49152 in all
- accepted: int32 [64, 1536], P('chain'), may hold values from 0 to 1535, each once within a row
- hidden_bias: bfloat16 [4096], P('rep'), may hold values from -3 to 3
- weights: bfloat16 [256, 4096], P(None, 'rep'), may hold values from -0.375 to 0.375
Outputs:
- update_visible: float32 [256], P('rep')
- update_hidden: float32 [4096], P('rep')
- update_weights: float32 [256, 4096], P('chain', 'rep')
Inputs may be any that keep to these rules, and one draw needn't show every extreme that they name: `spins`: every entry is -1 or 1. The counts sum to 49152; at least one index of chain has 1536. Each row is a permutation of the slot numbers; its first counts entries name that index's accepted slots.
All inputs are finite; a program needn't handle non-finite values. No bound on the sum of `counts` on one device may be relied on, other than what follows from the above.
Results may differ from a plain program's by a relative error of at most 0.02.
Values may be sent and summed in bfloat16 or wider, within the bound.
No kernel may reach another device: no remote copies, remote signals or barrier semaphores. Data moves between devices by JAX's collectives and lax.ppermute only.
A program may use at most 64 MiB of HBM per device.

v0:
```python
import jax
import jax.numpy as jnp
from jax import lax
from jax.sharding import Mesh
from jax.sharding import PartitionSpec as P

N_SITES = 256
HIDDEN_SIZE = 4096
KEEP_DEV = 768
ITERS = 3
CHAIN = ("chain_0", "chain_1", "chain_2")
CHAIN_REP = ("chain_0", "chain_1", "chain_2", "rep")


PRECISE = lax.Precision.HIGHEST
DIAG_SHIFT = 0.05
EPSILON = 1e-06


def sent_to_all(array, axis):
    copies = jnp.broadcast_to(array, (lax.axis_size(axis), *array.shape))
    return lax.all_to_all(copies, axis, split_axis=0, concat_axis=0, tiled=True)


def of_everyone(array, axis):
    return sent_to_all(array, axis).sum(axis=0)


def in_blocks(array, dim, size):
    before, after = (array.shape[:dim], array.shape[dim + 1 :])
    return jnp.moveaxis(array.reshape(*before, size, -1, *after), dim, 0)


def sum_at_owner(array, axis, dim):
    blocks = in_blocks(array, dim, lax.axis_size(axis))
    arrived = lax.all_to_all(blocks, axis, split_axis=0, concat_axis=0, tiled=True)
    return arrived.astype(jnp.float32).sum(axis=0)


def in_one(arrays, axis):
    ends = [0]
    for a in arrays:
        ends.append(ends[-1] + a.size)
    so_far = of_everyone(jnp.concatenate([a.ravel() for a in arrays]), axis)
    return tuple((so_far[b:e].reshape(a.shape) for a, b, e in zip(arrays, ends, ends[1:])))


def laid_out(blocks, dim):
    blocks = jnp.moveaxis(blocks, 0, dim)
    lengths = blocks.shape
    return blocks.reshape(*lengths[:dim], lengths[dim] * lengths[dim + 1], *lengths[dim + 2 :])


def gathered_copies(array, axis, dim):
    blocks = sent_to_all(array, axis)
    return laid_out(blocks, dim)


def over_axes(array, axes):
    for axis in axes:
        array = lax.psum(array, axis)
    return array


def activations(sample_rows, hidden_bias, weights):
    preact = hidden_bias.astype(jnp.float32) + jnp.dot(
        sample_rows, weights, preferred_element_type=jnp.float32
    )
    return jnp.tanh(preact).astype(jnp.bfloat16)


def combine(base_vec, extra_vec, factor):
    return tuple((first + factor * second for first, second in zip(base_vec, extra_vec)))


def per_device(spins, energies, counts, accepted, hidden_bias, weights):
    chain_count = lax.axis_size(CHAIN)
    slot_count = spins.shape[0]
    site_count = spins.shape[1]
    visible_part = site_count // lax.axis_size("rep")
    own_count = counts[0]
    accepted_row = accepted[0]
    sample_total = KEEP_DEV * chain_count
    samples = spins[accepted_row]
    hidden_acts = activations(samples, hidden_bias, weights)
    live_rows = (jnp.arange(slot_count, dtype=jnp.int32) < own_count).astype(jnp.float32)
    energy = energies[accepted_row].astype(jnp.float32)
    visible = lax.dynamic_slice_in_dim(
        samples, lax.axis_index("rep") * visible_part, visible_part, 1
    )
    mean_energy = of_everyone(jnp.sum(energy * live_rows), CHAIN) / sample_total
    centered = (energy - mean_energy) * live_rows

    def pull(row_weight):
        weighted = hidden_acts.astype(jnp.float32) * row_weight[:, None]
        grad_hid = jnp.sum(weighted, axis=0)
        grad_vis = jnp.dot(
            row_weight, visible, precision=PRECISE, preferred_element_type=jnp.float32
        )
        grad_mat = sum_at_owner(
            jnp.einsum(
                "ri,rj->ij",
                samples,
                weighted,
                precision=PRECISE,
                preferred_element_type=jnp.float32,
            ).astype(jnp.bfloat16),
            CHAIN,
            0,
        )
        grad_vis, grad_hid = in_one((grad_vis, grad_hid), CHAIN)
        return (grad_vis / sample_total, grad_hid / sample_total, grad_mat / sample_total)

    def inner(pairs):
        collected = []
        leading = (lax.axis_index(CHAIN) == 0).astype(jnp.float32)
        for first_vec, second_vec in pairs:
            small_part = jnp.sum(first_vec[0] * second_vec[0]) + jnp.sum(
                first_vec[1] * second_vec[1]
            )
            collected.append(jnp.sum(first_vec[2] * second_vec[2]) + leading * small_part)
        return over_axes(jnp.stack(collected), CHAIN_REP)

    force = pull(centered)
    solution = tuple((jnp.zeros_like(member) for member in force))
    residual = force
    direction = force
    resid_sq = inner(((residual, residual),))[0]
    for iteration in range(ITERS):
        vis_part, hid_part, mat_part = direction
        mixture = jnp.dot(
            samples,
            gathered_copies(mat_part, CHAIN, 0),
            precision=PRECISE,
            preferred_element_type=jnp.float32,
        )
        row_values = jnp.sum(mixture * hidden_acts, axis=1)
        row_values = row_values + jnp.dot(
            hidden_acts, hid_part, precision=PRECISE, preferred_element_type=jnp.float32
        )
        row_values = row_values + jnp.dot(
            visible, vis_part, precision=PRECISE, preferred_element_type=jnp.float32
        )
        row_values = of_everyone(row_values, "rep")
        row_mean = of_everyone(jnp.sum(row_values * live_rows), CHAIN) / sample_total
        image = combine(pull((row_values - row_mean) * live_rows), direction, DIAG_SHIFT)
        products = inner(((direction, image), (residual, image), (image, image)))
        step_size = resid_sq / products[0]
        resid_next = resid_sq - 2.0 * step_size * products[1] + step_size * step_size * products[2]
        solution = combine(solution, direction, step_size)
        residual = combine(residual, image, -step_size)
        if iteration + 1 < ITERS:
            direction = combine(residual, direction, resid_next / resid_sq)
            resid_sq = resid_next
    norm_sq = inner(((solution, solution),))[0]
    param_total = N_SITES * HIDDEN_SIZE + HIDDEN_SIZE + N_SITES
    scale = lax.rsqrt(norm_sq / param_total + EPSILON)
    vis_out = solution[0] * scale
    hid_out = solution[1] * scale
    mat_out = solution[2] * scale
    return (vis_out, hid_out, mat_out)


def solution(mesh):
    split = Mesh(
        mesh.devices.reshape(4, 8, 2, mesh.shape["rep"]), ("chain_0", "chain_1", "chain_2", "rep")
    )
    in_specs = (P(CHAIN, None), P(CHAIN), P(CHAIN), P(CHAIN, None), P("rep"), P(None, "rep"))
    out_specs = (P("rep"), P("rep"), P(CHAIN, "rep"))
    return jax.shard_map(
        per_device, mesh=split, in_specs=in_specs, out_specs=out_specs, check_vma=False
    )
```

profile of v0, /device:TPU:2, one launch (start us, length us, event | category | flops | bytes accessed | tf_op | source)
XLA Modules:
  0.0 558.6 jit_solution(16267248121020614092)
XLA Ops:
  2.1 9.5 %gather_fusion = bf16[1536]{0:T(1024)(128)(2,1)S(1)} fusion(bf16[1536]{0:T(1024)(128)(2,1)S(1)} %copy-done.1, s32[2048]{0:T(1024)S(1)} %pad_clamp_fusion), kind=kCustom, calls=%fused_computation | custom fusion | bytes 12288 | tf_op jit(solution)/shard_map/gather | solution.py:87
  13.5 13.9 %all-to-all-start = ((f32[64,1,1]{2,1,0:T(1,128)}), f32[64,1,1]{2,1,0:T(1,128)S(1)}, u32[]{:S(2)}, u32[]{:S(2)}) async-start(f32[64,1,1]{2,1,0:T(1,128)} %broadcast_in_dim.49), calls=%async_computation | async-start | bytes 65536 | tf_op jit(solution)/shard_map/all_to_all | solution.py:22
  27.4 4.8 gather_fusion.1
  32.1 3.8 all-to-all-done
  37.3 1.6 fusion.1
  38.9 2.0 fusion.20
  41.6 6.6 %all-to-all-start.2 = ((bf16[64,4,512]{2,1,0:T(4,128)(2,1)}), bf16[64,4,512]{2,1,0:T(4,128)(2,1)S(1)}, u32[]{:S(2)}, u32[]{:S(2)}) async-start(bf16[64,4,512]{2,1,0:T(4,128)(2,1)} %reshape.124), calls=%async_computation.2 | async-start | bytes 524288 | tf_op jit(solution)/shard_map/all_to_all | solution.py:36
  48.7 11.0 %all-to-all-done.2 = bf16[64,4,512]{2,1,0:T(4,128)(2,1)S(1)} async-done(((bf16[64,4,512]{2,1,0:T(4,128)(2,1)}), bf16[64,4,512]{2,1,0:T(4,128)(2,1)S(1)}, u32[]{:S(2)}, u32[]{:S(2)}) %all-to-all-start.2) | async-done | bytes 262176 | tf_op jit(solution)/shard_map/all_to_all | solution.py:36
  60.4 6.6 %all-to-all-start.1 = ((f32[64,1,544]{2,1,0:T(1,128)}), f32[64,1,544]{2,1,0:T(1,128)}, u32[]{:S(2)}, u32[]{:S(2)}) async-start(f32[64,1,544]{2,1,0:T(1,128)} %broadcast_in_dim.50), calls=%async_computation.1 | async-start | bytes 327680 | tf_op jit(solution)/shard_map/all_to_all | solution.py:22
  67.2 9.6 %all-to-all-done.1 = f32[64,1,544]{2,1,0:T(1,128)} async-done(((f32[64,1,544]{2,1,0:T(1,128)}), f32[64,1,544]{2,1,0:T(1,128)}, u32[]{:S(2)}, u32[]{:S(2)}) %all-to-all-start.1) | async-done | bytes 139296 | tf_op jit(solution)/shard_map/all_to_all | solution.py:22
  77.7 6.3 %all-to-all-start.3 = ((f32[64,4,512]{2,1,0:T(4,128)}), f32[64,4,512]{2,1,0:T(4,128)}, u32[]{:S(2)}, u32[]{:S(2)}) async-start(f32[64,4,512]{2,1,0:T(4,128)} %broadcast_in_dim.51), calls=%async_computation.3 | async-start | bytes 1048576 | tf_op jit(solution)/shard_map/all_to_all | solution.py:22
  85.6 1.3 convolution_reduce_fusion.5
  87.0 13.6 %all-to-all-done.3 = f32[64,4,512]{2,1,0:T(4,128)} async-done(((f32[64,4,512]{2,1,0:T(4,128)}), f32[64,4,512]{2,1,0:T(4,128)}, u32[]{:S(2)}, u32[]{:S(2)}) %all-to-all-start.3) | async-done | bytes 524320 | tf_op jit(solution)/shard_map/all_to_all | solution.py:22
  100.6 2.0 reshape.125
  102.6 2.7 fusion.14
  105.3 15.1 %all_to_all.101 = f32[8,1,1536]{2,1,0:T(1,128)S(1)} all-to-all(f32[8,1,1536]{2,1,0:T(1,128)S(1)} %broadcast_in_dim.52), channel_id=1, replica_groups=mesh['chain_0'=4,'chain_1'=8,'chain_2'=2,'rep'=8] {'rep'}, dimensions={0} | all-to-all | bytes 98304 | tf_op jit(solution)/shard_map/all_to_all | solution.py:22
  121.8 15.5 %all_to_all.102 = f32[64,1,1]{2,1,0:T(1,128)S(1)} all-to-all(f32[64,1,1]{2,1,0:T(1,128)S(1)} %broadcast_in_dim.53), channel_id=1, replica_groups=mesh['chain_0'=4,'chain_1'=8,'chain_2'=2,'rep'=8] {'chain_0','chain_1','..., dimensions={0} | all-to-all | bytes 512 | tf_op jit(solution)/shard_map/all_to_all | solution.py:22
  140.2 5.5 all-to-all-start.7
  145.7 2.7 fusion.19
  148.4 1.7 reshape.126
  150.1 5.4 all-to-all-done.7
  156.2 6.1 %all-to-all-start.6 = ((bf16[64,4,512]{2,1,0:T(4,128)(2,1)}), bf16[64,4,512]{2,1,0:T(4,128)(2,1)S(1)}, u32[]{:S(2)}, u32[]{:S(2)}) async-start(bf16[64,4,512]{2,1,0:T(4,128)(2,1)} %reshape.126), calls=%async_computation.6 | async-start | bytes 524288 | tf_op jit(solution)/shard_map/all_to_all | solution.py:36
  168.6 5.2 all-to-all-done.6
  176.8 9.8 %all-reduce.2 = (f32[1]{0:T(128)}, f32[3]{0:T(128)S(1)}) all-reduce(f32[1]{0:T(128)} %bitcast.3, f32[3]{0:T(128)S(1)} %pad_maximum_fusion.4), channel_id=1, replica_groups=mesh['chain_0'=4,'chain_1'=8,'chain_2'=2,'rep'=8] {'chain_0'}, use_global_device_ids=true, to_apply=%region_8.0 | all-reduce | flops 4 | bytes 32 | tf_op jit(solution)/shard_map/psum | solution.py:61
  186.6 16.0 %all-reduce.1 = (f32[1]{0:T(128)}, f32[3]{0:T(128)S(1)}) all-reduce(f32[1]{0:T(128)} %get-tuple-element.34, f32[3]{0:T(128)S(1)} %get-tuple-element.35), channel_id=1, replica_groups=mesh['chain_0'=4,'chain_1'=8,'chain_2'=2,'rep'=8] {'chain_1'}, use_global_device_ids=true, to_apply=%region_9.0 | all-reduce | flops 4 | bytes 32 | tf_op jit(solution)/shard_map/psum | solution.py:61
  202.6 3.1 all-reduce.3
  205.6 15.3 %all-reduce = (f32[]{:T(128)}, f32[3]{0:T(128)S(1)}) all-reduce(f32[]{:T(128)} %bitcast.4, f32[3]{0:T(128)S(1)} %get-tuple-element.37), channel_id=1, replica_groups=mesh['chain_0'=4,'chain_1'=8,'chain_2'=2,'rep'=8] {'rep'}, use_global_device_ids=true, to_apply=%region_11.0 | all-reduce | flops 4 | bytes 32 | tf_op jit(solution)/shard_map/psum | solution.py:61
  226.5 7.4 %all-to-all-start.8 = ((f32[64,4,512]{2,1,0:T(4,128)}), f32[64,4,512]{2,1,0:T(4,128)}, u32[]{:S(2)}, u32[]{:S(2)}) async-start(f32[64,4,512]{2,1,0:T(4,128)} %broadcast_in_dim.55), calls=%async_computation.8 | async-start | bytes 1048576 | tf_op jit(solution)/shard_map/all_to_all | solution.py:22
  234.5 1.3 convolution_reduce_fusion.4
  235.8 14.6 %all-to-all-done.8 = f32[64,4,512]{2,1,0:T(4,128)} async-done(((f32[64,4,512]{2,1,0:T(4,128)}), f32[64,4,512]{2,1,0:T(4,128)}, u32[]{:S(2)}, u32[]{:S(2)}) %all-to-all-start.8) | async-done | bytes 524320 | tf_op jit(solution)/shard_map/all_to_all | solution.py:22
  250.4 2.0 reshape.127
  252.5 2.7 fusion.15
  255.2 11.9 %all_to_all.103 = f32[8,1,1536]{2,1,0:T(1,128)S(1)} all-to-all(f32[8,1,1536]{2,1,0:T(1,128)S(1)} %broadcast_in_dim.56), channel_id=1, replica_groups=mesh['chain_0'=4,'chain_1'=8,'chain_2'=2,'rep'=8] {'rep'}, dimensions={0} | all-to-all | bytes 98304 | tf_op jit(solution)/shard_map/all_to_all | solution.py:22
  268.4 15.6 %all_to_all.104 = f32[64,1,1]{2,1,0:T(1,128)S(1)} all-to-all(f32[64,1,1]{2,1,0:T(1,128)S(1)} %broadcast_in_dim.57), channel_id=1, replica_groups=mesh['chain_0'=4,'chain_1'=8,'chain_2'=2,'rep'=8] {'chain_0','chain_1','..., dimensions={0} | all-to-all | bytes 512 | tf_op jit(solution)/shard_map/all_to_all | solution.py:22
  286.9 5.5 all-to-all-start.12
  292.4 2.7 fusion.18
  295.1 1.7 reshape.128
  296.8 5.4 all-to-all-done.12
  302.9 6.1 %all-to-all-start.11 = ((bf16[64,4,512]{2,1,0:T(4,128)(2,1)}), bf16[64,4,512]{2,1,0:T(4,128)(2,1)S(1)}, u32[]{:S(2)}, u32[]{:S(2)}) async-start(bf16[64,4,512]{2,1,0:T(4,128)(2,1)} %reshape.128), calls=%async_computation.11 | async-start | bytes 524288 | tf_op jit(solution)/shard_map/all_to_all | solution.py:36
  315.3 5.3 all-to-all-done.11
  323.5 8.7 %psum.148 = f32[3]{0:T(128)S(1)} all-reduce(f32[3]{0:T(128)S(1)} %pad_maximum_fusion.5), channel_id=1, replica_groups=mesh['chain_0'=4,'chain_1'=8,'chain_2'=2,'rep'=8] {'chain_0'}, use_global_device_ids=true, to_apply=%region_45.0 | all-reduce | flops 3 | bytes 24 | tf_op jit(solution)/shard_map/psum | solution.py:61
  332.1 15.4 %psum.149 = f32[3]{0:T(128)S(1)} all-reduce(f32[3]{0:T(128)S(1)} %psum.148), channel_id=1, replica_groups=mesh['chain_0'=4,'chain_1'=8,'chain_2'=2,'rep'=8] {'chain_1'}, use_global_device_ids=true, to_apply=%region_46.0 | all-reduce | flops 3 | bytes 24 | tf_op jit(solution)/shard_map/psum | solution.py:61
  347.5 2.5 psum.150
  350.0 14.7 %psum.151 = f32[3]{0:T(128)S(1)} all-reduce(f32[3]{0:T(128)S(1)} %psum.150), channel_id=1, replica_groups=mesh['chain_0'=4,'chain_1'=8,'chain_2'=2,'rep'=8] {'rep'}, use_global_device_ids=true, to_apply=%region_48.0 | all-reduce | flops 3 | bytes 24 | tf_op jit(solution)/shard_map/psum | solution.py:61
  368.3 7.4 %all-to-all-start.13 = ((f32[64,4,512]{2,1,0:T(4,128)}), f32[64,4,512]{2,1,0:T(4,128)}, u32[]{:S(2)}, u32[]{:S(2)}) async-start(f32[64,4,512]{2,1,0:T(4,128)} %broadcast_in_dim.59), calls=%async_computation.13 | async-start | bytes 1048576 | tf_op jit(solution)/shard_map/all_to_all | solution.py:22
  377.6 14.6 %all-to-all-done.13 = f32[64,4,512]{2,1,0:T(4,128)} async-done(((f32[64,4,512]{2,1,0:T(4,128)}), f32[64,4,512]{2,1,0:T(4,128)}, u32[]{:S(2)}, u32[]{:S(2)}) %all-to-all-start.13) | async-done | bytes 524320 | tf_op jit(solution)/shard_map/all_to_all | solution.py:22
  392.3 2.0 reshape.129
  394.3 2.7 fusion.16
  397.0 11.9 %all_to_all.105 = f32[8,1,1536]{2,1,0:T(1,128)S(1)} all-to-all(f32[8,1,1536]{2,1,0:T(1,128)S(1)} %broadcast_in_dim.60), channel_id=1, replica_groups=mesh['chain_0'=4,'chain_1'=8,'chain_2'=2,'rep'=8] {'rep'}, dimensions={0} | all-to-all | bytes 98304 | tf_op jit(solution)/shard_map/all_to_all | solution.py:22
  410.2 15.3 %all_to_all.106 = f32[64,1,1]{2,1,0:T(1,128)S(1)} all-to-all(f32[64,1,1]{2,1,0:T(1,128)S(1)} %broadcast_in_dim.61), channel_id=1, replica_groups=mesh['chain_0'=4,'chain_1'=8,'chain_2'=2,'rep'=8] {'chain_0','chain_1','..., dimensions={0} | all-to-all | bytes 512 | tf_op jit(solution)/shard_map/all_to_all | solution.py:22
  428.5 5.8 %all-to-all-start.17 = ((f32[64,1,544]{2,1,0:T(1,128)}), f32[64,1,544]{2,1,0:T(1,128)S(1)}, u32[]{:S(2)}, u32[]{:S(2)}) async-start(f32[64,1,544]{2,1,0:T(1,128)} %broadcast_in_dim.62), calls=%async_computation.17 | async-start | bytes 327680 | tf_op jit(solution)/shard_map/all_to_all | solution.py:22
  434.3 2.7 fusion.17
  436.9 1.7 reshape.130
  438.7 5.4 all-to-all-done.17
  444.1 6.1 %all-to-all-start.16 = ((bf16[64,4,512]{2,1,0:T(4,128)(2,1)}), bf16[64,4,512]{2,1,0:T(4,128)(2,1)S(1)}, u32[]{:S(2)}, u32[]{:S(2)}) async-start(bf16[64,4,512]{2,1,0:T(4,128)(2,1)} %reshape.130), calls=%async_computation.16 | async-start | bytes 524288 | tf_op jit(solution)/shard_map/all_to_all | solution.py:36
  455.4 6.3 %all-to-all-done.16 = bf16[64,4,512]{2,1,0:T(4,128)(2,1)S(1)} async-done(((bf16[64,4,512]{2,1,0:T(4,128)(2,1)}), bf16[64,4,512]{2,1,0:T(4,128)(2,1)S(1)}, u32[]{:S(2)}, u32[]{:S(2)}) %all-to-all-start.16) | async-done | bytes 262176 | tf_op jit(solution)/shard_map/all_to_all | solution.py:36
  464.5 8.7 %psum.152 = f32[3]{0:T(128)S(1)} all-reduce(f32[3]{0:T(128)S(1)} %pad_maximum_fusion.6), channel_id=1, replica_groups=mesh['chain_0'=4,'chain_1'=8,'chain_2'=2,'rep'=8] {'chain_0'}, use_global_device_ids=true, to_apply=%region_65.0 | all-reduce | flops 3 | bytes 24 | tf_op jit(solution)/shard_map/psum | solution.py:61
  473.2 15.4 %psum.153 = f32[3]{0:T(128)S(1)} all-reduce(f32[3]{0:T(128)S(1)} %psum.152), channel_id=1, replica_groups=mesh['chain_0'=4,'chain_1'=8,'chain_2'=2,'rep'=8] {'chain_1'}, use_global_device_ids=true, to_apply=%region_66.0 | all-reduce | flops 3 | bytes 24 | tf_op jit(solution)/shard_map/psum | solution.py:61
  488.6 2.5 psum.154
  491.0 14.7 %psum.155 = f32[3]{0:T(128)S(1)} all-reduce(f32[3]{0:T(128)S(1)} %psum.154), channel_id=1, replica_groups=mesh['chain_0'=4,'chain_1'=8,'chain_2'=2,'rep'=8] {'rep'}, use_global_device_ids=true, to_apply=%region_68.0 | all-reduce | flops 3 | bytes 24 | tf_op jit(solution)/shard_map/psum | solution.py:61
  509.6 10.9 %psum.156 = f32[1]{0:T(128)} all-reduce(f32[1]{0:T(128)} %bitcast.29), channel_id=1, replica_groups=mesh['chain_0'=4,'chain_1'=8,'chain_2'=2,'rep'=8] {'chain_0'}, use_global_device_ids=true, to_apply=%region_72.0 | all-reduce | flops 1 | bytes 8 | tf_op jit(solution)/shard_map/psum | solution.py:61
  520.5 16.0 %psum.157 = f32[1]{0:T(128)} all-reduce(f32[1]{0:T(128)} %psum.156), channel_id=1, replica_groups=mesh['chain_0'=4,'chain_1'=8,'chain_2'=2,'rep'=8] {'chain_1'}, use_global_device_ids=true, to_apply=%region_73.0 | all-reduce | flops 1 | bytes 8 | tf_op jit(solution)/shard_map/psum | solution.py:61
  536.5 3.1 psum.158
  539.6 16.2 %psum.159 = f32[1]{0:T(128)} all-reduce(f32[1]{0:T(128)} %psum.158), channel_id=1, replica_groups=mesh['chain_0'=4,'chain_1'=8,'chain_2'=2,'rep'=8] {'rep'}, use_global_device_ids=true, to_apply=%region_75.0 | all-reduce | flops 1 | bytes 8 | tf_op jit(solution)/shard_map/psum | solution.py:61
  (101 shorter events, 38.5 us)
Async XLA Ops:
  0.6 26.7 %copy-start = (bf16[1536,256]{1,0:T(8,128)(2,1)S(1)}, bf16[1536,256]{1,0:T(8,128)(2,1)}, u32[]{:S(2)}) copy-start(bf16[1536,256]{1,0:T(8,128)(2,1)} %param.6) | copy-start | bytes 2359300
  0.6 1.5 copy-start.1
  13.5 22.5 %all-to-all-start = ((f32[64,1,1]{2,1,0:T(1,128)}), f32[64,1,1]{2,1,0:T(1,128)S(1)}, u32[]{:S(2)}, u32[]{:S(2)}) async-start(f32[64,1,1]{2,1,0:T(1,128)} %broadcast_in_dim.49), calls=%async_computation | async-start | bytes 65536 | tf_op jit(solution)/shard_map/all_to_all | solution.py:22
  27.3 4.8 copy-start.4
  41.6 18.1 %all-to-all-start.2 = ((bf16[64,4,512]{2,1,0:T(4,128)(2,1)}), bf16[64,4,512]{2,1,0:T(4,128)(2,1)S(1)}, u32[]{:S(2)}, u32[]{:S(2)}) async-start(bf16[64,4,512]{2,1,0:T(4,128)(2,1)} %reshape.124), calls=%async_computation.2 | async-start | bytes 524288 | tf_op jit(solution)/shard_map/all_to_all | solution.py:36
  60.4 16.4 %all-to-all-start.1 = ((f32[64,1,544]{2,1,0:T(1,128)}), f32[64,1,544]{2,1,0:T(1,128)}, u32[]{:S(2)}, u32[]{:S(2)}) async-start(f32[64,1,544]{2,1,0:T(1,128)} %broadcast_in_dim.50), calls=%async_computation.1 | async-start | bytes 327680 | tf_op jit(solution)/shard_map/all_to_all | solution.py:22
  77.7 22.9 %all-to-all-start.3 = ((f32[64,4,512]{2,1,0:T(4,128)}), f32[64,4,512]{2,1,0:T(4,128)}, u32[]{:S(2)}, u32[]{:S(2)}) async-start(f32[64,4,512]{2,1,0:T(4,128)} %broadcast_in_dim.51), calls=%async_computation.3 | async-start | bytes 1048576 | tf_op jit(solution)/shard_map/all_to_all | solution.py:22
  140.2 15.3 %all-to-all-start.7 = ((f32[64,1,544]{2,1,0:T(1,128)}), f32[64,1,544]{2,1,0:T(1,128)S(1)}, u32[]{:S(2)}, u32[]{:S(2)}) async-start(f32[64,1,544]{2,1,0:T(1,128)} %broadcast_in_dim.54), calls=%async_computation.7 | async-start | bytes 327680 | tf_op jit(solution)/shard_map/all_to_all | solution.py:22
  155.5 0.7 copy-start.2
  156.2 17.7 %all-to-all-start.6 = ((bf16[64,4,512]{2,1,0:T(4,128)(2,1)}), bf16[64,4,512]{2,1,0:T(4,128)(2,1)S(1)}, u32[]{:S(2)}, u32[]{:S(2)}) async-start(bf16[64,4,512]{2,1,0:T(4,128)(2,1)} %reshape.126), calls=%async_computation.6 | async-start | bytes 524288 | tf_op jit(solution)/shard_map/all_to_all | solution.py:36
  226.5 24.0 %all-to-all-start.8 = ((f32[64,4,512]{2,1,0:T(4,128)}), f32[64,4,512]{2,1,0:T(4,128)}, u32[]{:S(2)}, u32[]{:S(2)}) async-start(f32[64,4,512]{2,1,0:T(4,128)} %broadcast_in_dim.55), calls=%async_computation.8 | async-start | bytes 1048576 | tf_op jit(solution)/shard_map/all_to_all | solution.py:22
  286.9 15.3 %all-to-all-start.12 = ((f32[64,1,544]{2,1,0:T(1,128)}), f32[64,1,544]{2,1,0:T(1,128)S(1)}, u32[]{:S(2)}, u32[]{:S(2)}) async-start(f32[64,1,544]{2,1,0:T(1,128)} %broadcast_in_dim.58), calls=%async_computation.12 | async-start | bytes 327680 | tf_op jit(solution)/shard_map/all_to_all | solution.py:22
  302.2 0.7 copy-start.3
  302.9 17.7 %all-to-all-start.11 = ((bf16[64,4,512]{2,1,0:T(4,128)(2,1)}), bf16[64,4,512]{2,1,0:T(4,128)(2,1)S(1)}, u32[]{:S(2)}, u32[]{:S(2)}) async-start(bf16[64,4,512]{2,1,0:T(4,128)(2,1)} %reshape.128), calls=%async_computation.11 | async-start | bytes 524288 | tf_op jit(solution)/shard_map/all_to_all | solution.py:36
  368.3 24.0 %all-to-all-start.13 = ((f32[64,4,512]{2,1,0:T(4,128)}), f32[64,4,512]{2,1,0:T(4,128)}, u32[]{:S(2)}, u32[]{:S(2)}) async-start(f32[64,4,512]{2,1,0:T(4,128)} %broadcast_in_dim.59), calls=%async_computation.13 | async-start | bytes 1048576 | tf_op jit(solution)/shard_map/all_to_all | solution.py:22
  428.5 15.6 %all-to-all-start.17 = ((f32[64,1,544]{2,1,0:T(1,128)}), f32[64,1,544]{2,1,0:T(1,128)S(1)}, u32[]{:S(2)}, u32[]{:S(2)}) async-start(f32[64,1,544]{2,1,0:T(1,128)} %broadcast_in_dim.62), calls=%async_computation.17 | async-start | bytes 327680 | tf_op jit(solution)/shard_map/all_to_all | solution.py:22
  444.1 17.7 %all-to-all-start.16 = ((bf16[64,4,512]{2,1,0:T(4,128)(2,1)}), bf16[64,4,512]{2,1,0:T(4,128)(2,1)S(1)}, u32[]{:S(2)}, u32[]{:S(2)}) async-start(bf16[64,4,512]{2,1,0:T(4,128)(2,1)} %reshape.130), calls=%async_computation.16 | async-start | bytes 524288 | tf_op jit(solution)/shard_map/all_to_all | solution.py:36
where the time goes:
time: 569 us; the launch traced here: 559 us
  blocking collectives  258 us (45%)
  waiting for transfers between devices  100 us (18%)
  starting transfers between devices  83.3 us (15%)
  local copies, waits for them, and re-layouts  37.9 us (7%)
  between operations  30.8 us (5%)
  matrix products  26.6 us (5%)
  other arithmetic  21.7 us (4%)
    psum x16, blocking collectives, over_axes(): array = lax.psum(array, axis)  173 us
    all_to_all x6, blocking collectives, sent_to_all(): return lax.all_to_all(copies, axis, split_axis=0, concat_axis=0, tiled=True)  85.3 us
    all_to_all x8, waiting for transfers between devices, sent_to_all(): return lax.all_to_all(copies, axis, split_axis=0, concat_axis=0, tiled=True)  72.5 us
    all_to_all x8, starting transfers between devices, sent_to_all(): return lax.all_to_all(copies, axis, split_axis=0, concat_axis=0, tiled=True)  58.4 us
    all_to_all x4, waiting for transfers between devices, sum_at_owner(): lax.all_to_all(blocks, axis, split_axis=0, concat_axis=0, tiled=True)  27.8 us
    all_to_all x4, starting transfers between devices, sum_at_owner(): lax.all_to_all(blocks, axis, split_axis=0, concat_axis=0, tiled=True)  24.9 us
  transfers between devices with their start and end apart: 12, of which 12 were waited for; matrix products, arithmetic and copies ran while one was open for 6% of the time, Pallas kernels for 0%

commit v1 on v0

v1 whole, which is shorter than its diff:
```python
import jax
import jax.numpy as jnp
from jax import lax
from jax.experimental import pallas as pl
from jax.experimental.pallas import tpu as pltpu
from jax.sharding import Mesh
from jax.sharding import PartitionSpec as P

KEEP_DEV = 768
SHIFT = 0.05
EPSILON = 1e-06
ENERGY_MID = -110.0
CHAIN = ("chain_0", "chain_1", "chain_2")
F32 = jnp.float32
BF16 = jnp.bfloat16
HIGH = lax.Precision.HIGHEST

SITES = 256
HIDDEN = 512
OWNERS = 64
ROWS = 4
TAIL = 128
WIDE = HIDDEN + TAIL
SLOTS = 1536
TOTAL = float(KEEP_DEV * OWNERS)
SCALARS = 8


def iota(shape, dim):
    return lax.broadcasted_iota(jnp.int32, shape, dim)


def dot(a, b, dims=((1,), (0,)), precision=None):
    return lax.dot_general(a, b, (dims, ((), ())), precision=precision, preferred_element_type=F32)


def by_lanes(a, b):
    return dot(a, b, ((1,), (1,)))


def eye(n):
    return jnp.where(iota((n, n), 0) == iota((n, n), 1), 1.0, 0.0).astype(BF16)


def two(x):
    high = x.astype(BF16)
    return high, (x - high.astype(F32)).astype(BF16)


def total(x):
    return jnp.sum(x, keepdims=True)


def scalar_lanes(scalars):
    lane = iota((1, TAIL), 1)
    out = jnp.zeros((1, TAIL), F32)
    for i, value in enumerate(scalars):
        one = value.astype(BF16).astype(F32)
        second = (value - one).astype(BF16).astype(F32)
        third = value - one - second
        for k, piece in enumerate((one, second, third)):
            out = jnp.where(lane == 32 + 3 * i + k, piece, out)
    return out


def own_hidden(shape):
    row, col = iota(shape, 0), iota(shape, 1)
    return row == ROWS * (col >> 3)


def pull(weights, st, tt):
    high, low = two(weights)
    spins = st.astype(F32)
    grad = by_lanes((spins * high.astype(F32)).astype(BF16), tt)
    grad = grad + by_lanes((spins * low.astype(F32)).astype(BF16), tt)
    sub = iota((16, SLOTS), 0)
    pair = jnp.where(sub == 0, high.astype(F32), jnp.where(sub == 1, low.astype(F32), 0.0)).astype(BF16)
    both = by_lanes(pair, tt)
    return grad, both[0:1, :] + both[1:2, :]


def tail_of(grad, hidden, scalars):
    visible = grad[:, HIDDEN : HIDDEN + 1]
    v_high = visible.astype(BF16).astype(F32)
    lane, row = iota((SITES, TAIL), 1), iota((SITES, TAIL), 0)
    tail = jnp.where(lane == 0, v_high, jnp.where(lane == 1, visible - v_high, 0.0))
    h_high, h_low = two(hidden[:, :HIDDEN])
    mine = own_hidden((SITES, HIDDEN))
    j, l = iota((HIDDEN, TAIL), 0) & 7, iota((HIDDEN, TAIL), 1)
    for piece, base in ((h_high, 8), (h_low, 16)):
        spread = jnp.where(mine, piece.astype(F32), 0.0).astype(BF16)
        tail = tail + dot(spread, jnp.where(l == base + j, 1.0, 0.0).astype(BF16))
    return tail + jnp.where((row & 3) == 1, scalar_lanes(scalars), 0.0)


def store_rows(out_ref, first, grad, tail):
    for c in range(OWNERS):
        rows = slice(ROWS * c, ROWS * (c + 1))
        out_ref[c, first : first + ROWS, 0:HIDDEN] = grad[rows, 0:HIDDEN].astype(BF16)
        out_ref[c, first : first + ROWS, HIDDEN:WIDE] = tail[rows, :].astype(BF16)


def combined(tail):
    a, b = iota((TAIL, TAIL), 0), iota((TAIL, TAIL), 1)
    take = (b == 0) & (a < 2)
    take = take | ((b >= 8) & (b < 16) & ((a == b) | (a == b + 8)))
    first = 32 + 3 * (b - 64)
    take = take | ((b >= 64) & (b < 64 + SCALARS) & (a >= first) & (a < first + 3))
    return dot(tail, jnp.where(take, 1.0, 0.0).astype(F32), precision=HIGH)


def store_copies(out_ref, rows):
    lane = iota((ROWS, TAIL), 1)
    tail = rows[:, HIDDEN:WIDE]
    tail = jnp.where(lane == 0, tail * 0.125, jnp.where((lane >= 8) & (lane < 16), tail, 0.0))
    high = tail.astype(BF16).astype(F32)
    a, b = iota((TAIL, TAIL), 0), iota((TAIL, TAIL), 1)
    move = ((a == 0) & (b == 1)) | ((a >= 8) & (a < 16) & (b == a + 8))
    low = dot(tail - high, jnp.where(move, 1.0, 0.0).astype(F32), precision=HIGH)
    packed = (high + low).astype(BF16)
    coupling = rows[:, 0:HIDDEN].astype(BF16)
    for c in range(OWNERS):
        out_ref[c, :, 0:HIDDEN] = coupling
        out_ref[c, :, HIDDEN:WIDE] = packed


def setup_kernel(count_ref, spins_ref, energy_ref, accepted_ref, weights_ref, bias_ref, st_ref, tt_ref, vec_ref, out_ref):
    accepted = accepted_ref[...]
    live = iota((16, SLOTS), 1) < count_ref[0]
    major = jnp.where((iota((16, SLOTS), 0) == (accepted >> 7)) & live, 1.0, 0.0).astype(BF16)
    minor = jnp.where(iota((TAIL, SLOTS), 0) == (accepted & 127), 1.0, 0.0).astype(BF16)
    table = by_lanes(major, minor)
    mask = jnp.concatenate([table[h : h + 1, :] for h in range(SLOTS // TAIL)], axis=1)
    spins = spins_ref[...]
    st_ref[...] = by_lanes(eye(SITES), spins).astype(BF16)
    turned = by_lanes(eye(HIDDEN), weights_ref[...]).astype(BF16)
    bias = by_lanes(eye(HIDDEN), jnp.broadcast_to(bias_ref[...].astype(F32), (16, HIDDEN)).astype(BF16))
    preact = bias[:, 0:1] + dot(turned, st_ref[...])
    tt_ref[0:HIDDEN, :] = jnp.tanh(preact).astype(BF16)
    sub = iota((TAIL, SLOTS), 0)
    tt_ref[HIDDEN:WIDE, :] = jnp.where(sub < 2, 1.0, 0.0).astype(BF16)
    energy = (energy_ref[...].astype(F32) - ENERGY_MID) * mask
    vec_ref[0:1, :] = mask
    vec_ref[1:2, :] = energy
    vec_ref[2:8, :] = jnp.zeros((6, SLOTS), F32)
    st, tt = st_ref[...], tt_ref[...]
    for first, row, scalars in ((0, energy, (total(energy),)), (ROWS, mask, ())):
        grad, hidden = pull(row, st, tt)
        store_rows(out_ref, first, grad, tail_of(grad, hidden, scalars))


def arrived(in_ref, first):
    rows = slice(first, first + ROWS)
    acc = [in_ref[c, rows, :].astype(F32) for c in range(4)]
    for c in range(4, OWNERS):
        acc[c % 4] = acc[c % 4] + in_ref[c, rows, :].astype(F32)
    acc = (acc[0] + acc[1]) + (acc[2] + acc[3])
    tail = combined(acc[:, HIDDEN:WIDE])
    scalars = [tail[1:2, 64 + i : 65 + i] for i in range(SCALARS)]
    return acc[:, 0:HIDDEN], tail, scalars


def lanes_of(values):
    lane = iota((8, TAIL), 1)
    out = jnp.zeros((8, TAIL), F32)
    for i, value in enumerate(values):
        out = jnp.where(lane == i, value, out)
    return out


def first_own_kernel(in_ref, vec_ref, res_ref, ones_ref, vec_out_ref, copies_ref):
    energy, energy_tail, scalars = arrived(in_ref, 0)
    ones, ones_tail, _ = arrived(in_ref, ROWS)
    mean = scalars[0] / TOTAL
    res_ref[:, 0:HIDDEN] = energy - mean * ones
    res_ref[:, HIDDEN:WIDE] = energy_tail - mean * ones_tail
    ones_ref[:, 0:HIDDEN] = ones
    ones_ref[:, HIDDEN:WIDE] = ones_tail
    mask, raw = vec_ref[0:1, :], vec_ref[1:2, :]
    vec_out_ref[0:1, :] = mask
    vec_out_ref[1:2, :] = raw - mean * mask
    vec_out_ref[2:8, :] = jnp.zeros((6, SLOTS), F32)
    store_copies(copies_ref, res_ref[...])


def push_kernel(in_ref, st_ref, tt_ref, parts_ref, bias_ref, rows_ref):
    for c in range(OWNERS):
        rows_ref[ROWS * c : ROWS * (c + 1), :] = in_ref[c].astype(F32)
    tail = rows_ref[:, HIDDEN:WIDE].astype(BF16)
    mine = own_hidden((SITES, HIDDEN))
    l, j = iota((TAIL, HIDDEN), 0), iota((TAIL, HIDDEN), 1) & 7
    spread = dot(tail, jnp.where((l == 8 + j) | (l == 16 + j), 1.0, 0.0).astype(BF16))
    hidden = jnp.sum(jnp.where(mine, spread, 0.0), axis=0, keepdims=True)
    pick = jnp.where((iota((16, TAIL), 0) == 0) & (iota((16, TAIL), 1) < 2), 8.0, 0.0).astype(BF16)
    visible = by_lanes(pick, tail)
    bias_ref[...] = jnp.zeros((8, HIDDEN), F32)
    bias_ref[0:1, :] = hidden
    bias_ref[1:2, 0:SITES] = visible[0:1, :]
    h_high, h_low = two(hidden)
    sub = iota((16, HIDDEN), 0)
    pair = jnp.where(sub == 0, h_high.astype(F32), jnp.where(sub == 1, h_low.astype(F32), 0.0)).astype(BF16)
    tt = tt_ref[...]
    side = dot(pair, tt[0:HIDDEN, :])
    turned = jnp.transpose(rows_ref[...]).astype(BF16)
    mixture = dot(turned, st_ref[...])
    values = jnp.sum(mixture * tt.astype(F32), axis=0, keepdims=True)
    values = (values + side[0:1, :] + side[1:2, :]) * (1.0 / TOTAL)
    for y in range(parts_ref.shape[0]):
        parts_ref[y] = values


def row_sum(parts_ref, mask):
    values = parts_ref[0]
    for y in range(1, parts_ref.shape[0]):
        values = values + parts_ref[y]
    return values * mask


def iteration_scalars(vec_ref, values):
    res, before, o_before, start = (vec_ref[i : i + 1, :] for i in (1, 2, 3, 4))
    return (
        total(res * values),
        total(values * values),
        total(values),
        total(values * o_before),
        total(values * before),
        total(res * o_before),
        total(values * start),
    )


def pull_kernel(parts_ref, vec_ref, st_ref, tt_ref, vec_out_ref, out_ref):
    values = row_sum(parts_ref, vec_ref[0:1, :])
    vec_out_ref[...] = vec_ref[...]
    vec_out_ref[5:6, :] = values
    grad, hidden = pull(values, st_ref[...], tt_ref[...])
    store_rows(out_ref, 0, grad, tail_of(grad, hidden, iteration_scalars(vec_ref, values)))


def conjugate(scalars, past):
    r_zr, zr_zr, zr_sum, zr_zd, zr_d, r_zd, zr_start = scalars[:7]
    if past is None:
        beta, zd_sum, zd_zd, zd_d = None, zr_sum, zr_zr, r_zr
    else:
        rr, sum_before, zz_before, zd_before = past
        beta = r_zr / rr
        zd_sum = zr_sum + beta * sum_before
        zd_zd = zr_zr + 2.0 * beta * zr_zd + beta * beta * zz_before
        zd_d = r_zr + beta * (zr_d + r_zd) + beta * beta * zd_before
    step = r_zr / (zd_zd - zd_sum * zd_sum / TOTAL + SHIFT * zd_d)
    return beta, step, (r_zr, zd_sum, zd_zd, zd_d)


def own_kernel(first, *refs):
    if first:
        in_ref, vec_ref, res_ref, ones_ref, sc_out, vec_out, res_out, dir_out, img_out, copies_ref = refs
    else:
        (in_ref, vec_ref, res_ref, ones_ref, sc_ref, dir_ref, img_ref,
         sc_out, vec_out, res_out, dir_out, img_out, copies_ref) = refs
    grad, tail, scalars = arrived(in_ref, 0)
    past = None if first else tuple(sc_ref[0:1, i : i + 1] for i in range(4))
    beta, step, now = conjugate(scalars, past)
    mean = scalars[2] / TOTAL
    zd_mean = now[1] / TOTAL
    if first:
        kept = (step, now[3])
    else:
        d0_zd1 = scalars[6] + beta * sc_ref[0:1, 5:6]
        kept = (sc_ref[0:1, 4:5], sc_ref[0:1, 5:6], step, now[3], d0_zd1, beta)
    sc_out[...] = lanes_of(now + kept)
    for part, new in ((slice(0, HIDDEN), grad), (slice(HIDDEN, WIDE), tail)):
        image, direction = new - mean * ones_ref[:, part], res_ref[:, part]
        if not first:
            image = image + beta * img_ref[:, part]
            direction = direction + beta * dir_ref[:, part]
        img_out[:, part] = image
        dir_out[:, part] = direction
        res_out[:, part] = res_ref[:, part] - step * (image + SHIFT * direction)
    mask, res, o_res = vec_ref[0:1, :], vec_ref[1:2, :], vec_ref[5:6, :]
    direction, o_dir = res, o_res
    if not first:
        direction = direction + beta * vec_ref[2:3, :]
        o_dir = o_dir + beta * vec_ref[3:4, :]
    vec_out[0:1, :] = mask
    vec_out[1:2, :] = res - step * (o_dir - zd_mean * mask + SHIFT * direction)
    vec_out[2:3, :] = direction
    vec_out[3:4, :] = o_dir
    vec_out[4:5, :] = direction if first else vec_ref[4:5, :]
    vec_out[5:8, :] = jnp.zeros((3, SLOTS), F32)
    store_copies(copies_ref, res_out[...])


def last_scalars_kernel(parts_ref, vec_ref, out_ref):
    values = row_sum(parts_ref, vec_ref[0:1, :])
    lane = iota((OWNERS, TAIL), 1)
    out = jnp.zeros((OWNERS, TAIL), F32)
    for i, value in enumerate(iteration_scalars(vec_ref, values)):
        out = jnp.where(lane == i, value, out)
    out_ref[...] = out


def last_kernel(rep_ref, in_ref, sc_ref, dir0_ref, dir1_ref, res2_ref, b0_ref, b1_ref, b2_ref, vis_ref, hid_ref, mat_ref):
    summed = jnp.sum(in_ref[...], axis=0, keepdims=True)
    scalars = [summed[:, i : i + 1] for i in range(SCALARS)]
    keep = [sc_ref[0:1, i : i + 1] for i in range(9)]
    beta2, step2, now = conjugate(scalars, tuple(keep[0:4]))
    step0, d0_zd0, step1, d1_zd1, d0_zd1 = keep[4:9]
    d0_zd2 = scalars[6] + beta2 * d0_zd1
    d1_zd2 = scalars[4] + beta2 * d1_zd1
    norm = step0 * step0 * d0_zd0 + step1 * step1 * d1_zd1 + step2 * step2 * now[3]
    norm = norm + 2.0 * (step0 * step1 * d0_zd1 + step0 * step2 * d0_zd2 + step1 * step2 * d1_zd2)
    params = float(SITES * HIDDEN * 8 + HIDDEN * 8 + SITES)
    scale = lax.rsqrt(norm / (TOTAL * params) + EPSILON) / TOTAL
    beta1 = sc_ref[0:1, 9:10]
    w0, w1, w2 = scale * step0, scale * (step1 + step2 * beta2), scale * step2
    mat_ref[...] = w0 * dir0_ref[:, 0:HIDDEN] + w1 * dir1_ref[:, 0:HIDDEN] + w2 * res2_ref[:, 0:HIDDEN]
    small = (w0 + w1 * beta1) * b0_ref[...] + w1 * b1_ref[...] + w2 * b2_ref[...]
    hid_ref[...] = small
    a, b = iota((SITES, TAIL), 0), iota((SITES, TAIL), 1)
    pick = jnp.where(a == 32 * rep_ref[0] + b, 1.0, 0.0).astype(F32)
    vis_ref[...] = dot(small[:, 0:SITES], pick, precision=HIGH)


def shape(dims, dtype=F32):
    return jax.ShapeDtypeStruct(dims, dtype)


def call(kernel, outs, name, n_in, smem=(), scratch=()):
    vmem = pl.BlockSpec(memory_space=pltpu.VMEM)
    scalar = pl.BlockSpec(memory_space=pltpu.SMEM)
    return pl.pallas_call(
        kernel,
        out_shape=outs,
        in_specs=[scalar if i in smem else vmem for i in range(n_in)],
        out_specs=[vmem] * len(outs),
        scratch_shapes=list(scratch),
        name=name,
    )


def over_chain(blocks):
    return lax.all_to_all(blocks, CHAIN, split_axis=0, concat_axis=0, tiled=True)


def per_device(spins, energies, counts, accepted, hidden_bias, weights):
    reps = lax.axis_size("rep")
    rows = shape((OWNERS, ROWS, WIDE), BF16)
    own = shape((ROWS, WIDE))
    vec_shape = shape((8, SLOTS))
    st, tt, vec, blocks = call(
        setup_kernel,
        [shape((SITES, SLOTS), BF16), shape((WIDE, SLOTS), BF16), vec_shape, shape((OWNERS, 2 * ROWS, WIDE), BF16)],
        "setup", 6, smem=(0,),
    )(counts, spins, energies[None, :], accepted, weights, hidden_bias[None, :])
    res, ones, vec, copies = call(first_own_kernel, [own, own, vec_shape, rows], "first_own", 2)(over_chain(blocks), vec)

    def push(copies):
        parts, small = call(
            push_kernel, [shape((reps, 1, SLOTS)), shape((8, HIDDEN))], "push", 3,
            scratch=[pltpu.VMEM((SITES, WIDE), F32)],
        )(over_chain(copies), st, tt)
        return lax.all_to_all(parts, "rep", split_axis=0, concat_axis=0, tiled=True), small

    state, smalls, directions = (), [], []
    for iteration in range(2):
        parts, small = push(copies)
        vec, blocks = call(pull_kernel, [vec_shape, rows], "pull", 4)(parts, vec, st, tt)
        sc, vec, res, direction, image, copies = call(
            lambda *refs, first=iteration == 0: own_kernel(first, *refs),
            [shape((8, TAIL)), vec_shape, own, own, own, rows], "own", 4 + len(state),
        )(over_chain(blocks), vec, res, ones, *state)
        state = (sc, direction, image)
        smalls.append(small)
        directions.append(direction)
    parts, small = push(copies)
    smalls.append(small)
    (sums,) = call(last_scalars_kernel, [shape((OWNERS, TAIL))], "last_scalars", 2)(parts, vec)
    vis, hid, mat = call(
        last_kernel, [shape((8, TAIL)), shape((8, HIDDEN)), shape((ROWS, HIDDEN))], "last", 9, smem=(0,)
    )(lax.axis_index("rep")[None].astype(jnp.int32), over_chain(sums), sc, *directions, res, *smalls)
    return vis[1, :32], hid[0], mat


def solution(mesh):
    split = Mesh(
        mesh.devices.reshape(4, 8, 2, mesh.shape["rep"]), ("chain_0", "chain_1", "chain_2", "rep")
    )
    in_specs = (P(CHAIN, None), P(CHAIN), P(CHAIN), P(CHAIN, None), P("rep"), P(None, "rep"))
    out_specs = (P("rep"), P("rep"), P(CHAIN, "rep"))
    return jax.shard_map(
        per_device, mesh=split, in_specs=in_specs, out_specs=out_specs, check_vma=False
    )
```

time: 569 us -> 234 us (0.41)
  the two profiles are of different devices: /device:TPU:2 before, /device:TPU:1 now
where the time goes in v1:
time: 234 us; the launch traced here: 233 us
  blocking collectives  171 us (73%)
  Pallas kernels  38.2 us (16%)
  waiting for transfers between devices  9.31 us (4%)
  starting transfers between devices  7.28 us (3%)
  local copies, waits for them, and re-layouts  5.65 us (2%)
    all_to_all x6, blocking collectives, over_chain(): lax.all_to_all(blocks, CHAIN, split_axis=0, concat_axis=0, tiled=True)  135 us
    all_to_all x3, blocking collectives, push(): lax.all_to_all(parts, 'rep', split_axis=0, concat_axis=0, tiled=True)  36 us
    pallas_call x3, Pallas kernels, push(): call(push_kernel, [shape((reps, 1, SLOTS)), shape((8, HIDDEN))], 'push',...  11 us
    all_to_all x1, waiting for transfers between devices, over_chain(): lax.all_to_all(blocks, CHAIN, split_axis=0, concat_axis=0, tiled=True)  9.31 us
    pallas_call x2, Pallas kernels, per_device(): call(pull_kernel, [vec_shape, rows], 'pull', 4)(parts, vec, st, tt)  9.26 us
    all_to_all x1, starting transfers between devices, over_chain(): lax.all_to_all(blocks, CHAIN, split_axis=0, concat_axis=0, tiled=True)  7.28 us
    pallas_call x1, Pallas kernels, per_device(): call(setup_kernel, [shape((SITES, SLOTS), BF16), shape((WIDE, SLOTS), BF1...  7.03 us
    pallas_call x2, Pallas kernels, per_device(): call(lambda *refs, first=iteration == 0: own_kernel(first, *refs), [shape...  4.86 us
  transfers between devices with their start and end apart: 1, of which 1 were waited for; matrix products, arithmetic and copies ran while one was open for 0% of the time, Pallas kernels for 0%

profile of v1, /device:TPU:1, one launch (start us, length us, event | category | flops | bytes accessed | tf_op | source)
XLA Modules:
  0.0 232.9 jit_solution(17652990605151673575)
XLA Ops:
  0.6 1.3 broadcast_in_dim.10.energy_ref
  1.9 1.3 broadcast_in_dim.11.bias_ref
  3.8 7.0 %setup.1 = (bf16[256,1536]{1,0:T(8,128)(2,1)}, bf16[640,1536]{1,0:T(8,128)(2,1)}, f32[8,1536]{1,0:T(8,128)}, bf16[64,8,640]{2,1,0:T(8,128)(2,1)}) custom-call(s32[1]{0:T(128)S(6)} %copy.10.count_ref, bf16[1536,256]{1,0:T(8,128)(2,1)} %spins_ref.1, bf16[1,1536]{1,0:T(2,128)(2,1)} %broadcast_in_dim.10.energy_ref, s32[1,1536]{1,0:T(1,128)} %accepted_ref.1, ...), custom_call_target="tpu_custom_call" | custom-call | tf_op jit(solution)/shard_map/setup/pallas_call | solution.py:350
  10.9 35.0 %all_to_all.56.in_ref = bf16[64,8,640]{2,1,0:T(8,128)(2,1)} all-to-all(bf16[64,8,640]{2,1,0:T(8,128)(2,1)} %get-tuple-element.35), channel_id=1, replica_groups=mesh['chain_0'=4,'chain_1'=8,'chain_2'=2,'rep'=8] {'chain_0','chain_1','..., dimensions={0} | all-to-all | bytes 1310720 | tf_op jit(solution)/shard_map/all_to_all | solution.py:342
  45.9 2.4 %first_own.1 = (f32[4,640]{1,0:T(4,128)}, f32[4,640]{1,0:T(4,128)}, f32[8,1536]{1,0:T(8,128)}, bf16[64,4,640]{2,1,0:T(4,128)(2,1)}) custom-call(bf16[64,8,640]{2,1,0:T(8,128)(2,1)} %all_to_all.56.in_ref, f32[8,1536]{1,0:T(8,128)} %get-tuple-element.36.vec_ref), custom_call_target="tpu_custom_call" | custom-call | tf_op jit(solution)/shard_map/first_own/pallas_call | solution.py:355
  48.3 19.6 %all_to_all.57.in_ref = bf16[64,4,640]{2,1,0:T(4,128)(2,1)} all-to-all(bf16[64,4,640]{2,1,0:T(4,128)(2,1)} %get-tuple-element.37), channel_id=1, replica_groups=mesh['chain_0'=4,'chain_1'=8,'chain_2'=2,'rep'=8] {'chain_0','chain_1','..., dimensions={0} | all-to-all | bytes 655360 | tf_op jit(solution)/shard_map/all_to_all | solution.py:342
  67.9 3.7 %push.3 = (f32[8,1,1536]{2,1,0:T(1,128)}, f32[8,512]{1,0:T(8,128)}) custom-call(bf16[64,4,640]{2,1,0:T(4,128)(2,1)} %all_to_all.57.in_ref, bf16[256,1536]{1,0:T(8,128)(2,1)} %get-tuple-element.38.st_ref, bf16[640,1536]{1,0:T(8,128)(2,1)} %get-tuple-element.39.tt_ref), custom_call_target="tpu_custom_call" | custom-call | tf_op jit(solution)/shard_map/push/pallas_call | solution.py:358
  71.5 14.0 %all_to_all.58.parts_ref = f32[8,1,1536]{2,1,0:T(1,128)} all-to-all(f32[8,1,1536]{2,1,0:T(1,128)} %get-tuple-element.40), channel_id=1, replica_groups=mesh['chain_0'=4,'chain_1'=8,'chain_2'=2,'rep'=8] {'rep'}, dimensions={0} | all-to-all | bytes 98304 | tf_op jit(solution)/shard_map/all_to_all | solution.py:362
  85.6 4.6 %pull.2 = (f32[8,1536]{1,0:T(8,128)}, bf16[64,4,640]{2,1,0:T(4,128)(2,1)}) custom-call(f32[8,1,1536]{2,1,0:T(1,128)} %all_to_all.58.parts_ref, f32[8,1536]{1,0:T(8,128)} %get-tuple-element.41.vec_ref, bf16[256,1536]{1,0:T(8,128)(2,1)} %get-tuple-element.38.st_ref, bf16[640,1536]{1,0:T(8,128)(2,1)} %get-tuple-element.39.tt_ref), custom_call_target="tpu_custom_call" | custom-call | tf_op jit(solution)/shard_map/pull/pallas_call | solution.py:367
  90.2 20.9 %all_to_all.59.refs_0_ = bf16[64,4,640]{2,1,0:T(4,128)(2,1)} all-to-all(bf16[64,4,640]{2,1,0:T(4,128)(2,1)} %get-tuple-element.42), channel_id=1, replica_groups=mesh['chain_0'=4,'chain_1'=8,'chain_2'=2,'rep'=8] {'chain_0','chain_1','..., dimensions={0} | all-to-all | bytes 655360 | tf_op jit(solution)/shard_map/all_to_all | solution.py:342
  111.1 2.3 %own.2 = (f32[8,128]{1,0:T(8,128)}, f32[8,1536]{1,0:T(8,128)}, f32[4,640]{1,0:T(4,128)}, f32[4,640]{1,0:T(4,128)}, f32[4,640]{1,0:T(4,128)}, /*index=5*/bf16[64,4,640]{2,1,0:T(4,128)(2,1)}) custom-call(bf16[64,4,640]{2,1,0:T(4,128)(2,1)} %all_to_all.59.refs_0_, f32[8,1536]{1,0:T(8,128)} %get-tuple-element.43.refs_1_, f32[4,640]{1,0:T(4,128)} %get-tuple-element.44.refs_2_, ...), custom_call_target="tpu_custom_call" | custom-call | tf_op jit(solution)/shard_map/own/pallas_call | solution.py:368
  113.4 19.5 %all_to_all.60.in_ref = bf16[64,4,640]{2,1,0:T(4,128)(2,1)} all-to-all(bf16[64,4,640]{2,1,0:T(4,128)(2,1)} %get-tuple-element.46), channel_id=1, replica_groups=mesh['chain_0'=4,'chain_1'=8,'chain_2'=2,'rep'=8] {'chain_0','chain_1','..., dimensions={0} | all-to-all | bytes 655360 | tf_op jit(solution)/shard_map/all_to_all | solution.py:342
  132.9 3.7 %push.4 = (f32[8,1,1536]{2,1,0:T(1,128)}, f32[8,512]{1,0:T(8,128)}) custom-call(bf16[64,4,640]{2,1,0:T(4,128)(2,1)} %all_to_all.60.in_ref, bf16[256,1536]{1,0:T(8,128)(2,1)} %get-tuple-element.38.st_ref, bf16[640,1536]{1,0:T(8,128)(2,1)} %get-tuple-element.39.tt_ref), custom_call_target="tpu_custom_call" | custom-call | tf_op jit(solution)/shard_map/push/pallas_call | solution.py:358
  136.6 11.0 %all_to_all.61.parts_ref = f32[8,1,1536]{2,1,0:T(1,128)} all-to-all(f32[8,1,1536]{2,1,0:T(1,128)} %get-tuple-element.47), channel_id=1, replica_groups=mesh['chain_0'=4,'chain_1'=8,'chain_2'=2,'rep'=8] {'rep'}, dimensions={0} | all-to-all | bytes 98304 | tf_op jit(solution)/shard_map/all_to_all | solution.py:362
  147.6 4.6 %pull.3 = (f32[8,1536]{1,0:T(8,128)}, bf16[64,4,640]{2,1,0:T(4,128)(2,1)}) custom-call(f32[8,1,1536]{2,1,0:T(1,128)} %all_to_all.61.parts_ref, f32[8,1536]{1,0:T(8,128)} %get-tuple-element.48.vec_ref, bf16[256,1536]{1,0:T(8,128)(2,1)} %get-tuple-element.38.st_ref, bf16[640,1536]{1,0:T(8,128)(2,1)} %get-tuple-element.39.tt_ref), custom_call_target="tpu_custom_call" | custom-call | tf_op jit(solution)/shard_map/pull/pallas_call | solution.py:367
  152.2 20.6 %all_to_all.62.refs_0_ = bf16[64,4,640]{2,1,0:T(4,128)(2,1)} all-to-all(bf16[64,4,640]{2,1,0:T(4,128)(2,1)} %get-tuple-element.49), channel_id=1, replica_groups=mesh['chain_0'=4,'chain_1'=8,'chain_2'=2,'rep'=8] {'chain_0','chain_1','..., dimensions={0} | all-to-all | bytes 655360 | tf_op jit(solution)/shard_map/all_to_all | solution.py:342
  172.8 2.5 %own.3 = (f32[8,128]{1,0:T(8,128)}, f32[8,1536]{1,0:T(8,128)}, f32[4,640]{1,0:T(4,128)}, f32[4,640]{1,0:T(4,128)}, f32[4,640]{1,0:T(4,128)}, /*index=5*/bf16[64,4,640]{2,1,0:T(4,128)(2,1)}) custom-call(bf16[64,4,640]{2,1,0:T(4,128)(2,1)} %all_to_all.62.refs_0_, f32[8,1536]{1,0:T(8,128)} %get-tuple-element.50.refs_1_, f32[4,640]{1,0:T(4,128)} %get-tuple-element.51.refs_2_, ...), custom_call_target="tpu_custom_call" | custom-call | tf_op jit(solution)/shard_map/own/pallas_call | solution.py:368
  175.4 19.5 %all_to_all.63.in_ref = bf16[64,4,640]{2,1,0:T(4,128)(2,1)} all-to-all(bf16[64,4,640]{2,1,0:T(4,128)(2,1)} %get-tuple-element.55), channel_id=1, replica_groups=mesh['chain_0'=4,'chain_1'=8,'chain_2'=2,'rep'=8] {'chain_0','chain_1','..., dimensions={0} | all-to-all | bytes 655360 | tf_op jit(solution)/shard_map/all_to_all | solution.py:342
  194.9 3.7 %push.5 = (f32[8,1,1536]{2,1,0:T(1,128)}, f32[8,512]{1,0:T(8,128)}) custom-call(bf16[64,4,640]{2,1,0:T(4,128)(2,1)} %all_to_all.63.in_ref, bf16[256,1536]{1,0:T(8,128)(2,1)} %get-tuple-element.38.st_ref, bf16[640,1536]{1,0:T(8,128)(2,1)} %get-tuple-element.39.tt_ref), custom_call_target="tpu_custom_call" | custom-call | tf_op jit(solution)/shard_map/push/pallas_call | solution.py:358
  198.5 11.0 %all_to_all.64.parts_ref = f32[8,1,1536]{2,1,0:T(1,128)} all-to-all(f32[8,1,1536]{2,1,0:T(1,128)} %get-tuple-element.56), channel_id=1, replica_groups=mesh['chain_0'=4,'chain_1'=8,'chain_2'=2,'rep'=8] {'rep'}, dimensions={0} | all-to-all | bytes 98304 | tf_op jit(solution)/shard_map/all_to_all | solution.py:362
  209.5 1.6 last_scalars.1
  211.1 7.3 %all-to-all-start.9 = ((f32[64,1,128]{2,1,0:T(1,128)}), f32[64,1,128]{2,1,0:T(1,128)S(1)}, u32[]{:S(2)}, u32[]{:S(2)}) async-start(f32[64,1,128]{2,1,0:T(1,128)} %bitcast.9), calls=%async_computation.9 | async-start | bytes 65536 | tf_op jit(solution)/shard_map/all_to_all | solution.py:342
  218.4 9.3 %all-to-all-done.9 = f32[64,1,128]{2,1,0:T(1,128)S(1)} async-done(((f32[64,1,128]{2,1,0:T(1,128)}), f32[64,1,128]{2,1,0:T(1,128)S(1)}, u32[]{:S(2)}, u32[]{:S(2)}) %all-to-all-start.9) | async-done | bytes 32800 | tf_op jit(solution)/shard_map/all_to_all | solution.py:342
  227.7 0.0 copy-start
  227.7 0.6 copy-done
  228.3 2.1 last.1
  230.5 1.3 slice.7
  231.7 1.2 slice_bitcast_fusion
Async XLA Ops:
  211.1 16.6 %all-to-all-start.9 = ((f32[64,1,128]{2,1,0:T(1,128)}), f32[64,1,128]{2,1,0:T(1,128)S(1)}, u32[]{:S(2)}, u32[]{:S(2)}) async-start(f32[64,1,128]{2,1,0:T(1,128)} %bitcast.9), calls=%async_computation.9 | async-start | bytes 65536 | tf_op jit(solution)/shard_map/all_to_all | solution.py:342
  227.7 0.6 copy-start

commit v2 on v1

--- a/solution.py
+++ b/solution.py
@@ -24,6 +24,7 @@
 SLOTS = 1536
 TOTAL = float(KEEP_DEV * OWNERS)
 SCALARS = 8
+VMEM_LIMIT = 24 * 2**20
 
 
 def iota(shape, dim):
@@ -68,23 +69,26 @@
     return row == ROWS * (col >> 3)
 
 
+def row_pair(high, low):
+    sub = iota((16, high.shape[1]), 0)
+    return jnp.where(sub == 0, high.astype(F32), jnp.where(sub == 1, low.astype(F32), 0.0)).astype(BF16)
+
+
 def pull(weights, st, tt):
     high, low = two(weights)
     spins = st.astype(F32)
-    grad = by_lanes((spins * high.astype(F32)).astype(BF16), tt)
-    grad = grad + by_lanes((spins * low.astype(F32)).astype(BF16), tt)
-    sub = iota((16, SLOTS), 0)
-    pair = jnp.where(sub == 0, high.astype(F32), jnp.where(sub == 1, low.astype(F32), 0.0)).astype(BF16)
-    both = by_lanes(pair, tt)
-    return grad, both[0:1, :] + both[1:2, :]
-
-
-def tail_of(grad, hidden, scalars):
-    visible = grad[:, HIDDEN : HIDDEN + 1]
+    visible = jnp.sum(spins * weights, axis=1, keepdims=True)
+    both = jnp.concatenate([(spins * high.astype(F32)).astype(BF16), (spins * low.astype(F32)).astype(BF16)], axis=0)
+    grad = by_lanes(both, tt)
+    hidden = by_lanes(row_pair(high, low), tt)
+    return grad[:SITES] + grad[SITES:], visible, hidden[0:1, :] + hidden[1:2, :]
+
+
+def tail_of(visible, hidden, scalars):
     v_high = visible.astype(BF16).astype(F32)
     lane, row = iota((SITES, TAIL), 1), iota((SITES, TAIL), 0)
     tail = jnp.where(lane == 0, v_high, jnp.where(lane == 1, visible - v_high, 0.0))
-    h_high, h_low = two(hidden[:, :HIDDEN])
+    h_high, h_low = two(hidden)
     mine = own_hidden((SITES, HIDDEN))
     j, l = iota((HIDDEN, TAIL), 0) & 7, iota((HIDDEN, TAIL), 1)
     for piece, base in ((h_high, 8), (h_low, 16)):
@@ -96,17 +100,19 @@
 def store_rows(out_ref, first, grad, tail):
     for c in range(OWNERS):
         rows = slice(ROWS * c, ROWS * (c + 1))
-        out_ref[c, first : first + ROWS, 0:HIDDEN] = grad[rows, 0:HIDDEN].astype(BF16)
+        out_ref[c, first : first + ROWS, 0:HIDDEN] = grad[rows, :].astype(BF16)
         out_ref[c, first : first + ROWS, HIDDEN:WIDE] = tail[rows, :].astype(BF16)
 
 
+def to_left(x, count):
+    return pltpu.roll(x, TAIL - count, 1)
+
+
 def combined(tail):
-    a, b = iota((TAIL, TAIL), 0), iota((TAIL, TAIL), 1)
-    take = (b == 0) & (a < 2)
-    take = take | ((b >= 8) & (b < 16) & ((a == b) | (a == b + 8)))
-    first = 32 + 3 * (b - 64)
-    take = take | ((b >= 64) & (b < 64 + SCALARS) & (a >= first) & (a < first + 3))
-    return dot(tail, jnp.where(take, 1.0, 0.0).astype(F32), precision=HIGH)
+    lane = iota((ROWS, TAIL), 1)
+    one = to_left(tail, 1)
+    second = jnp.where(lane >= 32, one + to_left(tail, 2), jnp.where(lane >= 8, to_left(tail, 8), one))
+    return tail + second
 
 
 def store_copies(out_ref, rows):
@@ -114,10 +120,9 @@
     tail = rows[:, HIDDEN:WIDE]
     tail = jnp.where(lane == 0, tail * 0.125, jnp.where((lane >= 8) & (lane < 16), tail, 0.0))
     high = tail.astype(BF16).astype(F32)
-    a, b = iota((TAIL, TAIL), 0), iota((TAIL, TAIL), 1)
-    move = ((a == 0) & (b == 1)) | ((a >= 8) & (a < 16) & (b == a + 8))
-    low = dot(tail - high, jnp.where(move, 1.0, 0.0).astype(F32), precision=HIGH)
-    packed = (high + low).astype(BF16)
+    low = tail - high
+    packed = high + jnp.where(lane == 1, pltpu.roll(low, 1, 1), jnp.where(lane >= 16, pltpu.roll(low, 8, 1), 0.0))
+    packed = packed.astype(BF16)
     coupling = rows[:, 0:HIDDEN].astype(BF16)
     for c in range(OWNERS):
         out_ref[c, :, 0:HIDDEN] = coupling
@@ -134,19 +139,21 @@
     spins = spins_ref[...]
     st_ref[...] = by_lanes(eye(SITES), spins).astype(BF16)
     turned = by_lanes(eye(HIDDEN), weights_ref[...]).astype(BF16)
-    bias = by_lanes(eye(HIDDEN), jnp.broadcast_to(bias_ref[...].astype(F32), (16, HIDDEN)).astype(BF16))
+    bias = by_lanes(eye(HIDDEN), jnp.broadcast_to(bias_ref[...].astype(F32).reshape(1, HIDDEN), (16, HIDDEN)).astype(BF16))
     preact = bias[:, 0:1] + dot(turned, st_ref[...])
-    tt_ref[0:HIDDEN, :] = jnp.tanh(preact).astype(BF16)
-    sub = iota((TAIL, SLOTS), 0)
-    tt_ref[HIDDEN:WIDE, :] = jnp.where(sub < 2, 1.0, 0.0).astype(BF16)
-    energy = (energy_ref[...].astype(F32) - ENERGY_MID) * mask
+    tt_ref[...] = jnp.tanh(preact).astype(BF16)
+    energy = (energy_ref[...].astype(F32).reshape(1, SLOTS) - ENERGY_MID) * mask
     vec_ref[0:1, :] = mask
     vec_ref[1:2, :] = energy
     vec_ref[2:8, :] = jnp.zeros((6, SLOTS), F32)
     st, tt = st_ref[...], tt_ref[...]
-    for first, row, scalars in ((0, energy, (total(energy),)), (ROWS, mask, ())):
-        grad, hidden = pull(row, st, tt)
-        store_rows(out_ref, first, grad, tail_of(grad, hidden, scalars))
+    spins = st.astype(F32)
+    both = jnp.concatenate([(spins * energy).astype(BF16), (spins * mask).astype(BF16)], axis=0)
+    grad = by_lanes(both, tt)
+    hidden = by_lanes(row_pair(energy.astype(BF16), mask.astype(BF16)), tt)
+    for k, (row, scalars) in enumerate(((energy, (total(energy),)), (mask, ()))):
+        visible = jnp.sum(spins * row, axis=1, keepdims=True)
+        store_rows(out_ref, ROWS * k, grad[SITES * k : SITES * (k + 1)], tail_of(visible, hidden[k : k + 1], scalars))
 
 
 def arrived(in_ref, first):
@@ -156,7 +163,7 @@
         acc[c % 4] = acc[c % 4] + in_ref[c, rows, :].astype(F32)
     acc = (acc[0] + acc[1]) + (acc[2] + acc[3])
     tail = combined(acc[:, HIDDEN:WIDE])
-    scalars = [tail[1:2, 64 + i : 65 + i] for i in range(SCALARS)]
+    scalars = [tail[1:2, 32 + 3 * i : 33 + 3 * i] for i in range(SCALARS)]
     return acc[:, 0:HIDDEN], tail, scalars
 
 
@@ -196,13 +203,11 @@
     bias_ref[...] = jnp.zeros((8, HIDDEN), F32)
     bias_ref[0:1, :] = hidden
     bias_ref[1:2, 0:SITES] = visible[0:1, :]
-    h_high, h_low = two(hidden)
-    sub = iota((16, HIDDEN), 0)
-    pair = jnp.where(sub == 0, h_high.astype(F32), jnp.where(sub == 1, h_low.astype(F32), 0.0)).astype(BF16)
-    tt = tt_ref[...]
-    side = dot(pair, tt[0:HIDDEN, :])
-    turned = jnp.transpose(rows_ref[...]).astype(BF16)
-    mixture = dot(turned, st_ref[...])
+    tt, st = tt_ref[...], st_ref[...]
+    pick = jnp.where((iota((16, TAIL), 0) == iota((16, TAIL), 1)) & (iota((16, TAIL), 1) < 2), 1.0, 0.0)
+    side = dot(row_pair(*two(hidden)), tt) + dot(by_lanes(pick.astype(BF16), tail).astype(BF16), st)
+    turned = jnp.transpose(rows_ref[:, 0:HIDDEN]).astype(BF16)
+    mixture = dot(turned, st)
     values = jnp.sum(mixture * tt.astype(F32), axis=0, keepdims=True)
     values = (values + side[0:1, :] + side[1:2, :]) * (1.0 / TOTAL)
     for y in range(parts_ref.shape[0]):
@@ -233,8 +238,8 @@
     values = row_sum(parts_ref, vec_ref[0:1, :])
     vec_out_ref[...] = vec_ref[...]
     vec_out_ref[5:6, :] = values
-    grad, hidden = pull(values, st_ref[...], tt_ref[...])
-    store_rows(out_ref, 0, grad, tail_of(grad, hidden, iteration_scalars(vec_ref, values)))
+    grad, visible, hidden = pull(values, st_ref[...], tt_ref[...])
+    store_rows(out_ref, 0, grad, tail_of(visible, hidden, iteration_scalars(vec_ref, values)))
 
 
 def conjugate(scalars, past):
@@ -315,10 +320,10 @@
     w0, w1, w2 = scale * step0, scale * (step1 + step2 * beta2), scale * step2
     mat_ref[...] = w0 * dir0_ref[:, 0:HIDDEN] + w1 * dir1_ref[:, 0:HIDDEN] + w2 * res2_ref[:, 0:HIDDEN]
     small = (w0 + w1 * beta1) * b0_ref[...] + w1 * b1_ref[...] + w2 * b2_ref[...]
-    hid_ref[...] = small
+    hid_ref[...] = small[0]
     a, b = iota((SITES, TAIL), 0), iota((SITES, TAIL), 1)
     pick = jnp.where(a == 32 * rep_ref[0] + b, 1.0, 0.0).astype(F32)
-    vis_ref[...] = dot(small[:, 0:SITES], pick, precision=HIGH)
+    vis_ref[...] = dot(small[:, 0:SITES], pick, precision=HIGH)[1, 0:32]
 
 
 def shape(dims, dtype=F32):
@@ -335,6 +340,7 @@
         out_specs=[vmem] * len(outs),
         scratch_shapes=list(scratch),
         name=name,
+        compiler_params=pltpu.CompilerParams(vmem_limit_bytes=VMEM_LIMIT),
     )
 
 
@@ -349,9 +355,9 @@
     vec_shape = shape((8, SLOTS))
     st, tt, vec, blocks = call(
         setup_kernel,
-        [shape((SITES, SLOTS), BF16), shape((WIDE, SLOTS), BF16), vec_shape, shape((OWNERS, 2 * ROWS, WIDE), BF16)],
+        [shape((SITES, SLOTS), BF16), shape((HIDDEN, SLOTS), BF16), vec_shape, shape((OWNERS, 2 * ROWS, WIDE), BF16)],
         "setup", 6, smem=(0,),
-    )(counts, spins, energies[None, :], accepted, weights, hidden_bias[None, :])
+    )(counts, *(pltpu.with_memory_space_constraint(a, pltpu.HBM) for a in (spins, energies, accepted, weights, hidden_bias)))
     res, ones, vec, copies = call(first_own_kernel, [own, own, vec_shape, rows], "first_own", 2)(over_chain(blocks), vec)
 
     def push(copies):
@@ -376,9 +382,9 @@
     smalls.append(small)
     (sums,) = call(last_scalars_kernel, [shape((OWNERS, TAIL))], "last_scalars", 2)(parts, vec)
     vis, hid, mat = call(
-        last_kernel, [shape((8, TAIL)), shape((8, HIDDEN)), shape((ROWS, HIDDEN))], "last", 9, smem=(0,)
+        last_kernel, [shape((32,)), shape((HIDDEN,)), shape((ROWS, HIDDEN))], "last", 9, smem=(0,)
     )(lax.axis_index("rep")[None].astype(jnp.int32), over_chain(sums), sc, *directions, res, *smalls)
-    return vis[1, :32], hid[0], mat
+    return vis, hid, mat
 
 
 def solution(mesh):

time: 234 us -> 199 us (0.85)
  Pallas kernels: 38.2 us -> 15 us
  local copies, waits for them, and re-layouts: 5.65 us -> 0 us
  blocking collectives: 171 us -> 166 us
    pallas_call x3, Pallas kernels: 11 us -> 3.44 us  [push(): call(push_kernel, [shape((reps, 1, SLOTS)), shape((8, HIDDEN))], 'push',...]
    pallas_call x2, Pallas kernels: 9.26 us -> 3.44 us  [per_device(): call(pull_kernel, [vec_shape, rows], 'pull', 4)(parts, vec, st, tt)]
    pallas_call x2, Pallas kernels: 9.16 us -> 5.46 us  [the longest x1 4.24 us: per_device(): call(setup_kernel, [shape((SITES, SLOTS), BF16), shape((HIDDEN, SLOTS), B...]
    all_to_all x3, blocking collectives: 36 us -> 32.5 us  [push(): lax.all_to_all(parts, 'rep', split_axis=0, concat_axis=0, tiled=True)]
    pallas_call x2, Pallas kernels: 4.86 us -> 1.53 us  [per_device(): call(lambda *refs, first=iteration == 0: own_kernel(first, *refs), [shape...]
    broadcast_in_dim x2 -> x0, local copies, waits for them, and re-layouts: 2.54 us -> none  [the longest x1 1.29 us: per_device(): energies[None, :]]
where the time goes in v2:
time: 199 us
  blocking collectives  166 us (83%)
  Pallas kernels  15 us (8%)
  waiting for transfers between devices  9.3 us (5%)
  starting transfers between devices  7.28 us (4%)
    all_to_all x6, blocking collectives, over_chain(): lax.all_to_all(blocks, CHAIN, split_axis=0, concat_axis=0, tiled=True)  134 us
    all_to_all x3, blocking collectives, push(): lax.all_to_all(parts, 'rep', split_axis=0, concat_axis=0, tiled=True)  32.5 us
    all_to_all x1, waiting for transfers between devices, over_chain(): lax.all_to_all(blocks, CHAIN, split_axis=0, concat_axis=0, tiled=True)  9.3 us
    all_to_all x1, starting transfers between devices, over_chain(): lax.all_to_all(blocks, CHAIN, split_axis=0, concat_axis=0, tiled=True)  7.28 us
    pallas_call x1, Pallas kernels, per_device(): call(setup_kernel, [shape((SITES, SLOTS), BF16), shape((HIDDEN, SLOTS), B...  4.24 us
  transfers between devices with their start and end apart: 1, of which 1 were waited for; matrix products, arithmetic and copies ran while one was open for 0% of the time, Pallas kernels for 0%

profile of v2, /device:TPU:1, one launch (start us, length us, event | category | flops | bytes accessed | tf_op | source)
XLA Modules:
  0.0 199.0 jit_solution(4154948680575097770)
XLA Ops:
  1.3 4.2 %setup.1 = (bf16[256,1536]{1,0:T(8,128)(2,1)S(1)}, bf16[512,1536]{1,0:T(8,128)(2,1)S(1)}, f32[8,1536]{1,0:T(8,128)S(1)}, bf16[64,8,640]{2,1,0:T(8,128)(2,1)S(1)}) custom-call(s32[1]{0:T(128)S(6)} %copy.10.count_ref, bf16[1536,256]{1,0:T(8,128)(2,1)} %spins_ref.1, bf16[1536]{0:T(1024)(128)(2,1)} %energy_ref.1, s32[1,1536]{1,0:T(1,128)} %accepted_ref.1, ...), custom_call_target="tpu_custom_call" | custom-call | tf_op jit(solution)/shard_map/setup/pallas_call | solution.py:356
  5.5 34.7 %all_to_all.56.in_ref = bf16[64,8,640]{2,1,0:T(8,128)(2,1)S(1)} all-to-all(bf16[64,8,640]{2,1,0:T(8,128)(2,1)S(1)} %get-tuple-element.32), channel_id=1, replica_groups=mesh['chain_0'=4,'chain_1'=8,'chain_2'=2,'rep'=8] {'chain_0','chain_1','..., dimensions={0} | all-to-all | bytes 1310720 | tf_op jit(solution)/shard_map/all_to_all | solution.py:348
  40.2 0.3 first_own.1
  40.6 19.3 %all_to_all.57.in_ref = bf16[64,4,640]{2,1,0:T(4,128)(2,1)S(1)} all-to-all(bf16[64,4,640]{2,1,0:T(4,128)(2,1)S(1)} %get-tuple-element.34), channel_id=1, replica_groups=mesh['chain_0'=4,'chain_1'=8,'chain_2'=2,'rep'=8] {'chain_0','chain_1','..., dimensions={0} | all-to-all | bytes 655360 | tf_op jit(solution)/shard_map/all_to_all | solution.py:348
  59.9 1.1 push.3
  61.0 13.7 %all_to_all.58.parts_ref = f32[8,1,1536]{2,1,0:T(1,128)S(1)} all-to-all(f32[8,1,1536]{2,1,0:T(1,128)S(1)} %get-tuple-element.37), channel_id=1, replica_groups=mesh['chain_0'=4,'chain_1'=8,'chain_2'=2,'rep'=8] {'rep'}, dimensions={0} | all-to-all | bytes 98304 | tf_op jit(solution)/shard_map/all_to_all | solution.py:368
  74.7 1.7 pull.2
  76.5 20.6 %all_to_all.59.refs_0_ = bf16[64,4,640]{2,1,0:T(4,128)(2,1)S(1)} all-to-all(bf16[64,4,640]{2,1,0:T(4,128)(2,1)S(1)} %get-tuple-element.39), channel_id=1, replica_groups=mesh['chain_0'=4,'chain_1'=8,'chain_2'=2,'rep'=8] {'chain_0','chain_1','..., dimensions={0} | all-to-all | bytes 655360 | tf_op jit(solution)/shard_map/all_to_all | solution.py:348
  97.1 0.4 own.2
  97.5 19.2 %all_to_all.60.in_ref = bf16[64,4,640]{2,1,0:T(4,128)(2,1)S(1)} all-to-all(bf16[64,4,640]{2,1,0:T(4,128)(2,1)S(1)} %get-tuple-element.43), channel_id=1, replica_groups=mesh['chain_0'=4,'chain_1'=8,'chain_2'=2,'rep'=8] {'chain_0','chain_1','..., dimensions={0} | all-to-all | bytes 655360 | tf_op jit(solution)/shard_map/all_to_all | solution.py:348
  116.7 1.1 push.4
  117.9 9.4 %all_to_all.61.parts_ref = f32[8,1,1536]{2,1,0:T(1,128)S(1)} all-to-all(f32[8,1,1536]{2,1,0:T(1,128)S(1)} %get-tuple-element.44), channel_id=1, replica_groups=mesh['chain_0'=4,'chain_1'=8,'chain_2'=2,'rep'=8] {'rep'}, dimensions={0} | all-to-all | bytes 98304 | tf_op jit(solution)/shard_map/all_to_all | solution.py:368
  127.3 1.7 pull.3
  129.0 20.5 %all_to_all.62.refs_0_ = bf16[64,4,640]{2,1,0:T(4,128)(2,1)S(1)} all-to-all(bf16[64,4,640]{2,1,0:T(4,128)(2,1)S(1)} %get-tuple-element.46), channel_id=1, replica_groups=mesh['chain_0'=4,'chain_1'=8,'chain_2'=2,'rep'=8] {'chain_0','chain_1','..., dimensions={0} | all-to-all | bytes 655360 | tf_op jit(solution)/shard_map/all_to_all | solution.py:348
  149.5 1.1 own.3
  150.6 19.2 %all_to_all.63.in_ref = bf16[64,4,640]{2,1,0:T(4,128)(2,1)S(1)} all-to-all(bf16[64,4,640]{2,1,0:T(4,128)(2,1)S(1)} %get-tuple-element.52), channel_id=1, replica_groups=mesh['chain_0'=4,'chain_1'=8,'chain_2'=2,'rep'=8] {'chain_0','chain_1','..., dimensions={0} | all-to-all | bytes 655360 | tf_op jit(solution)/shard_map/all_to_all | solution.py:348
  169.8 1.1 push.5
  171.0 9.4 %all_to_all.64.parts_ref = f32[8,1,1536]{2,1,0:T(1,128)S(1)} all-to-all(f32[8,1,1536]{2,1,0:T(1,128)S(1)} %get-tuple-element.53), channel_id=1, replica_groups=mesh['chain_0'=4,'chain_1'=8,'chain_2'=2,'rep'=8] {'rep'}, dimensions={0} | all-to-all | bytes 98304 | tf_op jit(solution)/shard_map/all_to_all | solution.py:368
  180.4 0.8 last_scalars.1
  181.2 7.3 %all-to-all-start.9 = ((f32[64,1,128]{2,1,0:T(1,128)}), f32[64,1,128]{2,1,0:T(1,128)S(1)}, u32[]{:S(2)}, u32[]{:S(2)}) async-start(f32[64,1,128]{2,1,0:T(1,128)} %bitcast.2), calls=%async_computation.9 | async-start | bytes 65536 | tf_op jit(solution)/shard_map/all_to_all | solution.py:348
  188.5 9.3 %all-to-all-done.9 = f32[64,1,128]{2,1,0:T(1,128)S(1)} async-done(((f32[64,1,128]{2,1,0:T(1,128)}), f32[64,1,128]{2,1,0:T(1,128)S(1)}, u32[]{:S(2)}, u32[]{:S(2)}) %all-to-all-start.9) | async-done | bytes 32800 | tf_op jit(solution)/shard_map/all_to_all | solution.py:348
  197.8 1.2 last.1
Async XLA Ops:
  181.2 16.6 %all-to-all-start.9 = ((f32[64,1,128]{2,1,0:T(1,128)}), f32[64,1,128]{2,1,0:T(1,128)S(1)}, u32[]{:S(2)}, u32[]{:S(2)}) async-start(f32[64,1,128]{2,1,0:T(1,128)} %bitcast.2), calls=%async_computation.9 | async-start | bytes 65536 | tf_op jit(solution)/shard_map/all_to_all | solution.py:348

commit v3 on v2

v3 whole, which is shorter than its diff:
```python
import jax
import jax.numpy as jnp
from jax import lax
from jax.experimental import pallas as pl
from jax.experimental.pallas import tpu as pltpu
from jax.sharding import Mesh
from jax.sharding import PartitionSpec as P

KEEP_DEV = 768
SHIFT = 0.05
EPSILON = 1e-06
ENERGY_MID = -110.0
CHAIN = ("chain_0", "chain_1", "chain_2")
CHIPS = ("chain_0", "chain_1")
UNITS = ("chain_2", "rep")
F32 = jnp.float32
BF16 = jnp.bfloat16
HIGH = lax.Precision.HIGHEST

SITES = 256
CORES = 2
REPS = 8
HIDDEN = 256
OWNERS = 32
ROWS = 4
COUPLING = 2 * HIDDEN
TAIL = 128
WIDE = COUPLING + TAIL
OWN_SLOTS = 1536
SLOTS = CORES * OWN_SLOTS
SIDE = SITES + 16
PART = SLOTS + ROWS * HIDDEN + HIDDEN
TOTAL = float(KEEP_DEV * OWNERS * CORES)
SCALARS = 8
VMEM_LIMIT = 24 * 2**20


def iota(shape, dim):
    return lax.broadcasted_iota(jnp.int32, shape, dim)


def dot(a, b, dims=((1,), (0,)), precision=None):
    return lax.dot_general(a, b, (dims, ((), ())), precision=precision, preferred_element_type=F32)


def by_lanes(a, b):
    return dot(a, b, ((1,), (1,)))


def eye(n):
    return jnp.where(iota((n, n), 0) == iota((n, n), 1), 1.0, 0.0).astype(BF16)


def two(x):
    high = x.astype(BF16)
    return high, (x - high.astype(F32)).astype(BF16)


def total(x):
    return jnp.sum(x, keepdims=True)


def scalar_lanes(scalars):
    lane = iota((1, TAIL), 1)
    out = jnp.zeros((1, TAIL), F32)
    for i, value in enumerate(scalars):
        one = value.astype(BF16).astype(F32)
        second = (value - one).astype(BF16).astype(F32)
        third = value - one - second
        for k, piece in enumerate((one, second, third)):
            out = jnp.where(lane == 32 + 3 * i + k, piece, out)
    return out


def own_hidden(shape):
    row, col = iota(shape, 0), iota(shape, 1)
    return row == 8 * (col >> 3)


def row_pair(high, low):
    sub = iota((16, high.shape[1]), 0)
    return jnp.where(sub == 0, high.astype(F32), jnp.where(sub == 1, low.astype(F32), 0.0)).astype(BF16)


def pull(weights, st, tt):
    high, low = two(weights)
    spins = st.astype(F32)
    visible = jnp.sum(spins * weights, axis=1, keepdims=True)
    both = jnp.concatenate([(spins * high.astype(F32)).astype(BF16), (spins * low.astype(F32)).astype(BF16)], axis=0)
    grad = by_lanes(both, tt)
    hidden = by_lanes(row_pair(high, low), tt)
    return grad[:SITES] + grad[SITES:], visible, hidden[0:1, :] + hidden[1:2, :]


def tail_of(visible, hidden, scalars):
    v_high = visible.astype(BF16).astype(F32)
    lane, row = iota((SITES, TAIL), 1), iota((SITES, TAIL), 0)
    first = (row & 4) >> 1
    tail = jnp.where(lane == first, v_high, jnp.where(lane == first + 1, visible - v_high, 0.0))
    h_high, h_low = two(hidden)
    mine = own_hidden((SITES, HIDDEN))
    j, l = iota((HIDDEN, TAIL), 0) & 7, iota((HIDDEN, TAIL), 1)
    for piece, base in ((h_high, 8), (h_low, 16)):
        spread = jnp.where(mine, piece.astype(F32), 0.0).astype(BF16)
        tail = tail + dot(spread, jnp.where(l == base + j, 1.0, 0.0).astype(BF16))
    return tail + jnp.where((row & 7) == 1, scalar_lanes(scalars), 0.0)


def store_rows(out_ref, first, grad, tail):
    for c in range(OWNERS):
        near, far = slice(8 * c, 8 * c + ROWS), slice(8 * c + ROWS, 8 * c + 8)
        out_ref[c, first : first + ROWS, 0:HIDDEN] = grad[near, :].astype(BF16)
        out_ref[c, first : first + ROWS, HIDDEN:COUPLING] = grad[far, :].astype(BF16)
        out_ref[c, first : first + ROWS, COUPLING:WIDE] = (tail[near, :] + tail[far, :]).astype(BF16)


def to_left(x, count):
    return pltpu.roll(x, TAIL - count, 1)


def combined(tail):
    lane = iota((ROWS, TAIL), 1)
    one = to_left(tail, 1)
    second = jnp.where(lane >= 32, one + to_left(tail, 2), jnp.where(lane >= 8, to_left(tail, 8), one))
    return tail + second


def store_copies(out_ref, rows):
    lane = iota((ROWS, TAIL), 1)
    tail = rows[:, COUPLING:WIDE]
    tail = jnp.where((lane == 0) | (lane == 2), tail * (1.0 / (CORES * REPS)), jnp.where((lane >= 8) & (lane < 16), tail, 0.0))
    high = tail.astype(BF16).astype(F32)
    low = tail - high
    packed = high + jnp.where(lane < 8, pltpu.roll(low, 1, 1), jnp.where(lane >= 16, pltpu.roll(low, 8, 1), 0.0))
    packed = packed.astype(BF16)
    coupling = rows[:, 0:COUPLING].astype(BF16)
    for c in range(OWNERS):
        out_ref[c, :, 0:COUPLING] = coupling
        out_ref[c, :, COUPLING:WIDE] = packed


def share_kernel(count_ref, core_ref, rep_ref, spins_ref, energy_ref, accepted_ref, out_ref):
    accepted = accepted_ref[...]
    live = iota((16, OWN_SLOTS), 1) < count_ref[0]
    major = jnp.where((iota((16, OWN_SLOTS), 0) == (accepted >> 7)) & live, 1.0, 0.0).astype(BF16)
    minor = jnp.where(iota((TAIL, OWN_SLOTS), 0) == (accepted & 127), 1.0, 0.0).astype(BF16)
    table = by_lanes(major, minor)
    mask = jnp.concatenate([table[h : h + 1, :] for h in range(OWN_SLOTS // TAIL)], axis=1)
    energy = (energy_ref[...].astype(F32).reshape(1, OWN_SLOTS) - ENERGY_MID) * mask
    sites = by_lanes(eye(SITES), spins_ref[...]).astype(BF16)
    extra = row_pair(energy.astype(BF16), mask.astype(BF16))
    for core in range(CORES):
        out_ref[core, 0:SITES, :] = sites
        out_ref[core, SITES:SIDE, :] = extra


def setup_kernel(core_ref, shared_ref, weights_ref, bias_ref, st_ref, tt_ref, vec_ref, out_ref):
    upper = core_ref[0] == 1
    weights = jnp.where(upper, weights_ref[:, HIDDEN:], weights_ref[:, 0:HIDDEN])
    bias_row = bias_ref[...].astype(F32).reshape(1, CORES * HIDDEN)
    bias_row = jnp.where(upper, bias_row[:, HIDDEN:], bias_row[:, 0:HIDDEN])
    turned = by_lanes(eye(HIDDEN), weights).astype(BF16)
    bias = by_lanes(eye(HIDDEN), jnp.broadcast_to(bias_row, (16, HIDDEN)).astype(BF16))
    vec_ref[...] = jnp.zeros((8, SLOTS), F32)
    for core in range(CORES):
        half = slice(core * OWN_SLOTS, (core + 1) * OWN_SLOTS)
        sites = shared_ref[core, 0:SITES, :]
        extra = shared_ref[core, SITES:SIDE, :].astype(F32)
        st_ref[:, half] = sites
        tt_ref[:, half] = jnp.tanh(bias[:, 0:1] + dot(turned, sites)).astype(BF16)
        vec_ref[0:1, half] = extra[1:2, :]
        vec_ref[1:2, half] = extra[0:1, :]
    mask, energy = vec_ref[0:1, :], vec_ref[1:2, :]
    st, tt = st_ref[...], tt_ref[...]
    spins = st.astype(F32)
    both = jnp.concatenate([(spins * energy).astype(BF16), (spins * mask).astype(BF16)], axis=0)
    grad = by_lanes(both, tt)
    hidden = by_lanes(row_pair(energy.astype(BF16), mask.astype(BF16)), tt)
    for k, (row, scalars) in enumerate(((energy, (total(energy),)), (mask, ()))):
        visible = jnp.sum(spins * row, axis=1, keepdims=True)
        store_rows(out_ref, ROWS * k, grad[SITES * k : SITES * (k + 1)], tail_of(visible, hidden[k : k + 1], scalars))


def arrived(in_ref, first):
    rows = slice(first, first + ROWS)
    acc = [in_ref[c, rows, :].astype(F32) for c in range(4)]
    for c in range(4, OWNERS):
        acc[c % 4] = acc[c % 4] + in_ref[c, rows, :].astype(F32)
    acc = (acc[0] + acc[1]) + (acc[2] + acc[3])
    tail = combined(acc[:, COUPLING:WIDE])
    scalars = [tail[1:2, 32 + 3 * i : 33 + 3 * i] for i in range(SCALARS)]
    return acc[:, 0:COUPLING], tail, scalars


def lanes_of(values):
    lane = iota((8, TAIL), 1)
    out = jnp.zeros((8, TAIL), F32)
    for i, value in enumerate(values):
        out = jnp.where(lane == i, value, out)
    return out


def first_own_kernel(in_ref, vec_ref, res_ref, ones_ref, vec_out_ref, copies_ref):
    energy, energy_tail, scalars = arrived(in_ref, 0)
    ones, ones_tail, _ = arrived(in_ref, ROWS)
    mean = scalars[0] / TOTAL
    res_ref[:, 0:COUPLING] = energy - mean * ones
    res_ref[:, COUPLING:WIDE] = energy_tail - mean * ones_tail
    ones_ref[:, 0:COUPLING] = ones
    ones_ref[:, COUPLING:WIDE] = ones_tail
    mask, raw = vec_ref[0:1, :], vec_ref[1:2, :]
    vec_out_ref[0:1, :] = mask
    vec_out_ref[1:2, :] = raw - mean * mask
    vec_out_ref[2:8, :] = jnp.zeros((6, SLOTS), F32)
    store_copies(copies_ref, res_ref[...])


def push_kernel(in_ref, res_ref, st_ref, tt_ref, parts_ref, visible_ref, rows_ref, tail_ref):
    for c in range(OWNERS):
        near, far = slice(8 * c, 8 * c + ROWS), slice(8 * c + ROWS, 8 * c + 8)
        block = in_ref[c].astype(F32)
        rows_ref[near, :] = block[:, 0:HIDDEN]
        rows_ref[far, :] = block[:, HIDDEN:COUPLING]
        tail_ref[near, :] = block[:, COUPLING:WIDE]
        tail_ref[far, :] = block[:, COUPLING:WIDE]
    lane, row = iota((SITES, TAIL), 1), iota((SITES, TAIL), 0)
    tail = tail_ref[...]
    l, j = iota((TAIL, HIDDEN), 0), iota((TAIL, HIDDEN), 1) & 7
    spread = dot(tail.astype(BF16), jnp.where((l == 8 + j) | (l == 16 + j), 1.0, 0.0).astype(BF16))
    hidden = jnp.sum(jnp.where(own_hidden((SITES, HIDDEN)), spread, 0.0), axis=0, keepdims=True)
    seen = jnp.where((lane < 4) & ((lane & 2) == ((row & 4) >> 1)), tail, 0.0).astype(BF16)
    a, b = iota((16, TAIL), 0), iota((16, TAIL), 1)
    pair = by_lanes(jnp.where((b < 4) & ((b & 1) == a), 1.0, 0.0).astype(BF16), seen)
    visible_ref[...] = jnp.zeros((8, SITES), F32)
    visible_ref[0:1, :] = (pair[0:1, :] + pair[1:2, :]) * float(CORES * REPS)
    tt, st = tt_ref[...], st_ref[...]
    side = dot(row_pair(*two(hidden)), tt) + dot(pair.astype(BF16), st)
    turned = jnp.transpose(rows_ref[...]).astype(BF16)
    mixture = dot(turned, st)
    values = jnp.sum(mixture * tt.astype(F32), axis=0, keepdims=True)
    values = (values + side[0:1, :] + side[1:2, :]) * (1.0 / TOTAL)
    for p in range(CORES * REPS):
        parts_ref[p, :, 0:SLOTS] = values
        first = HIDDEN * (p // REPS)
        for r in range(ROWS):
            start = SLOTS + HIDDEN * r
            parts_ref[p, :, start : start + HIDDEN] = res_ref[r : r + 1, first : first + HIDDEN]
        parts_ref[p, :, PART - HIDDEN : PART] = hidden


def row_sum(parts_ref, mask):
    values = parts_ref[0, :, 0:SLOTS]
    for p in range(1, CORES * REPS):
        values = values + parts_ref[p, :, 0:SLOTS]
    return values * mask


def iteration_scalars(vec_ref, values):
    res, before, o_before, start = (vec_ref[i : i + 1, :] for i in (1, 2, 3, 4))
    return (
        total(res * values),
        total(values * values),
        total(values),
        total(values * o_before),
        total(values * before),
        total(res * o_before),
        total(values * start),
    )


def pull_kernel(parts_ref, vec_ref, st_ref, tt_ref, vec_out_ref, out_ref):
    values = row_sum(parts_ref, vec_ref[0:1, :])
    vec_out_ref[...] = vec_ref[...]
    vec_out_ref[5:6, :] = values
    grad, visible, hidden = pull(values, st_ref[...], tt_ref[...])
    store_rows(out_ref, 0, grad, tail_of(visible, hidden, iteration_scalars(vec_ref, values)))


def conjugate(scalars, past):
    r_zr, zr_zr, zr_sum, zr_zd, zr_d, r_zd, zr_start = scalars[:7]
    if past is None:
        beta, zd_sum, zd_zd, zd_d = None, zr_sum, zr_zr, r_zr
    else:
        rr, sum_before, zz_before, zd_before = past
        beta = r_zr / rr
        zd_sum = zr_sum + beta * sum_before
        zd_zd = zr_zr + 2.0 * beta * zr_zd + beta * beta * zz_before
        zd_d = r_zr + beta * (zr_d + r_zd) + beta * beta * zd_before
    step = r_zr / (zd_zd - zd_sum * zd_sum / TOTAL + SHIFT * zd_d)
    return beta, step, (r_zr, zd_sum, zd_zd, zd_d)


def own_kernel(first, *refs):
    if first:
        in_ref, vec_ref, res_ref, ones_ref, sc_out, vec_out, res_out, dir_out, img_out, copies_ref = refs
    else:
        (in_ref, vec_ref, res_ref, ones_ref, sc_ref, dir_ref, img_ref,
         sc_out, vec_out, res_out, copies_ref) = refs
    grad, tail, scalars = arrived(in_ref, 0)
    past = None if first else tuple(sc_ref[0:1, i : i + 1] for i in range(4))
    beta, step, now = conjugate(scalars, past)
    mean = scalars[2] / TOTAL
    zd_mean = now[1] / TOTAL
    if first:
        kept = (step, now[3])
    else:
        d0_zd1 = scalars[6] + beta * sc_ref[0:1, 5:6]
        kept = (sc_ref[0:1, 4:5], sc_ref[0:1, 5:6], step, now[3], d0_zd1, beta)
    sc_out[...] = lanes_of(now + kept)
    for part, new in ((slice(0, COUPLING), grad), (slice(COUPLING, WIDE), tail)):
        image, direction = new - mean * ones_ref[:, part], res_ref[:, part]
        if not first:
            image = image + beta * img_ref[:, part]
            direction = direction + beta * dir_ref[:, part]
        if first:
            img_out[:, part] = image
            dir_out[:, part] = direction
        res_out[:, part] = res_ref[:, part] - step * (image + SHIFT * direction)
    mask, res, o_res = vec_ref[0:1, :], vec_ref[1:2, :], vec_ref[5:6, :]
    direction, o_dir = res, o_res
    if not first:
        direction = direction + beta * vec_ref[2:3, :]
        o_dir = o_dir + beta * vec_ref[3:4, :]
    vec_out[0:1, :] = mask
    vec_out[1:2, :] = res - step * (o_dir - zd_mean * mask + SHIFT * direction)
    vec_out[2:3, :] = direction
    vec_out[3:4, :] = o_dir
    vec_out[4:5, :] = direction if first else vec_ref[4:5, :]
    vec_out[5:8, :] = jnp.zeros((3, SLOTS), F32)
    store_copies(copies_ref, res_out[...])


def last_scalars_kernel(parts_ref, vec_ref, out_ref):
    values = row_sum(parts_ref, vec_ref[0:1, :])
    lane = iota((OWNERS, TAIL), 1)
    out = jnp.zeros((OWNERS, TAIL), F32)
    for i, value in enumerate(iteration_scalars(vec_ref, values)):
        out = jnp.where(lane == i, value, out)
    out_ref[...] = out


def last_kernel(rep_ref, in_ref, sc_ref, p0_ref, p1_ref, p2_ref, v0_ref, v1_ref, v2_ref, vis_ref, hid_ref, mat_ref):
    summed = jnp.sum(in_ref[...], axis=0, keepdims=True)
    scalars = [summed[:, i : i + 1] for i in range(SCALARS)]
    keep = [sc_ref[0:1, i : i + 1] for i in range(10)]
    beta2, step2, now = conjugate(scalars, tuple(keep[0:4]))
    step0, d0_zd0, step1, d1_zd1, d0_zd1, beta1 = keep[4:10]
    d0_zd2 = scalars[6] + beta2 * d0_zd1
    d1_zd2 = scalars[4] + beta2 * d1_zd1
    norm = step0 * step0 * d0_zd0 + step1 * step1 * d1_zd1 + step2 * step2 * now[3]
    norm = norm + 2.0 * (step0 * step1 * d0_zd1 + step0 * step2 * d0_zd2 + step1 * step2 * d1_zd2)
    params = float(SITES * HIDDEN * CORES * REPS + HIDDEN * CORES * REPS + SITES)
    scale = lax.rsqrt(norm / (TOTAL * params) + EPSILON) / TOTAL
    w1 = scale * (step1 + step2 * beta2)
    weights = (scale * step0 + w1 * beta1, w1, scale * step2)
    hidden = []
    for core in range(CORES):
        at = core * REPS + rep_ref[0]
        both = sum(w * ref[at][:, SLOTS:PART] for w, ref in zip(weights, (p0_ref, p1_ref, p2_ref)))
        for r in range(ROWS):
            mat_ref[r : r + 1, core * HIDDEN : (core + 1) * HIDDEN] = both[:, HIDDEN * r : HIDDEN * (r + 1)]
        hidden.append(both[:, ROWS * HIDDEN :])
    hid_ref[...] = jnp.concatenate(hidden, axis=1)[0]
    visible = sum(w * ref[...] for w, ref in zip(weights, (v0_ref, v1_ref, v2_ref)))
    a, b = iota((SITES, TAIL), 0), iota((SITES, TAIL), 1)
    pick = jnp.where(a == 32 * rep_ref[0] + b, 1.0, 0.0).astype(F32)
    vis_ref[...] = dot(visible, pick, precision=HIGH)[0, 0:32]


def shape(dims, dtype=F32):
    return jax.ShapeDtypeStruct(dims, dtype)


def call(kernel, outs, name, n_in, smem=(), scratch=()):
    vmem = pl.BlockSpec(memory_space=pltpu.VMEM)
    scalar = pl.BlockSpec(memory_space=pltpu.SMEM)
    return pl.pallas_call(
        kernel,
        out_shape=outs,
        in_specs=[scalar if i in smem else vmem for i in range(n_in)],
        out_specs=[vmem] * len(outs),
        scratch_shapes=list(scratch),
        name=name,
        compiler_params=pltpu.CompilerParams(vmem_limit_bytes=VMEM_LIMIT),
    )


def exchanged(blocks, axes):
    return lax.all_to_all(blocks, axes, split_axis=0, concat_axis=0, tiled=True)


def place(axis):
    return lax.axis_index(axis)[None].astype(jnp.int32)


def in_hbm(*arrays):
    return [pltpu.with_memory_space_constraint(a, pltpu.HBM) for a in arrays]


def per_device(spins, energies, counts, accepted, hidden_bias, weights):
    rows = shape((OWNERS, ROWS, WIDE), BF16)
    own = shape((ROWS, WIDE))
    vec_shape = shape((8, SLOTS))
    core, rep = place("chain_2"), place("rep")
    (shared,) = call(share_kernel, [shape((CORES, SIDE, OWN_SLOTS), BF16)], "share", 6, smem=(0, 1, 2))(
        counts, core, rep, *in_hbm(spins, energies, accepted)
    )
    st, tt, vec, blocks = call(
        setup_kernel,
        [shape((SITES, SLOTS), BF16), shape((HIDDEN, SLOTS), BF16), vec_shape, shape((OWNERS, 2 * ROWS, WIDE), BF16)],
        "setup", 4, smem=(0,),
    )(core, exchanged(shared, "chain_2"), *in_hbm(weights, hidden_bias))
    res, ones, vec, copies = call(first_own_kernel, [own, own, vec_shape, rows], "first_own", 2)(
        exchanged(blocks, CHIPS), vec
    )

    def push(copies, res):
        parts, visible = call(
            push_kernel, [shape((CORES * REPS, 1, PART)), shape((8, SITES))], "push", 4,
            scratch=[pltpu.VMEM((SITES, HIDDEN), F32), pltpu.VMEM((SITES, TAIL), F32)],
        )(exchanged(copies, CHIPS), res, st, tt)
        return exchanged(parts, UNITS), visible

    state, seen = (), []
    for iteration in range(2):
        seen.append(push(copies, res))
        vec, blocks = call(pull_kernel, [vec_shape, rows], "pull", 4)(seen[-1][0], vec, st, tt)
        first = iteration == 0
        sc, vec, res, *state, copies = call(
            lambda *refs, first=first: own_kernel(first, *refs),
            [shape((8, TAIL)), vec_shape, own, *([own, own] if first else []), rows], "own", 4 + len(state),
        )(exchanged(blocks, CHIPS), vec, res, ones, *state)
        state = (sc, *state)
    seen.append(push(copies, res))
    (sums,) = call(last_scalars_kernel, [shape((OWNERS, TAIL))], "last_scalars", 2)(seen[-1][0], vec)
    return call(
        last_kernel, [shape((32,)), shape((CORES * HIDDEN,)), shape((ROWS, CORES * HIDDEN))], "last", 9, smem=(0,)
    )(rep, exchanged(sums, CHIPS), sc, *(p for p, _ in seen), *(v for _, v in seen))


def solution(mesh):
    split = Mesh(
        mesh.devices.reshape(4, 8, 2, mesh.shape["rep"]), ("chain_0", "chain_1", "chain_2", "rep")
    )
    in_specs = (P(CHAIN, None), P(CHAIN), P(CHAIN), P(CHAIN, None), P("rep"), P(None, "rep"))
    out_specs = (P("rep"), P("rep"), P(CHAIN, "rep"))
    return jax.shard_map(
        per_device, mesh=split, in_specs=in_specs, out_specs=out_specs, check_vma=False
    )
```

time: 199 us -> 183 us (0.920); the launches traced: 199 us -> 181 us
  waiting for transfers between devices: 9.3 us -> 0 us
  starting transfers between devices: 7.28 us -> 0 us
  blocking collectives: 166 us -> 164 us
    all_to_all x1 -> x0, waiting for transfers between devices: 9.3 us -> none  [over_chain(): lax.all_to_all(blocks, CHAIN, split_axis=0, concat_axis=0, tiled=True)]
    all_to_all x1 -> x0, starting transfers between devices: 7.28 us -> none  [over_chain(): lax.all_to_all(blocks, CHAIN, split_axis=0, concat_axis=0, tiled=True)]
    all_to_all x9 -> x11, blocking collectives: 166 us -> 164 us  [exchanged(): return lax.all_to_all(blocks, axes, split_axis=0, concat_axis=0, tiled=True)]
    pallas_call x8 -> x9, Pallas kernels: 9.64 us -> 10.8 us  [the longest x3 3.54 us: push(): call(push_kernel, [shape((CORES * REPS, 1, PART)), shape((8, SITES))], 'p...]
  transfers between devices with their start and end apart: 1 -> 0, of which waited for: 1 -> 0; matrix products, arithmetic and copies ran while one was open for 0% -> 0% of each run, Pallas kernels for 0% -> 0%
where the time goes in v3:
time: 183 us; the launch traced here: 181 us
  blocking collectives  164 us (90%)
  Pallas kernels  14.8 us (8%)
    all_to_all x11, blocking collectives, exchanged(): return lax.all_to_all(blocks, axes, split_axis=0, concat_axis=0, tiled=True)  164 us

profile of v3, /device:TPU:1, one launch (start us, length us, event | category | flops | bytes accessed | tf_op | source)
XLA Modules:
  0.0 180.6 jit_solution(12519861102412086873)
XLA Ops:
  1.3 1.7 share.1
  3.0 11.5 %all_to_all.61.shared_ref = bf16[2,272,1536]{2,1,0:T(8,128)(2,1)S(1)} all-to-all(bf16[2,272,1536]{2,1,0:T(8,128)(2,1)S(1)} %share.1), channel_id=1, replica_groups=mesh['chain_0'=4,'chain_1'=8,'chain_2'=2,'rep'=8] {'chain_2'}, dimensions={0} | all-to-all | bytes 3342336 | tf_op jit(solution)/shard_map/all_to_all | solution.py:389
  14.5 3.5 %setup.1 = (bf16[256,3072]{1,0:T(8,128)(2,1)S(1)}, bf16[256,3072]{1,0:T(8,128)(2,1)S(1)}, f32[8,3072]{1,0:T(8,128)S(1)}, bf16[32,8,640]{2,1,0:T(8,128)(2,1)S(1)}) custom-call(s32[1]{0:T(128)} %bitcast.1.core_ref, bf16[2,272,1536]{2,1,0:T(8,128)(2,1)S(1)} %all_to_all.61.shared_ref, bf16[256,512]{1,0:T(8,128)(2,1)} %weights_ref.1, bf16[512]{0:T(512)(128)(2,1)} %bias_ref.1), custom_call_target="tpu_custom_call" | custom-call | tf_op jit(solution)/shard_map/setup/pallas_call | solution.py:408
  17.9 17.8 %all_to_all.62.in_ref = bf16[32,8,640]{2,1,0:T(8,128)(2,1)S(1)} all-to-all(bf16[32,8,640]{2,1,0:T(8,128)(2,1)S(1)} %get-tuple-element.31), channel_id=1, replica_groups=mesh['chain_0'=4,'chain_1'=8,'chain_2'=2,'rep'=8] {'chain_0','chain_1'}, dimensions={0} | all-to-all | bytes 655360 | tf_op jit(solution)/shard_map/all_to_all | solution.py:389
  35.8 0.3 first_own.1
  36.0 16.6 %all_to_all.63.in_ref = bf16[32,4,640]{2,1,0:T(4,128)(2,1)S(1)} all-to-all(bf16[32,4,640]{2,1,0:T(4,128)(2,1)S(1)} %get-tuple-element.33), channel_id=1, replica_groups=mesh['chain_0'=4,'chain_1'=8,'chain_2'=2,'rep'=8] {'chain_0','chain_1'}, dimensions={0} | all-to-all | bytes 327680 | tf_op jit(solution)/shard_map/all_to_all | solution.py:389
  52.6 1.2 push.3
  53.8 19.1 %all_to_all.64.parts_ref.p0_ref = f32[16,1,4352]{2,1,0:T(1,128)S(1)} all-to-all(f32[16,1,4352]{2,1,0:T(1,128)S(1)} %get-tuple-element.37), channel_id=1, replica_groups=mesh['chain_0'=4,'chain_1'=8,'chain_2'=2,'rep'=8] {'chain_2','rep'}, dimensions={0} | all-to-all | bytes 557056 | tf_op jit(solution)/shard_map/all_to_all | solution.py:389
  72.9 1.7 pull.2
  74.6 12.7 %all_to_all.65.refs_0_ = bf16[32,4,640]{2,1,0:T(4,128)(2,1)S(1)} all-to-all(bf16[32,4,640]{2,1,0:T(4,128)(2,1)S(1)} %get-tuple-element.39), channel_id=1, replica_groups=mesh['chain_0'=4,'chain_1'=8,'chain_2'=2,'rep'=8] {'chain_0','chain_1'}, dimensions={0} | all-to-all | bytes 327680 | tf_op jit(solution)/shard_map/all_to_all | solution.py:389
  87.3 0.4 own.2
  87.7 13.2 %all_to_all.66.in_ref = bf16[32,4,640]{2,1,0:T(4,128)(2,1)S(1)} all-to-all(bf16[32,4,640]{2,1,0:T(4,128)(2,1)S(1)} %get-tuple-element.42), channel_id=1, replica_groups=mesh['chain_0'=4,'chain_1'=8,'chain_2'=2,'rep'=8] {'chain_0','chain_1'}, dimensions={0} | all-to-all | bytes 327680 | tf_op jit(solution)/shard_map/all_to_all | solution.py:389
  100.9 1.2 push.4
  102.1 17.9 %all_to_all.67.parts_ref.p1_ref = f32[16,1,4352]{2,1,0:T(1,128)S(1)} all-to-all(f32[16,1,4352]{2,1,0:T(1,128)S(1)} %get-tuple-element.44), channel_id=1, replica_groups=mesh['chain_0'=4,'chain_1'=8,'chain_2'=2,'rep'=8] {'chain_2','rep'}, dimensions={0} | all-to-all | bytes 557056 | tf_op jit(solution)/shard_map/all_to_all | solution.py:389
  120.0 1.7 pull.3
  121.7 12.6 %all_to_all.68.refs_0_ = bf16[32,4,640]{2,1,0:T(4,128)(2,1)S(1)} all-to-all(bf16[32,4,640]{2,1,0:T(4,128)(2,1)S(1)} %get-tuple-element.46), channel_id=1, replica_groups=mesh['chain_0'=4,'chain_1'=8,'chain_2'=2,'rep'=8] {'chain_0','chain_1'}, dimensions={0} | all-to-all | bytes 327680 | tf_op jit(solution)/shard_map/all_to_all | solution.py:389
  134.3 0.6 own.3
  134.9 13.2 %all_to_all.69.in_ref = bf16[32,4,640]{2,1,0:T(4,128)(2,1)S(1)} all-to-all(bf16[32,4,640]{2,1,0:T(4,128)(2,1)S(1)} %get-tuple-element.51), channel_id=1, replica_groups=mesh['chain_0'=4,'chain_1'=8,'chain_2'=2,'rep'=8] {'chain_0','chain_1'}, dimensions={0} | all-to-all | bytes 327680 | tf_op jit(solution)/shard_map/all_to_all | solution.py:389
  148.0 1.2 push.5
  149.2 17.9 %all_to_all.70.parts_ref.p2_ref = f32[16,1,4352]{2,1,0:T(1,128)S(1)} all-to-all(f32[16,1,4352]{2,1,0:T(1,128)S(1)} %get-tuple-element.53), channel_id=1, replica_groups=mesh['chain_0'=4,'chain_1'=8,'chain_2'=2,'rep'=8] {'chain_2','rep'}, dimensions={0} | all-to-all | bytes 557056 | tf_op jit(solution)/shard_map/all_to_all | solution.py:389
  167.1 0.2 last_scalars.1
  167.4 12.0 %all_to_all.71 = f32[32,1,128]{2,1,0:T(1,128)S(1)} all-to-all(f32[32,1,128]{2,1,0:T(1,128)S(1)} %bitcast.7), channel_id=1, replica_groups=mesh['chain_0'=4,'chain_1'=8,'chain_2'=2,'rep'=8] {'chain_0','chain_1'}, dimensions={0} | all-to-all | bytes 32768 | tf_op jit(solution)/shard_map/all_to_all | solution.py:389
  179.4 1.2 last.1

commit v4 on v3

v4 whole, which is shorter than its diff:
```python
import jax
import jax.numpy as jnp
from jax import lax
from jax.experimental import pallas as pl
from jax.experimental.pallas import tpu as pltpu
from jax.sharding import Mesh
from jax.sharding import PartitionSpec as P

KEEP_DEV = 768
SHIFT = 0.05
EPSILON = 1e-06
ENERGY_MID = -110.0
CHAIN = ("chain_0", "chain_1", "chain_2")
CHIPS = ("chain_0", "chain_1")
UNITS = ("chain_2", "rep")
F32 = jnp.float32
BF16 = jnp.bfloat16
HIGH = lax.Precision.HIGHEST

SITES = 256
CORES = 2
REPS = 8
HIDDEN = 512
OWNERS = 32
ROWS = 4
HALF = OWNERS * ROWS
TAIL = 128
WIDE = HIDDEN + TAIL
FIRST = 40
OWN_SLOTS = 1536
SLOTS = CORES * OWN_SLOTS
SIDE = SITES + 16
TOTAL = float(KEEP_DEV * OWNERS * CORES)
SCALARS = 8
VMEM_LIMIT = 24 * 2**20


def iota(shape, dim):
    return lax.broadcasted_iota(jnp.int32, shape, dim)


def dot(a, b, dims=((1,), (0,)), precision=None):
    return lax.dot_general(a, b, (dims, ((), ())), precision=precision, preferred_element_type=F32)


def by_lanes(a, b):
    return dot(a, b, ((1,), (1,)))


def eye(n):
    return jnp.where(iota((n, n), 0) == iota((n, n), 1), 1.0, 0.0).astype(BF16)


def two(x):
    high = x.astype(BF16)
    return high, (x - high.astype(F32)).astype(BF16)


def total(x):
    return jnp.sum(x, keepdims=True)


def scalar_lanes(scalars):
    lane = iota((1, TAIL), 1)
    out = jnp.zeros((1, TAIL), F32)
    for i, value in enumerate(scalars):
        one = value.astype(BF16).astype(F32)
        second = (value - one).astype(BF16).astype(F32)
        third = value - one - second
        for k, piece in enumerate((one, second, third)):
            out = jnp.where(lane == FIRST + 3 * i + k, piece, out)
    return out


def own_hidden(shape):
    row, col = iota(shape, 0), iota(shape, 1)
    return row == 8 * (col >> 4)


def row_pair(high, low):
    sub = iota((16, high.shape[1]), 0)
    return jnp.where(sub == 0, high.astype(F32), jnp.where(sub == 1, low.astype(F32), 0.0)).astype(BF16)


def pull(weights, st, half, tt):
    high, low = two(weights)
    spins = half.astype(F32)
    both = jnp.concatenate([(spins * high.astype(F32)).astype(BF16), (spins * low.astype(F32)).astype(BF16)], axis=0)
    grad = by_lanes(both, tt)
    pair = row_pair(high, low)
    visible, hidden = by_lanes(st, pair), by_lanes(pair, tt)
    return grad[:HALF] + grad[HALF:], visible[:, 0:1] + visible[:, 1:2], hidden[0:1, :] + hidden[1:2, :]


def tail_of(visible, hidden, scalars):
    v_high = visible.astype(BF16).astype(F32)
    lane, row = iota((SITES, TAIL), 1), iota((SITES, TAIL), 0)
    first = (row & 4) >> 1
    tail = jnp.where(lane == first, v_high, jnp.where(lane == first + 1, visible - v_high, 0.0))
    h_high, h_low = two(hidden)
    mine = own_hidden((SITES, HIDDEN))
    j, l = iota((HIDDEN, TAIL), 0) & 15, iota((HIDDEN, TAIL), 1)
    for piece, base in ((h_high, 8), (h_low, 24)):
        spread = jnp.where(mine, piece.astype(F32), 0.0).astype(BF16)
        tail = tail + dot(spread, jnp.where(l == base + j, 1.0, 0.0).astype(BF16))
    return tail + jnp.where((row & 7) == 1, scalar_lanes(scalars), 0.0)


def store_rows(out_ref, first, grad, tail):
    for c in range(OWNERS):
        near, far = slice(8 * c, 8 * c + ROWS), slice(8 * c + ROWS, 8 * c + 8)
        out_ref[c, first : first + ROWS, 0:HIDDEN] = grad[ROWS * c : ROWS * (c + 1), :].astype(BF16)
        out_ref[c, first : first + ROWS, HIDDEN:WIDE] = (tail[near, :] + tail[far, :]).astype(BF16)


def to_left(x, count):
    return pltpu.roll(x, TAIL - count, 1)


def combined(tail):
    lane = iota((ROWS, TAIL), 1)
    one = to_left(tail, 1)
    second = jnp.where(lane >= FIRST, one + to_left(tail, 2), jnp.where(lane >= 8, to_left(tail, 16), one))
    return tail + second


def store_copies(out_ref, rows):
    lane = iota((ROWS, TAIL), 1)
    tail = rows[:, HIDDEN:WIDE]
    tail = jnp.where((lane == 0) | (lane == 2), tail * (1.0 / (CORES * REPS)), jnp.where((lane >= 8) & (lane < 24), tail * (1.0 / CORES), 0.0))
    high = tail.astype(BF16).astype(F32)
    low = tail - high
    packed = high + jnp.where(lane < 8, pltpu.roll(low, 1, 1), jnp.where(lane >= 24, pltpu.roll(low, 16, 1), 0.0))
    packed = packed.astype(BF16)
    coupling = rows[:, 0:HIDDEN].astype(BF16)
    for c in range(OWNERS):
        out_ref[c, :, 0:HIDDEN] = coupling
        out_ref[c, :, HIDDEN:WIDE] = packed


def share_kernel(count_ref, core_ref, rep_ref, spins_ref, energy_ref, accepted_ref, out_ref):
    accepted = accepted_ref[...]
    live = iota((16, OWN_SLOTS), 1) < count_ref[0]
    major = jnp.where((iota((16, OWN_SLOTS), 0) == (accepted >> 7)) & live, 1.0, 0.0).astype(BF16)
    minor = jnp.where(iota((TAIL, OWN_SLOTS), 0) == (accepted & 127), 1.0, 0.0).astype(BF16)
    table = by_lanes(major, minor)
    mask = jnp.concatenate([table[h : h + 1, :] for h in range(OWN_SLOTS // TAIL)], axis=1)
    energy = (energy_ref[...].astype(F32).reshape(1, OWN_SLOTS) - ENERGY_MID) * mask
    sites = by_lanes(eye(SITES), spins_ref[...]).astype(BF16)
    extra = row_pair(energy.astype(BF16), mask.astype(BF16))
    for core in range(CORES):
        out_ref[core, 0:SITES, :] = sites
        out_ref[core, SITES:SIDE, :] = extra


def setup_kernel(core_ref, shared_ref, weights_ref, bias_ref, st_ref, half_ref, tt_ref, vec_ref, out_ref):
    turned = by_lanes(eye(HIDDEN), weights_ref[...]).astype(BF16)
    bias_row = jnp.broadcast_to(bias_ref[...].astype(F32).reshape(1, HIDDEN), (16, HIDDEN))
    bias = by_lanes(eye(HIDDEN), bias_row.astype(BF16))
    row, site = iota((HALF, SITES), 0), iota((HALF, SITES), 1)
    mine = jnp.where(site == 8 * (row >> 2) + 4 * core_ref[0] + (row & 3), 1.0, 0.0).astype(BF16)
    vec_ref[...] = jnp.zeros((8, SLOTS), F32)
    for core in range(CORES):
        part = slice(core * OWN_SLOTS, (core + 1) * OWN_SLOTS)
        sites = shared_ref[core, 0:SITES, :]
        extra = shared_ref[core, SITES:SIDE, :].astype(F32)
        st_ref[:, part] = sites
        half_ref[:, part] = dot(mine, sites).astype(BF16)
        tt_ref[:, part] = jnp.tanh(bias[:, 0:1] + dot(turned, sites)).astype(BF16)
        vec_ref[0:1, part] = extra[1:2, :]
        vec_ref[1:2, part] = extra[0:1, :]
    mask, energy = vec_ref[0:1, :], vec_ref[1:2, :]
    spins = half_ref[...].astype(F32)
    both = jnp.concatenate([(spins * energy).astype(BF16), (spins * mask).astype(BF16)], axis=0)
    tt = tt_ref[...]
    grad = by_lanes(both, tt)
    pair = row_pair(energy.astype(BF16), mask.astype(BF16))
    visible, hidden = by_lanes(st_ref[...], pair), by_lanes(pair, tt)
    for k, scalars in enumerate(((total(energy),), ())):
        tail = tail_of(visible[:, k : k + 1], hidden[k : k + 1], scalars)
        store_rows(out_ref, ROWS * k, grad[HALF * k : HALF * (k + 1)], tail)


def arrived(in_ref, first):
    rows = slice(first, first + ROWS)
    acc = [in_ref[c, rows, :].astype(F32) for c in range(4)]
    for c in range(4, OWNERS):
        acc[c % 4] = acc[c % 4] + in_ref[c, rows, :].astype(F32)
    acc = (acc[0] + acc[1]) + (acc[2] + acc[3])
    tail = combined(acc[:, HIDDEN:WIDE])
    scalars = [tail[1:2, FIRST + 3 * i : FIRST + 3 * i + 1] for i in range(SCALARS)]
    return acc[:, 0:HIDDEN], tail, scalars


def lanes_of(values):
    lane = iota((8, TAIL), 1)
    out = jnp.zeros((8, TAIL), F32)
    for i, value in enumerate(values):
        out = jnp.where(lane == i, value, out)
    return out


def first_own_kernel(in_ref, vec_ref, res_ref, ones_ref, vec_out_ref, copies_ref):
    energy, energy_tail, scalars = arrived(in_ref, 0)
    ones, ones_tail, _ = arrived(in_ref, ROWS)
    mean = scalars[0] / TOTAL
    res_ref[:, 0:HIDDEN] = energy - mean * ones
    res_ref[:, HIDDEN:WIDE] = energy_tail - mean * ones_tail
    ones_ref[:, 0:HIDDEN] = ones
    ones_ref[:, HIDDEN:WIDE] = ones_tail
    mask, raw = vec_ref[0:1, :], vec_ref[1:2, :]
    vec_out_ref[0:1, :] = mask
    vec_out_ref[1:2, :] = raw - mean * mask
    vec_out_ref[2:8, :] = jnp.zeros((6, SLOTS), F32)
    store_copies(copies_ref, res_ref[...])


def push_kernel(in_ref, st_ref, half_ref, tt_ref, parts_ref, small_ref, rows_ref, tail_ref):
    for c in range(OWNERS):
        block = in_ref[c].astype(F32)
        rows_ref[ROWS * c : ROWS * (c + 1), :] = block[:, 0:HIDDEN]
        tail_ref[8 * c : 8 * c + ROWS, :] = block[:, HIDDEN:WIDE]
        tail_ref[8 * c + ROWS : 8 * c + 8, :] = block[:, HIDDEN:WIDE]
    lane, row = iota((SITES, TAIL), 1), iota((SITES, TAIL), 0)
    tail = tail_ref[...]
    l, j = iota((TAIL, HIDDEN), 0), iota((TAIL, HIDDEN), 1) & 15
    spread = dot(tail.astype(BF16), jnp.where((l == 8 + j) | (l == 24 + j), 1.0, 0.0).astype(BF16))
    hidden = jnp.sum(jnp.where(own_hidden((SITES, HIDDEN)), spread, 0.0), axis=0, keepdims=True)
    seen = jnp.where((lane < 4) & ((lane & 2) == ((row & 4) >> 1)), tail, 0.0).astype(BF16)
    a, b = iota((16, TAIL), 0), iota((16, TAIL), 1)
    pair = by_lanes(jnp.where((b < 4) & ((b & 1) == a), 1.0, 0.0).astype(BF16), seen)
    small_ref[...] = jnp.zeros((8, HIDDEN), F32)
    small_ref[0:1, :] = hidden * float(CORES)
    small_ref[1:2, 0:SITES] = (pair[0:1, :] + pair[1:2, :]) * float(CORES * REPS)
    tt = tt_ref[...]
    side = dot(row_pair(*two(hidden)), tt) + dot(pair.astype(BF16), st_ref[...])
    turned = jnp.transpose(rows_ref[...]).astype(BF16)
    mixture = dot(turned, half_ref[...])
    values = jnp.sum(mixture * tt.astype(F32), axis=0, keepdims=True)
    values = (values + side[0:1, :] + side[1:2, :]) * (1.0 / TOTAL)
    packed = jnp.concatenate([values[:, 0:OWN_SLOTS], values[:, OWN_SLOTS:]], axis=0).astype(BF16)
    for p in range(CORES * REPS):
        parts_ref[p] = packed


def row_sum(parts_ref, mask):
    values = parts_ref[0].astype(F32)
    for p in range(1, CORES * REPS):
        values = values + parts_ref[p].astype(F32)
    return jnp.concatenate([values[0:1, :], values[1:2, :]], axis=1) * mask


def iteration_scalars(vec_ref, values):
    res, before, o_before, start = (vec_ref[i : i + 1, :] for i in (1, 2, 3, 4))
    return (
        total(res * values),
        total(values * values),
        total(values),
        total(values * o_before),
        total(values * before),
        total(res * o_before),
        total(values * start),
    )


def pull_kernel(parts_ref, vec_ref, st_ref, half_ref, tt_ref, vec_out_ref, out_ref):
    values = row_sum(parts_ref, vec_ref[0:1, :])
    vec_out_ref[...] = vec_ref[...]
    vec_out_ref[5:6, :] = values
    grad, visible, hidden = pull(values, st_ref[...], half_ref[...], tt_ref[...])
    store_rows(out_ref, 0, grad, tail_of(visible, hidden, iteration_scalars(vec_ref, values)))


def conjugate(scalars, past):
    r_zr, zr_zr, zr_sum, zr_zd, zr_d, r_zd, zr_start = scalars[:7]
    if past is None:
        beta, zd_sum, zd_zd, zd_d = None, zr_sum, zr_zr, r_zr
    else:
        rr, sum_before, zz_before, zd_before = past
        beta = r_zr / rr
        zd_sum = zr_sum + beta * sum_before
        zd_zd = zr_zr + 2.0 * beta * zr_zd + beta * beta * zz_before
        zd_d = r_zr + beta * (zr_d + r_zd) + beta * beta * zd_before
    step = r_zr / (zd_zd - zd_sum * zd_sum / TOTAL + SHIFT * zd_d)
    return beta, step, (r_zr, zd_sum, zd_zd, zd_d)


def own_kernel(first, *refs):
    if first:
        in_ref, vec_ref, res_ref, ones_ref, sc_out, vec_out, res_out, dir_out, img_out, copies_ref = refs
    else:
        (in_ref, vec_ref, res_ref, ones_ref, sc_ref, dir_ref, img_ref,
         sc_out, vec_out, res_out, copies_ref) = refs
    grad, tail, scalars = arrived(in_ref, 0)
    past = None if first else tuple(sc_ref[0:1, i : i + 1] for i in range(4))
    beta, step, now = conjugate(scalars, past)
    mean = scalars[2] / TOTAL
    zd_mean = now[1] / TOTAL
    if first:
        kept = (step, now[3])
    else:
        d0_zd1 = scalars[6] + beta * sc_ref[0:1, 5:6]
        kept = (sc_ref[0:1, 4:5], sc_ref[0:1, 5:6], step, now[3], d0_zd1, beta)
    sc_out[...] = lanes_of(now + kept)
    for part, new in ((slice(0, HIDDEN), grad), (slice(HIDDEN, WIDE), tail)):
        image, direction = new - mean * ones_ref[:, part], res_ref[:, part]
        if not first:
            image = image + beta * img_ref[:, part]
            direction = direction + beta * dir_ref[:, part]
        if first:
            img_out[:, part] = image
            dir_out[:, part] = direction
        res_out[:, part] = res_ref[:, part] - step * (image + SHIFT * direction)
    mask, res, o_res = vec_ref[0:1, :], vec_ref[1:2, :], vec_ref[5:6, :]
    direction, o_dir = res, o_res
    if not first:
        direction = direction + beta * vec_ref[2:3, :]
        o_dir = o_dir + beta * vec_ref[3:4, :]
    vec_out[0:1, :] = mask
    vec_out[1:2, :] = res - step * (o_dir - zd_mean * mask + SHIFT * direction)
    vec_out[2:3, :] = direction
    vec_out[3:4, :] = o_dir
    vec_out[4:5, :] = direction if first else vec_ref[4:5, :]
    vec_out[5:8, :] = jnp.zeros((3, SLOTS), F32)
    store_copies(copies_ref, res_out[...])


def last_scalars_kernel(parts_ref, vec_ref, out_ref):
    values = row_sum(parts_ref, vec_ref[0:1, :])
    lane = iota((OWNERS, TAIL), 1)
    out = jnp.zeros((OWNERS, TAIL), F32)
    for i, value in enumerate(iteration_scalars(vec_ref, values)):
        out = jnp.where(lane == i, value, out)
    out_ref[...] = out


def last_kernel(rep_ref, in_ref, sc_ref, r0_ref, r1_ref, r2_ref, v0_ref, v1_ref, v2_ref, vis_ref, hid_ref, mat_ref):
    summed = jnp.sum(in_ref[...], axis=0, keepdims=True)
    scalars = [summed[:, i : i + 1] for i in range(SCALARS)]
    keep = [sc_ref[0:1, i : i + 1] for i in range(10)]
    beta2, step2, now = conjugate(scalars, tuple(keep[0:4]))
    step0, d0_zd0, step1, d1_zd1, d0_zd1, beta1 = keep[4:10]
    d0_zd2 = scalars[6] + beta2 * d0_zd1
    d1_zd2 = scalars[4] + beta2 * d1_zd1
    norm = step0 * step0 * d0_zd0 + step1 * step1 * d1_zd1 + step2 * step2 * now[3]
    norm = norm + 2.0 * (step0 * step1 * d0_zd1 + step0 * step2 * d0_zd2 + step1 * step2 * d1_zd2)
    params = float(SITES * HIDDEN * REPS + HIDDEN * REPS + SITES)
    scale = lax.rsqrt(norm / (TOTAL * params) + EPSILON) / TOTAL
    w1 = scale * (step1 + step2 * beta2)
    weights = (scale * step0 + w1 * beta1, w1, scale * step2)
    mat_ref[...] = sum(w * ref[:, 0:HIDDEN] for w, ref in zip(weights, (r0_ref, r1_ref, r2_ref)))
    small = sum(w * ref[...] for w, ref in zip(weights, (v0_ref, v1_ref, v2_ref)))
    hid_ref[...] = small[0]
    a, b = iota((SITES, TAIL), 0), iota((SITES, TAIL), 1)
    pick = jnp.where(a == 32 * rep_ref[0] + b, 1.0, 0.0).astype(F32)
    vis_ref[...] = dot(small[:, 0:SITES], pick, precision=HIGH)[1, 0:32]


def shape(dims, dtype=F32):
    return jax.ShapeDtypeStruct(dims, dtype)


def call(kernel, outs, name, n_in, smem=(), scratch=()):
    vmem = pl.BlockSpec(memory_space=pltpu.VMEM)
    scalar = pl.BlockSpec(memory_space=pltpu.SMEM)
    return pl.pallas_call(
        kernel,
        out_shape=outs,
        in_specs=[scalar if i in smem else vmem for i in range(n_in)],
        out_specs=[vmem] * len(outs),
        scratch_shapes=list(scratch),
        name=name,
        compiler_params=pltpu.CompilerParams(vmem_limit_bytes=VMEM_LIMIT),
    )


def exchanged(blocks, axes):
    return lax.all_to_all(blocks, axes, split_axis=0, concat_axis=0, tiled=True)


def place(axis):
    return lax.axis_index(axis)[None].astype(jnp.int32)


def in_hbm(*arrays):
    return [pltpu.with_memory_space_constraint(a, pltpu.HBM) for a in arrays]


def per_device(spins, energies, counts, accepted, hidden_bias, weights):
    rows = shape((OWNERS, ROWS, WIDE), BF16)
    own = shape((ROWS, WIDE))
    vec_shape = shape((8, SLOTS))
    core, rep = place("chain_2"), place("rep")
    (shared,) = call(share_kernel, [shape((CORES, SIDE, OWN_SLOTS), BF16)], "share", 6, smem=(0, 1, 2))(
        counts, core, rep, *in_hbm(spins, energies, accepted)
    )
    spins_and_acts = [shape((n, SLOTS), BF16) for n in (SITES, HALF, HIDDEN)]
    *operands, vec, blocks = call(
        setup_kernel,
        [*spins_and_acts, vec_shape, shape((OWNERS, 2 * ROWS, WIDE), BF16)],
        "setup", 4, smem=(0,),
    )(core, exchanged(shared, "chain_2"), *in_hbm(weights, hidden_bias))
    res, ones, vec, copies = call(first_own_kernel, [own, own, vec_shape, rows], "first_own", 2)(
        exchanged(blocks, CHIPS), vec
    )

    def push(copies):
        parts, small = call(
            push_kernel, [shape((CORES * REPS, 2, OWN_SLOTS), BF16), shape((8, HIDDEN))], "push", 4,
            scratch=[pltpu.VMEM((HALF, HIDDEN), F32), pltpu.VMEM((SITES, TAIL), F32)],
        )(exchanged(copies, CHIPS), *operands)
        return exchanged(parts, UNITS), small

    state, smalls, residuals = (), [], [res]
    for iteration in range(2):
        parts, small = push(copies)
        vec, blocks = call(pull_kernel, [vec_shape, rows], "pull", 5)(parts, vec, *operands)
        first = iteration == 0
        sc, vec, res, *state, copies = call(
            lambda *refs, first=first: own_kernel(first, *refs),
            [shape((8, TAIL)), vec_shape, own, *([own, own] if first else []), rows], "own", 4 + len(state),
        )(exchanged(blocks, CHIPS), vec, res, ones, *state)
        state = (sc, *state)
        smalls.append(small)
        residuals.append(res)
    parts, small = push(copies)
    smalls.append(small)
    (sums,) = call(last_scalars_kernel, [shape((OWNERS, TAIL))], "last_scalars", 2)(parts, vec)
    return call(
        last_kernel, [shape((32,)), shape((HIDDEN,)), shape((ROWS, HIDDEN))], "last", 9, smem=(0,)
    )(rep, exchanged(sums, CHIPS), sc, *residuals, *smalls)


def solution(mesh):
    split = Mesh(
        mesh.devices.reshape(4, 8, 2, mesh.shape["rep"]), ("chain_0", "chain_1", "chain_2", "rep")
    )
    in_specs = (P(CHAIN, None), P(CHAIN), P(CHAIN), P(CHAIN, None), P("rep"), P(None, "rep"))
    out_specs = (P("rep"), P("rep"), P(CHAIN, "rep"))
    return jax.shard_map(
        per_device, mesh=split, in_specs=in_specs, out_specs=out_specs, check_vma=False
    )
```

time: 183 us -> 177 us (0.967)
  blocking collectives: 164 us -> 154 us
  Pallas kernels: 14.8 us -> 20.7 us
    all_to_all x11, blocking collectives: 164 us -> 154 us  [exchanged(): return lax.all_to_all(blocks, axes, split_axis=0, concat_axis=0, tiled=True)]
    pallas_call x7, Pallas kernels: 11.6 us -> 17.5 us  [the longest x3 5.47 us: push(): call(push_kernel, [shape((CORES * REPS, 2, OWN_SLOTS), BF16), shape((8, H...]
where the time goes in v4:
time: 177 us; the launch traced here: 176 us
  blocking collectives  154 us (87%)
  Pallas kernels  20.7 us (12%)
    all_to_all x11, blocking collectives, exchanged(): return lax.all_to_all(blocks, axes, split_axis=0, concat_axis=0, tiled=True)  154 us
    pallas_call x3, Pallas kernels, push(): call(push_kernel, [shape((CORES * REPS, 2, OWN_SLOTS), BF16), shape((8, H...  5.47 us
    pallas_call x2, Pallas kernels, per_device(): call(pull_kernel, [vec_shape, rows], 'pull', 5)(parts, vec, *operands)  5.43 us
    pallas_call x1, Pallas kernels, per_device(): call(setup_kernel, [*spins_and_acts, vec_shape, shape((OWNERS, 2 * ROWS,...  5.43 us

profile of v4, /device:TPU:1, one launch (start us, length us, event | category | flops | bytes accessed | tf_op | source)
XLA Modules:
  0.0 176.3 jit_solution(2175833882883648337)
XLA Ops:
  1.3 1.7 share.1
  3.0 11.5 %all_to_all.61.shared_ref = bf16[2,272,1536]{2,1,0:T(8,128)(2,1)S(1)} all-to-all(bf16[2,272,1536]{2,1,0:T(8,128)(2,1)S(1)} %share.1), channel_id=1, replica_groups=mesh['chain_0'=4,'chain_1'=8,'chain_2'=2,'rep'=8] {'chain_2'}, dimensions={0} | all-to-all | bytes 3342336 | tf_op jit(solution)/shard_map/all_to_all | solution.py:378
  14.5 5.4 %setup.1 = (bf16[256,3072]{1,0:T(8,128)(2,1)S(1)}, bf16[128,3072]{1,0:T(8,128)(2,1)S(1)}, bf16[512,3072]{1,0:T(8,128)(2,1)S(1)}, f32[8,3072]{1,0:T(8,128)S(1)}, bf16[32,8,640]{2,1,0:T(8,128)(2,1)S(1)}) custom-call(s32[1]{0:T(128)} %bitcast.1.core_ref, bf16[2,272,1536]{2,1,0:T(8,128)(2,1)S(1)} %all_to_all.61.shared_ref, bf16[256,512]{1,0:T(8,128)(2,1)} %weights_ref.1, ...), custom_call_target="tpu_custom_call" | custom-call | tf_op jit(solution)/shard_map/setup/pallas_call | solution.py:398
  19.9 17.8 %all_to_all.62.in_ref = bf16[32,8,640]{2,1,0:T(8,128)(2,1)S(1)} all-to-all(bf16[32,8,640]{2,1,0:T(8,128)(2,1)S(1)} %get-tuple-element.32), channel_id=1, replica_groups=mesh['chain_0'=4,'chain_1'=8,'chain_2'=2,'rep'=8] {'chain_0','chain_1'}, dimensions={0} | all-to-all | bytes 655360 | tf_op jit(solution)/shard_map/all_to_all | solution.py:378
  37.7 0.3 first_own.1
  38.0 16.6 %all_to_all.63.in_ref = bf16[32,4,640]{2,1,0:T(4,128)(2,1)S(1)} all-to-all(bf16[32,4,640]{2,1,0:T(4,128)(2,1)S(1)} %get-tuple-element.34), channel_id=1, replica_groups=mesh['chain_0'=4,'chain_1'=8,'chain_2'=2,'rep'=8] {'chain_0','chain_1'}, dimensions={0} | all-to-all | bytes 327680 | tf_op jit(solution)/shard_map/all_to_all | solution.py:378
  54.6 1.8 %push.3 = (bf16[16,2,1536]{2,1,0:T(2,128)(2,1)S(1)}, f32[8,512]{1,0:T(8,128)S(1)}) custom-call(bf16[32,4,640]{2,1,0:T(4,128)(2,1)S(1)} %all_to_all.63.in_ref, bf16[256,3072]{1,0:T(8,128)(2,1)S(1)} %get-tuple-element.35.st_ref, bf16[128,3072]{1,0:T(8,128)(2,1)S(1)} %get-tuple-element.36.half_ref, bf16[512,3072]{1,0:T(8,128)(2,1)S(1)} %get-tuple-element.37.tt_ref), custom_call_target="tpu_custom_call" | custom-call | tf_op jit(solution)/shard_map/push/pallas_call | solution.py:408
  56.4 16.8 %all_to_all.64.parts_ref = bf16[16,2,1536]{2,1,0:T(2,128)(2,1)S(1)} all-to-all(bf16[16,2,1536]{2,1,0:T(2,128)(2,1)S(1)} %get-tuple-element.38), channel_id=1, replica_groups=mesh['chain_0'=4,'chain_1'=8,'chain_2'=2,'rep'=8] {'chain_2','rep'}, dimensions={0} | all-to-all | bytes 196608 | tf_op jit(solution)/shard_map/all_to_all | solution.py:378
  73.2 2.7 %pull.2 = (f32[8,3072]{1,0:T(8,128)S(1)}, bf16[32,4,640]{2,1,0:T(4,128)(2,1)S(1)}) custom-call(bf16[16,2,1536]{2,1,0:T(2,128)(2,1)S(1)} %all_to_all.64.parts_ref, f32[8,3072]{1,0:T(8,128)S(1)} %get-tuple-element.39.vec_ref, bf16[256,3072]{1,0:T(8,128)(2,1)S(1)} %get-tuple-element.35.st_ref, bf16[128,3072]{1,0:T(8,128)(2,1)S(1)} %get-tuple-element.36.half_ref, ...), custom_call_target="tpu_custom_call" | custom-call | tf_op jit(solution)/shard_map/pull/pallas_call | solution.py:417
  75.9 12.7 %all_to_all.65.refs_0_ = bf16[32,4,640]{2,1,0:T(4,128)(2,1)S(1)} all-to-all(bf16[32,4,640]{2,1,0:T(4,128)(2,1)S(1)} %get-tuple-element.40), channel_id=1, replica_groups=mesh['chain_0'=4,'chain_1'=8,'chain_2'=2,'rep'=8] {'chain_0','chain_1'}, dimensions={0} | all-to-all | bytes 327680 | tf_op jit(solution)/shard_map/all_to_all | solution.py:378
  88.6 0.4 own.2
  89.1 13.0 %all_to_all.66.in_ref = bf16[32,4,640]{2,1,0:T(4,128)(2,1)S(1)} all-to-all(bf16[32,4,640]{2,1,0:T(4,128)(2,1)S(1)} %get-tuple-element.44), channel_id=1, replica_groups=mesh['chain_0'=4,'chain_1'=8,'chain_2'=2,'rep'=8] {'chain_0','chain_1'}, dimensions={0} | all-to-all | bytes 327680 | tf_op jit(solution)/shard_map/all_to_all | solution.py:378
  102.1 1.8 %push.4 = (bf16[16,2,1536]{2,1,0:T(2,128)(2,1)S(1)}, f32[8,512]{1,0:T(8,128)S(1)}) custom-call(bf16[32,4,640]{2,1,0:T(4,128)(2,1)S(1)} %all_to_all.66.in_ref, bf16[256,3072]{1,0:T(8,128)(2,1)S(1)} %get-tuple-element.35.st_ref, bf16[128,3072]{1,0:T(8,128)(2,1)S(1)} %get-tuple-element.36.half_ref, bf16[512,3072]{1,0:T(8,128)(2,1)S(1)} %get-tuple-element.37.tt_ref), custom_call_target="tpu_custom_call" | custom-call | tf_op jit(solution)/shard_map/push/pallas_call | solution.py:408
  104.0 14.1 %all_to_all.67.parts_ref = bf16[16,2,1536]{2,1,0:T(2,128)(2,1)S(1)} all-to-all(bf16[16,2,1536]{2,1,0:T(2,128)(2,1)S(1)} %get-tuple-element.45), channel_id=1, replica_groups=mesh['chain_0'=4,'chain_1'=8,'chain_2'=2,'rep'=8] {'chain_2','rep'}, dimensions={0} | all-to-all | bytes 196608 | tf_op jit(solution)/shard_map/all_to_all | solution.py:378
  118.0 2.7 %pull.3 = (f32[8,3072]{1,0:T(8,128)S(1)}, bf16[32,4,640]{2,1,0:T(4,128)(2,1)S(1)}) custom-call(bf16[16,2,1536]{2,1,0:T(2,128)(2,1)S(1)} %all_to_all.67.parts_ref, f32[8,3072]{1,0:T(8,128)S(1)} %get-tuple-element.46.vec_ref, bf16[256,3072]{1,0:T(8,128)(2,1)S(1)} %get-tuple-element.35.st_ref, bf16[128,3072]{1,0:T(8,128)(2,1)S(1)} %get-tuple-element.36.half_ref, ...), custom_call_target="tpu_custom_call" | custom-call | tf_op jit(solution)/shard_map/pull/pallas_call | solution.py:417
  120.7 12.6 %all_to_all.68.refs_0_ = bf16[32,4,640]{2,1,0:T(4,128)(2,1)S(1)} all-to-all(bf16[32,4,640]{2,1,0:T(4,128)(2,1)S(1)} %get-tuple-element.47), channel_id=1, replica_groups=mesh['chain_0'=4,'chain_1'=8,'chain_2'=2,'rep'=8] {'chain_0','chain_1'}, dimensions={0} | all-to-all | bytes 327680 | tf_op jit(solution)/shard_map/all_to_all | solution.py:378
  133.3 0.6 own.3
  133.9 13.1 %all_to_all.69.in_ref = bf16[32,4,640]{2,1,0:T(4,128)(2,1)S(1)} all-to-all(bf16[32,4,640]{2,1,0:T(4,128)(2,1)S(1)} %get-tuple-element.53), channel_id=1, replica_groups=mesh['chain_0'=4,'chain_1'=8,'chain_2'=2,'rep'=8] {'chain_0','chain_1'}, dimensions={0} | all-to-all | bytes 327680 | tf_op jit(solution)/shard_map/all_to_all | solution.py:378
  146.9 1.8 %push.5 = (bf16[16,2,1536]{2,1,0:T(2,128)(2,1)S(1)}, f32[8,512]{1,0:T(8,128)S(1)}) custom-call(bf16[32,4,640]{2,1,0:T(4,128)(2,1)S(1)} %all_to_all.69.in_ref, bf16[256,3072]{1,0:T(8,128)(2,1)S(1)} %get-tuple-element.35.st_ref, bf16[128,3072]{1,0:T(8,128)(2,1)S(1)} %get-tuple-element.36.half_ref, bf16[512,3072]{1,0:T(8,128)(2,1)S(1)} %get-tuple-element.37.tt_ref), custom_call_target="tpu_custom_call" | custom-call | tf_op jit(solution)/shard_map/push/pallas_call | solution.py:408
  148.8 14.1 %all_to_all.70.parts_ref = bf16[16,2,1536]{2,1,0:T(2,128)(2,1)S(1)} all-to-all(bf16[16,2,1536]{2,1,0:T(2,128)(2,1)S(1)} %get-tuple-element.54), channel_id=1, replica_groups=mesh['chain_0'=4,'chain_1'=8,'chain_2'=2,'rep'=8] {'chain_2','rep'}, dimensions={0} | all-to-all | bytes 196608 | tf_op jit(solution)/shard_map/all_to_all | solution.py:378
  162.8 0.2 last_scalars.1
  163.1 12.0 %all_to_all.71 = f32[32,1,128]{2,1,0:T(1,128)S(1)} all-to-all(f32[32,1,128]{2,1,0:T(1,128)S(1)} %bitcast.7), channel_id=1, replica_groups=mesh['chain_0'=4,'chain_1'=8,'chain_2'=2,'rep'=8] {'chain_0','chain_1'}, dimensions={0} | all-to-all | bytes 32768 | tf_op jit(solution)/shard_map/all_to_all | solution.py:378
  175.0 1.2 last.1

commit v5 on v4

--- a/solution.py
+++ b/solution.py
@@ -85,11 +85,12 @@
 def pull(weights, st, half, tt):
     high, low = two(weights)
     spins = half.astype(F32)
-    both = jnp.concatenate([(spins * high.astype(F32)).astype(BF16), (spins * low.astype(F32)).astype(BF16)], axis=0)
-    grad = by_lanes(both, tt)
     pair = row_pair(high, low)
-    visible, hidden = by_lanes(st, pair), by_lanes(pair, tt)
-    return grad[:HALF] + grad[HALF:], visible[:, 0:1] + visible[:, 1:2], hidden[0:1, :] + hidden[1:2, :]
+    rows = [(spins * high.astype(F32)).astype(BF16), (spins * low.astype(F32)).astype(BF16), pair]
+    grad = by_lanes(jnp.concatenate(rows, axis=0), tt)
+    visible = by_lanes(st, pair)
+    hidden = grad[2 * HALF : 2 * HALF + 1] + grad[2 * HALF + 1 : 2 * HALF + 2]
+    return grad[:HALF] + grad[HALF : 2 * HALF], visible[:, 0:1] + visible[:, 1:2], hidden
 
 
 def tail_of(visible, hidden, scalars):
@@ -138,7 +139,9 @@
         out_ref[c, :, HIDDEN:WIDE] = packed
 
 
-def share_kernel(count_ref, core_ref, rep_ref, spins_ref, energy_ref, accepted_ref, out_ref):
+def share_kernel(
+    count_ref, core_ref, rep_ref, spins_ref, energy_ref, accepted_ref, weights_ref, bias_ref, out_ref, turned_ref
+):
     accepted = accepted_ref[...]
     live = iota((16, OWN_SLOTS), 1) < count_ref[0]
     major = jnp.where((iota((16, OWN_SLOTS), 0) == (accepted >> 7)) & live, 1.0, 0.0).astype(BF16)
@@ -151,12 +154,14 @@
     for core in range(CORES):
         out_ref[core, 0:SITES, :] = sites
         out_ref[core, SITES:SIDE, :] = extra
-
-
-def setup_kernel(core_ref, shared_ref, weights_ref, bias_ref, st_ref, half_ref, tt_ref, vec_ref, out_ref):
-    turned = by_lanes(eye(HIDDEN), weights_ref[...]).astype(BF16)
     bias_row = jnp.broadcast_to(bias_ref[...].astype(F32).reshape(1, HIDDEN), (16, HIDDEN))
-    bias = by_lanes(eye(HIDDEN), bias_row.astype(BF16))
+    turned_ref[:, 0:SITES] = by_lanes(eye(HIDDEN), weights_ref[...]).astype(BF16)
+    turned_ref[:, SITES:SIDE] = by_lanes(eye(HIDDEN), bias_row.astype(BF16)).astype(BF16)
+
+
+def setup_kernel(core_ref, shared_ref, turned_ref, st_ref, half_ref, tt_ref, vec_ref, out_ref):
+    turned = turned_ref[:, 0:SITES]
+    bias = turned_ref[:, SITES : SITES + 1].astype(F32)
     row, site = iota((HALF, SITES), 0), iota((HALF, SITES), 1)
     mine = jnp.where(site == 8 * (row >> 2) + 4 * core_ref[0] + (row & 3), 1.0, 0.0).astype(BF16)
     vec_ref[...] = jnp.zeros((8, SLOTS), F32)
@@ -165,17 +170,17 @@
         sites = shared_ref[core, 0:SITES, :]
         extra = shared_ref[core, SITES:SIDE, :].astype(F32)
         st_ref[:, part] = sites
-        half_ref[:, part] = dot(mine, sites).astype(BF16)
-        tt_ref[:, part] = jnp.tanh(bias[:, 0:1] + dot(turned, sites)).astype(BF16)
+        half_ref[0:HALF, part] = dot(mine, sites).astype(BF16)
+        half_ref[HALF:, part] = jnp.ones((16, OWN_SLOTS), BF16)
+        tt_ref[:, part] = jnp.tanh(bias + dot(turned, sites)).astype(BF16)
         vec_ref[0:1, part] = extra[1:2, :]
         vec_ref[1:2, part] = extra[0:1, :]
     mask, energy = vec_ref[0:1, :], vec_ref[1:2, :]
-    spins = half_ref[...].astype(F32)
-    both = jnp.concatenate([(spins * energy).astype(BF16), (spins * mask).astype(BF16)], axis=0)
-    tt = tt_ref[...]
-    grad = by_lanes(both, tt)
+    spins = half_ref[0:HALF, :].astype(F32)
     pair = row_pair(energy.astype(BF16), mask.astype(BF16))
-    visible, hidden = by_lanes(st_ref[...], pair), by_lanes(pair, tt)
+    rows = [(spins * energy).astype(BF16), (spins * mask).astype(BF16), pair]
+    grad = by_lanes(jnp.concatenate(rows, axis=0), tt_ref[...])
+    visible, hidden = by_lanes(st_ref[...], pair), grad[2 * HALF :]
     for k, scalars in enumerate(((total(energy),), ())):
         tail = tail_of(visible[:, k : k + 1], hidden[k : k + 1], scalars)
         store_rows(out_ref, ROWS * k, grad[HALF * k : HALF * (k + 1)], tail)
@@ -232,11 +237,11 @@
     small_ref[...] = jnp.zeros((8, HIDDEN), F32)
     small_ref[0:1, :] = hidden * float(CORES)
     small_ref[1:2, 0:SITES] = (pair[0:1, :] + pair[1:2, :]) * float(CORES * REPS)
-    tt = tt_ref[...]
-    side = dot(row_pair(*two(hidden)), tt) + dot(pair.astype(BF16), st_ref[...])
+    side = dot(pair.astype(BF16), st_ref[...])
     turned = jnp.transpose(rows_ref[...]).astype(BF16)
-    mixture = dot(turned, half_ref[...])
-    values = jnp.sum(mixture * tt.astype(F32), axis=0, keepdims=True)
+    columns = by_lanes(eye(HIDDEN), row_pair(*two(hidden))).astype(BF16)
+    mixture = dot(jnp.concatenate([turned, columns], axis=1), half_ref[...])
+    values = jnp.sum(mixture * tt_ref[...].astype(F32), axis=0, keepdims=True)
     values = (values + side[0:1, :] + side[1:2, :]) * (1.0 / TOTAL)
     packed = jnp.concatenate([values[:, 0:OWN_SLOTS], values[:, OWN_SLOTS:]], axis=0).astype(BF16)
     for p in range(CORES * REPS):
@@ -267,7 +272,7 @@
     values = row_sum(parts_ref, vec_ref[0:1, :])
     vec_out_ref[...] = vec_ref[...]
     vec_out_ref[5:6, :] = values
-    grad, visible, hidden = pull(values, st_ref[...], half_ref[...], tt_ref[...])
+    grad, visible, hidden = pull(values, st_ref[...], half_ref[0:HALF, :], tt_ref[...])
     store_rows(out_ref, 0, grad, tail_of(visible, hidden, iteration_scalars(vec_ref, values)))
 
 
@@ -391,15 +396,15 @@
     own = shape((ROWS, WIDE))
     vec_shape = shape((8, SLOTS))
     core, rep = place("chain_2"), place("rep")
-    (shared,) = call(share_kernel, [shape((CORES, SIDE, OWN_SLOTS), BF16)], "share", 6, smem=(0, 1, 2))(
-        counts, core, rep, *in_hbm(spins, energies, accepted)
-    )
-    spins_and_acts = [shape((n, SLOTS), BF16) for n in (SITES, HALF, HIDDEN)]
+    shared, turned = call(
+        share_kernel, [shape((CORES, SIDE, OWN_SLOTS), BF16), shape((HIDDEN, SIDE), BF16)], "share", 8, smem=(0, 1, 2)
+    )(counts, core, rep, *in_hbm(spins, energies, accepted, weights, hidden_bias))
+    spins_and_acts = [shape((n, SLOTS), BF16) for n in (SITES, HALF + 16, HIDDEN)]
     *operands, vec, blocks = call(
         setup_kernel,
         [*spins_and_acts, vec_shape, shape((OWNERS, 2 * ROWS, WIDE), BF16)],
-        "setup", 4, smem=(0,),
-    )(core, exchanged(shared, "chain_2"), *in_hbm(weights, hidden_bias))
+        "setup", 3, smem=(0,),
+    )(core, exchanged(shared, "chain_2"), turned)
     res, ones, vec, copies = call(first_own_kernel, [own, own, vec_shape, rows], "first_own", 2)(
         exchanged(blocks, CHIPS), vec
     )

time: 177 us -> 174 us (0.983)
  Pallas kernels: 20.7 us -> 16.9 us
    pallas_call x1, Pallas kernels: 5.43 us -> 3.12 us  [per_device(): call(setup_kernel, [*spins_and_acts, vec_shape, shape((OWNERS, 2 * ROWS,...]
where the time goes in v5:
time: 174 us; the launch traced here: 172 us
  blocking collectives  154 us (89%)
  Pallas kernels  16.9 us (10%)
    all_to_all x11, blocking collectives, exchanged(): return lax.all_to_all(blocks, axes, split_axis=0, concat_axis=0, tiled=True)  154 us
    pallas_call x3, Pallas kernels, push(): call(push_kernel, [shape((CORES * REPS, 2, OWN_SLOTS), BF16), shape((8, H...  5.32 us
    pallas_call x2, Pallas kernels, per_device(): call(pull_kernel, [vec_shape, rows], 'pull', 5)(parts, vec, *operands)  3.67 us

profile of v5, /device:TPU:1, one launch (start us, length us, event | category | flops | bytes accessed | tf_op | source)
XLA Modules:
  0.0 172.4 jit_solution(2199595313419394311)
XLA Ops:
  1.3 2.0 %share.1 = (bf16[2,272,1536]{2,1,0:T(8,128)(2,1)S(1)}, bf16[512,272]{1,0:T(8,128)(2,1)S(1)}) custom-call(s32[1]{0:T(128)S(6)} %copy.10.count_ref, s32[1]{0:T(128)} %bitcast.1.core_ref, s32[1]{0:T(128)} %bitcast.rep_ref, bf16[1536,256]{1,0:T(8,128)(2,1)} %spins_ref.1, bf16[1536]{0:T(1024)(128)(2,1)} %energy_ref.1, s32[1,1536]{1,0:T(1,128)} %accepted_ref.1, ...), custom_call_target="tpu_custom_call" | custom-call | tf_op jit(solution)/shard_map/share/pallas_call | solution.py:399
  3.3 11.5 %all_to_all.61.shared_ref = bf16[2,272,1536]{2,1,0:T(8,128)(2,1)S(1)} all-to-all(bf16[2,272,1536]{2,1,0:T(8,128)(2,1)S(1)} %get-tuple-element.34), channel_id=1, replica_groups=mesh['chain_0'=4,'chain_1'=8,'chain_2'=2,'rep'=8] {'chain_2'}, dimensions={0} | all-to-all | bytes 3342336 | tf_op jit(solution)/shard_map/all_to_all | solution.py:383
  14.8 3.1 %setup.1 = (bf16[256,3072]{1,0:T(8,128)(2,1)S(1)}, bf16[144,3072]{1,0:T(8,128)(2,1)S(1)}, bf16[512,3072]{1,0:T(8,128)(2,1)S(1)}, f32[8,3072]{1,0:T(8,128)S(1)}, bf16[32,8,640]{2,1,0:T(8,128)(2,1)S(1)}) custom-call(s32[1]{0:T(128)} %bitcast.1.core_ref, bf16[2,272,1536]{2,1,0:T(8,128)(2,1)S(1)} %all_to_all.61.shared_ref, ...), custom_call_target="tpu_custom_call" | custom-call | tf_op jit(solution)/shard_map/setup/pallas_call | solution.py:403
  18.0 17.8 %all_to_all.62.in_ref = bf16[32,8,640]{2,1,0:T(8,128)(2,1)S(1)} all-to-all(bf16[32,8,640]{2,1,0:T(8,128)(2,1)S(1)} %get-tuple-element.36), channel_id=1, replica_groups=mesh['chain_0'=4,'chain_1'=8,'chain_2'=2,'rep'=8] {'chain_0','chain_1'}, dimensions={0} | all-to-all | bytes 655360 | tf_op jit(solution)/shard_map/all_to_all | solution.py:383
  35.8 0.3 first_own.1
  36.1 16.6 %all_to_all.63.in_ref = bf16[32,4,640]{2,1,0:T(4,128)(2,1)S(1)} all-to-all(bf16[32,4,640]{2,1,0:T(4,128)(2,1)S(1)} %get-tuple-element.38), channel_id=1, replica_groups=mesh['chain_0'=4,'chain_1'=8,'chain_2'=2,'rep'=8] {'chain_0','chain_1'}, dimensions={0} | all-to-all | bytes 327680 | tf_op jit(solution)/shard_map/all_to_all | solution.py:383
  52.6 1.8 %push.3 = (bf16[16,2,1536]{2,1,0:T(2,128)(2,1)S(1)}, f32[8,512]{1,0:T(8,128)S(1)}) custom-call(bf16[32,4,640]{2,1,0:T(4,128)(2,1)S(1)} %all_to_all.63.in_ref, bf16[256,3072]{1,0:T(8,128)(2,1)S(1)} %get-tuple-element.39.st_ref, bf16[144,3072]{1,0:T(8,128)(2,1)S(1)} %get-tuple-element.40.half_ref, bf16[512,3072]{1,0:T(8,128)(2,1)S(1)} %get-tuple-element.41.tt_ref), custom_call_target="tpu_custom_call" | custom-call | tf_op jit(solution)/shard_map/push/pallas_call | solution.py:413
  54.4 16.8 %all_to_all.64.parts_ref = bf16[16,2,1536]{2,1,0:T(2,128)(2,1)S(1)} all-to-all(bf16[16,2,1536]{2,1,0:T(2,128)(2,1)S(1)} %get-tuple-element.42), channel_id=1, replica_groups=mesh['chain_0'=4,'chain_1'=8,'chain_2'=2,'rep'=8] {'chain_2','rep'}, dimensions={0} | all-to-all | bytes 196608 | tf_op jit(solution)/shard_map/all_to_all | solution.py:383
  71.2 1.8 %pull.2 = (f32[8,3072]{1,0:T(8,128)S(1)}, bf16[32,4,640]{2,1,0:T(4,128)(2,1)S(1)}) custom-call(bf16[16,2,1536]{2,1,0:T(2,128)(2,1)S(1)} %all_to_all.64.parts_ref, f32[8,3072]{1,0:T(8,128)S(1)} %get-tuple-element.43.vec_ref, bf16[256,3072]{1,0:T(8,128)(2,1)S(1)} %get-tuple-element.39.st_ref, bf16[144,3072]{1,0:T(8,128)(2,1)S(1)} %get-tuple-element.40.half_ref, ...), custom_call_target="tpu_custom_call" | custom-call | tf_op jit(solution)/shard_map/pull/pallas_call | solution.py:422
  73.1 12.7 %all_to_all.65.refs_0_ = bf16[32,4,640]{2,1,0:T(4,128)(2,1)S(1)} all-to-all(bf16[32,4,640]{2,1,0:T(4,128)(2,1)S(1)} %get-tuple-element.44), channel_id=1, replica_groups=mesh['chain_0'=4,'chain_1'=8,'chain_2'=2,'rep'=8] {'chain_0','chain_1'}, dimensions={0} | all-to-all | bytes 327680 | tf_op jit(solution)/shard_map/all_to_all | solution.py:383
  85.8 0.4 own.2
  86.2 13.1 %all_to_all.66.in_ref = bf16[32,4,640]{2,1,0:T(4,128)(2,1)S(1)} all-to-all(bf16[32,4,640]{2,1,0:T(4,128)(2,1)S(1)} %get-tuple-element.48), channel_id=1, replica_groups=mesh['chain_0'=4,'chain_1'=8,'chain_2'=2,'rep'=8] {'chain_0','chain_1'}, dimensions={0} | all-to-all | bytes 327680 | tf_op jit(solution)/shard_map/all_to_all | solution.py:383
  99.3 1.8 %push.4 = (bf16[16,2,1536]{2,1,0:T(2,128)(2,1)S(1)}, f32[8,512]{1,0:T(8,128)S(1)}) custom-call(bf16[32,4,640]{2,1,0:T(4,128)(2,1)S(1)} %all_to_all.66.in_ref, bf16[256,3072]{1,0:T(8,128)(2,1)S(1)} %get-tuple-element.39.st_ref, bf16[144,3072]{1,0:T(8,128)(2,1)S(1)} %get-tuple-element.40.half_ref, bf16[512,3072]{1,0:T(8,128)(2,1)S(1)} %get-tuple-element.41.tt_ref), custom_call_target="tpu_custom_call" | custom-call | tf_op jit(solution)/shard_map/push/pallas_call | solution.py:413
  101.0 14.1 %all_to_all.67.parts_ref = bf16[16,2,1536]{2,1,0:T(2,128)(2,1)S(1)} all-to-all(bf16[16,2,1536]{2,1,0:T(2,128)(2,1)S(1)} %get-tuple-element.49), channel_id=1, replica_groups=mesh['chain_0'=4,'chain_1'=8,'chain_2'=2,'rep'=8] {'chain_2','rep'}, dimensions={0} | all-to-all | bytes 196608 | tf_op jit(solution)/shard_map/all_to_all | solution.py:383
  115.1 1.8 %pull.3 = (f32[8,3072]{1,0:T(8,128)S(1)}, bf16[32,4,640]{2,1,0:T(4,128)(2,1)S(1)}) custom-call(bf16[16,2,1536]{2,1,0:T(2,128)(2,1)S(1)} %all_to_all.67.parts_ref, f32[8,3072]{1,0:T(8,128)S(1)} %get-tuple-element.50.vec_ref, bf16[256,3072]{1,0:T(8,128)(2,1)S(1)} %get-tuple-element.39.st_ref, bf16[144,3072]{1,0:T(8,128)(2,1)S(1)} %get-tuple-element.40.half_ref, ...), custom_call_target="tpu_custom_call" | custom-call | tf_op jit(solution)/shard_map/pull/pallas_call | solution.py:422
  116.9 12.6 %all_to_all.68.refs_0_ = bf16[32,4,640]{2,1,0:T(4,128)(2,1)S(1)} all-to-all(bf16[32,4,640]{2,1,0:T(4,128)(2,1)S(1)} %get-tuple-element.51), channel_id=1, replica_groups=mesh['chain_0'=4,'chain_1'=8,'chain_2'=2,'rep'=8] {'chain_0','chain_1'}, dimensions={0} | all-to-all | bytes 327680 | tf_op jit(solution)/shard_map/all_to_all | solution.py:383
  129.5 0.6 own.3
  130.1 13.1 %all_to_all.69.in_ref = bf16[32,4,640]{2,1,0:T(4,128)(2,1)S(1)} all-to-all(bf16[32,4,640]{2,1,0:T(4,128)(2,1)S(1)} %get-tuple-element.57), channel_id=1, replica_groups=mesh['chain_0'=4,'chain_1'=8,'chain_2'=2,'rep'=8] {'chain_0','chain_1'}, dimensions={0} | all-to-all | bytes 327680 | tf_op jit(solution)/shard_map/all_to_all | solution.py:383
  143.1 1.8 %push.5 = (bf16[16,2,1536]{2,1,0:T(2,128)(2,1)S(1)}, f32[8,512]{1,0:T(8,128)S(1)}) custom-call(bf16[32,4,640]{2,1,0:T(4,128)(2,1)S(1)} %all_to_all.69.in_ref, bf16[256,3072]{1,0:T(8,128)(2,1)S(1)} %get-tuple-element.39.st_ref, bf16[144,3072]{1,0:T(8,128)(2,1)S(1)} %get-tuple-element.40.half_ref, bf16[512,3072]{1,0:T(8,128)(2,1)S(1)} %get-tuple-element.41.tt_ref), custom_call_target="tpu_custom_call" | custom-call | tf_op jit(solution)/shard_map/push/pallas_call | solution.py:413
  144.9 14.1 %all_to_all.70.parts_ref = bf16[16,2,1536]{2,1,0:T(2,128)(2,1)S(1)} all-to-all(bf16[16,2,1536]{2,1,0:T(2,128)(2,1)S(1)} %get-tuple-element.58), channel_id=1, replica_groups=mesh['chain_0'=4,'chain_1'=8,'chain_2'=2,'rep'=8] {'chain_2','rep'}, dimensions={0} | all-to-all | bytes 196608 | tf_op jit(solution)/shard_map/all_to_all | solution.py:383
  159.0 0.2 last_scalars.1
  159.2 12.0 %all_to_all.71 = f32[32,1,128]{2,1,0:T(1,128)S(1)} all-to-all(f32[32,1,128]{2,1,0:T(1,128)S(1)} %bitcast.7), channel_id=1, replica_groups=mesh['chain_0'=4,'chain_1'=8,'chain_2'=2,'rep'=8] {'chain_0','chain_1'}, dimensions={0} | all-to-all | bytes 32768 | tf_op jit(solution)/shard_map/all_to_all | solution.py:383
  171.2 1.2 last.1

commit v6 on v5

--- a/solution.py
+++ b/solution.py
@@ -140,10 +140,10 @@
 
 
 def share_kernel(
-    count_ref, core_ref, rep_ref, spins_ref, energy_ref, accepted_ref, weights_ref, bias_ref, out_ref, turned_ref
+    count_ref, spins_ref, energy_ref, accepted_ref, weights_ref, bias_ref, out_ref, turned_ref
 ):
     accepted = accepted_ref[...]
-    live = iota((16, OWN_SLOTS), 1) < count_ref[0]
+    live = iota((16, OWN_SLOTS), 1) < count_ref[...].reshape(1, 1)
     major = jnp.where((iota((16, OWN_SLOTS), 0) == (accepted >> 7)) & live, 1.0, 0.0).astype(BF16)
     minor = jnp.where(iota((TAIL, OWN_SLOTS), 0) == (accepted & 127), 1.0, 0.0).astype(BF16)
     table = by_lanes(major, minor)
@@ -159,24 +159,23 @@
     turned_ref[:, SITES:SIDE] = by_lanes(eye(HIDDEN), bias_row.astype(BF16)).astype(BF16)
 
 
-def setup_kernel(core_ref, shared_ref, turned_ref, st_ref, half_ref, tt_ref, vec_ref, out_ref):
+def setup_kernel(shared_ref, turned_ref, st_ref, half_ref, tt_ref, vec_ref, out_ref):
     turned = turned_ref[:, 0:SITES]
     bias = turned_ref[:, SITES : SITES + 1].astype(F32)
     row, site = iota((HALF, SITES), 0), iota((HALF, SITES), 1)
-    mine = jnp.where(site == 8 * (row >> 2) + 4 * core_ref[0] + (row & 3), 1.0, 0.0).astype(BF16)
+    mine = jnp.where(site == 8 * (row >> 2) + 4 * lax.axis_index("chain_2") + (row & 3), 1.0, 0.0).astype(BF16)
     vec_ref[...] = jnp.zeros((8, SLOTS), F32)
     for core in range(CORES):
         part = slice(core * OWN_SLOTS, (core + 1) * OWN_SLOTS)
         sites = shared_ref[core, 0:SITES, :]
         extra = shared_ref[core, SITES:SIDE, :].astype(F32)
         st_ref[:, part] = sites
-        half_ref[0:HALF, part] = dot(mine, sites).astype(BF16)
-        half_ref[HALF:, part] = jnp.ones((16, OWN_SLOTS), BF16)
+        half_ref[:, part] = dot(mine, sites).astype(BF16)
         tt_ref[:, part] = jnp.tanh(bias + dot(turned, sites)).astype(BF16)
         vec_ref[0:1, part] = extra[1:2, :]
         vec_ref[1:2, part] = extra[0:1, :]
     mask, energy = vec_ref[0:1, :], vec_ref[1:2, :]
-    spins = half_ref[0:HALF, :].astype(F32)
+    spins = half_ref[...].astype(F32)
     pair = row_pair(energy.astype(BF16), mask.astype(BF16))
     rows = [(spins * energy).astype(BF16), (spins * mask).astype(BF16), pair]
     grad = by_lanes(jnp.concatenate(rows, axis=0), tt_ref[...])
@@ -238,10 +237,10 @@
     small_ref[0:1, :] = hidden * float(CORES)
     small_ref[1:2, 0:SITES] = (pair[0:1, :] + pair[1:2, :]) * float(CORES * REPS)
     side = dot(pair.astype(BF16), st_ref[...])
-    turned = jnp.transpose(rows_ref[...]).astype(BF16)
-    columns = by_lanes(eye(HIDDEN), row_pair(*two(hidden))).astype(BF16)
-    mixture = dot(jnp.concatenate([turned, columns], axis=1), half_ref[...])
-    values = jnp.sum(mixture * tt_ref[...].astype(F32), axis=0, keepdims=True)
+    rows = jnp.concatenate([rows_ref[...].astype(BF16), row_pair(*two(hidden))], axis=0)
+    mixture = dot(rows, tt_ref[...])
+    side = side + mixture[HALF:, :]
+    values = jnp.sum(mixture[0:HALF, :] * half_ref[...].astype(F32), axis=0, keepdims=True)
     values = (values + side[0:1, :] + side[1:2, :]) * (1.0 / TOTAL)
     packed = jnp.concatenate([values[:, 0:OWN_SLOTS], values[:, OWN_SLOTS:]], axis=0).astype(BF16)
     for p in range(CORES * REPS):
@@ -272,7 +271,7 @@
     values = row_sum(parts_ref, vec_ref[0:1, :])
     vec_out_ref[...] = vec_ref[...]
     vec_out_ref[5:6, :] = values
-    grad, visible, hidden = pull(values, st_ref[...], half_ref[0:HALF, :], tt_ref[...])
+    grad, visible, hidden = pull(values, st_ref[...], half_ref[...], tt_ref[...])
     store_rows(out_ref, 0, grad, tail_of(visible, hidden, iteration_scalars(vec_ref, values)))
 
 
@@ -339,7 +338,7 @@
     out_ref[...] = out
 
 
-def last_kernel(rep_ref, in_ref, sc_ref, r0_ref, r1_ref, r2_ref, v0_ref, v1_ref, v2_ref, vis_ref, hid_ref, mat_ref):
+def last_kernel(in_ref, sc_ref, r0_ref, r1_ref, r2_ref, v0_ref, v1_ref, v2_ref, vis_ref, hid_ref, mat_ref):
     summed = jnp.sum(in_ref[...], axis=0, keepdims=True)
     scalars = [summed[:, i : i + 1] for i in range(SCALARS)]
     keep = [sc_ref[0:1, i : i + 1] for i in range(10)]
@@ -357,7 +356,7 @@
     small = sum(w * ref[...] for w, ref in zip(weights, (v0_ref, v1_ref, v2_ref)))
     hid_ref[...] = small[0]
     a, b = iota((SITES, TAIL), 0), iota((SITES, TAIL), 1)
-    pick = jnp.where(a == 32 * rep_ref[0] + b, 1.0, 0.0).astype(F32)
+    pick = jnp.where(a == 32 * lax.axis_index("rep") + b, 1.0, 0.0).astype(F32)
     vis_ref[...] = dot(small[:, 0:SITES], pick, precision=HIGH)[1, 0:32]
 
 
@@ -365,13 +364,12 @@
     return jax.ShapeDtypeStruct(dims, dtype)
 
 
-def call(kernel, outs, name, n_in, smem=(), scratch=()):
+def call(kernel, outs, name, n_in, scratch=()):
     vmem = pl.BlockSpec(memory_space=pltpu.VMEM)
-    scalar = pl.BlockSpec(memory_space=pltpu.SMEM)
     return pl.pallas_call(
         kernel,
         out_shape=outs,
-        in_specs=[scalar if i in smem else vmem for i in range(n_in)],
+        in_specs=[vmem] * n_in,
         out_specs=[vmem] * len(outs),
         scratch_shapes=list(scratch),
         name=name,
@@ -383,10 +381,6 @@
     return lax.all_to_all(blocks, axes, split_axis=0, concat_axis=0, tiled=True)
 
 
-def place(axis):
-    return lax.axis_index(axis)[None].astype(jnp.int32)
-
-
 def in_hbm(*arrays):
     return [pltpu.with_memory_space_constraint(a, pltpu.HBM) for a in arrays]
 
@@ -395,16 +389,15 @@
     rows = shape((OWNERS, ROWS, WIDE), BF16)
     own = shape((ROWS, WIDE))
     vec_shape = shape((8, SLOTS))
-    core, rep = place("chain_2"), place("rep")
     shared, turned = call(
-        share_kernel, [shape((CORES, SIDE, OWN_SLOTS), BF16), shape((HIDDEN, SIDE), BF16)], "share", 8, smem=(0, 1, 2)
-    )(counts, core, rep, *in_hbm(spins, energies, accepted, weights, hidden_bias))
-    spins_and_acts = [shape((n, SLOTS), BF16) for n in (SITES, HALF + 16, HIDDEN)]
+        share_kernel, [shape((CORES, SIDE, OWN_SLOTS), BF16), shape((HIDDEN, SIDE), BF16)], "share", 6
+    )(counts, *in_hbm(spins, energies, accepted, weights, hidden_bias))
+    spins_and_acts = [shape((n, SLOTS), BF16) for n in (SITES, HALF, HIDDEN)]
     *operands, vec, blocks = call(
         setup_kernel,
         [*spins_and_acts, vec_shape, shape((OWNERS, 2 * ROWS, WIDE), BF16)],
-        "setup", 3, smem=(0,),
-    )(core, exchanged(shared, "chain_2"), turned)
+        "setup", 2,
+    )(exchanged(shared, "chain_2"), turned)
     res, ones, vec, copies = call(first_own_kernel, [own, own, vec_shape, rows], "first_own", 2)(
         exchanged(blocks, CHIPS), vec
     )
@@ -432,8 +425,8 @@
     smalls.append(small)
     (sums,) = call(last_scalars_kernel, [shape((OWNERS, TAIL))], "last_scalars", 2)(parts, vec)
     return call(
-        last_kernel, [shape((32,)), shape((HIDDEN,)), shape((ROWS, HIDDEN))], "last", 9, smem=(0,)
-    )(rep, exchanged(sums, CHIPS), sc, *residuals, *smalls)
+        last_kernel, [shape((32,)), shape((HIDDEN,)), shape((ROWS, HIDDEN))], "last", 8
+    )(exchanged(sums, CHIPS), sc, *residuals, *smalls)
 
 
 def solution(mesh):

time: 174 us -> 171 us (0.983)
  Pallas kernels: 16.9 us -> 14.5 us
    pallas_call x3, Pallas kernels: 5.32 us -> 3.01 us  [push(): call(push_kernel, [shape((CORES * REPS, 2, OWN_SLOTS), BF16), shape((8, H...]
where the time goes in v6:
time: 171 us; the launch traced here: 170 us
  blocking collectives  154 us (90%)
  Pallas kernels  14.5 us (8%)
    all_to_all x11, blocking collectives, exchanged(): return lax.all_to_all(blocks, axes, split_axis=0, concat_axis=0, tiled=True)  154 us
    pallas_call x2, Pallas kernels, per_device(): call(pull_kernel, [vec_shape, rows], 'pull', 5)(parts, vec, *operands)  3.61 us

profile of v6, /device:TPU:1, one launch (start us, length us, event | category | flops | bytes accessed | tf_op | source)
XLA Modules:
  0.0 170.0 jit_solution(10829376562941005009)
XLA Ops:
  1.3 2.0 %share.1 = (bf16[2,272,1536]{2,1,0:T(8,128)(2,1)S(1)}, bf16[512,272]{1,0:T(8,128)(2,1)S(1)}) custom-call(s32[1]{0:T(128)S(6)} %copy.10.count_ref, bf16[1536,256]{1,0:T(8,128)(2,1)} %spins_ref.1, bf16[1536]{0:T(1024)(128)(2,1)} %energy_ref.1, s32[1,1536]{1,0:T(1,128)} %accepted_ref.1, bf16[256,512]{1,0:T(8,128)(2,1)} %weights_ref.1, bf16[512]{0:T(512)(128)(2,1)} %bias_ref.1), custom_call_target="tpu_custom_call" | custom-call | tf_op jit(solution)/shard_map/share/pallas_call | solution.py:392
  3.3 11.5 %all_to_all.61.shared_ref = bf16[2,272,1536]{2,1,0:T(8,128)(2,1)S(1)} all-to-all(bf16[2,272,1536]{2,1,0:T(8,128)(2,1)S(1)} %get-tuple-element.34), channel_id=1, replica_groups=mesh['chain_0'=4,'chain_1'=8,'chain_2'=2,'rep'=8] {'chain_2'}, dimensions={0} | all-to-all | bytes 3342336 | tf_op jit(solution)/shard_map/all_to_all | solution.py:381
  14.8 3.1 %setup.1 = (bf16[256,3072]{1,0:T(8,128)(2,1)S(1)}, bf16[128,3072]{1,0:T(8,128)(2,1)S(1)}, bf16[512,3072]{1,0:T(8,128)(2,1)S(1)}, f32[8,3072]{1,0:T(8,128)S(1)}, bf16[32,8,640]{2,1,0:T(8,128)(2,1)S(1)}) custom-call(bf16[2,272,1536]{2,1,0:T(8,128)(2,1)S(1)} %all_to_all.61.shared_ref, bf16[512,272]{1,0:T(8,128)(2,1)S(1)} %get-tuple-element.35.turned_ref), custom_call_target="tpu_custom_call" | custom-call | tf_op jit(solution)/shard_map/setup/pallas_call | solution.py:396
  17.9 17.8 %all_to_all.62.in_ref = bf16[32,8,640]{2,1,0:T(8,128)(2,1)S(1)} all-to-all(bf16[32,8,640]{2,1,0:T(8,128)(2,1)S(1)} %get-tuple-element.36), channel_id=1, replica_groups=mesh['chain_0'=4,'chain_1'=8,'chain_2'=2,'rep'=8] {'chain_0','chain_1'}, dimensions={0} | all-to-all | bytes 655360 | tf_op jit(solution)/shard_map/all_to_all | solution.py:381
  35.7 0.3 first_own.1
  36.0 16.6 %all_to_all.63.in_ref = bf16[32,4,640]{2,1,0:T(4,128)(2,1)S(1)} all-to-all(bf16[32,4,640]{2,1,0:T(4,128)(2,1)S(1)} %get-tuple-element.38), channel_id=1, replica_groups=mesh['chain_0'=4,'chain_1'=8,'chain_2'=2,'rep'=8] {'chain_0','chain_1'}, dimensions={0} | all-to-all | bytes 327680 | tf_op jit(solution)/shard_map/all_to_all | solution.py:381
  52.6 1.0 push.3
  53.6 16.8 %all_to_all.64.parts_ref = bf16[16,2,1536]{2,1,0:T(2,128)(2,1)S(1)} all-to-all(bf16[16,2,1536]{2,1,0:T(2,128)(2,1)S(1)} %get-tuple-element.42), channel_id=1, replica_groups=mesh['chain_0'=4,'chain_1'=8,'chain_2'=2,'rep'=8] {'chain_2','rep'}, dimensions={0} | all-to-all | bytes 196608 | tf_op jit(solution)/shard_map/all_to_all | solution.py:381
  70.4 1.8 %pull.2 = (f32[8,3072]{1,0:T(8,128)S(1)}, bf16[32,4,640]{2,1,0:T(4,128)(2,1)S(1)}) custom-call(bf16[16,2,1536]{2,1,0:T(2,128)(2,1)S(1)} %all_to_all.64.parts_ref, f32[8,3072]{1,0:T(8,128)S(1)} %get-tuple-element.43.vec_ref, bf16[256,3072]{1,0:T(8,128)(2,1)S(1)} %get-tuple-element.39.st_ref, bf16[128,3072]{1,0:T(8,128)(2,1)S(1)} %get-tuple-element.40.half_ref, ...), custom_call_target="tpu_custom_call" | custom-call | tf_op jit(solution)/shard_map/pull/pallas_call | solution.py:415
  72.2 12.7 %all_to_all.65.refs_0_ = bf16[32,4,640]{2,1,0:T(4,128)(2,1)S(1)} all-to-all(bf16[32,4,640]{2,1,0:T(4,128)(2,1)S(1)} %get-tuple-element.44), channel_id=1, replica_groups=mesh['chain_0'=4,'chain_1'=8,'chain_2'=2,'rep'=8] {'chain_0','chain_1'}, dimensions={0} | all-to-all | bytes 327680 | tf_op jit(solution)/shard_map/all_to_all | solution.py:381
  84.9 0.4 own.2
  85.3 13.1 %all_to_all.66.in_ref = bf16[32,4,640]{2,1,0:T(4,128)(2,1)S(1)} all-to-all(bf16[32,4,640]{2,1,0:T(4,128)(2,1)S(1)} %get-tuple-element.48), channel_id=1, replica_groups=mesh['chain_0'=4,'chain_1'=8,'chain_2'=2,'rep'=8] {'chain_0','chain_1'}, dimensions={0} | all-to-all | bytes 327680 | tf_op jit(solution)/shard_map/all_to_all | solution.py:381
  98.4 1.0 push.4
  99.4 14.1 %all_to_all.67.parts_ref = bf16[16,2,1536]{2,1,0:T(2,128)(2,1)S(1)} all-to-all(bf16[16,2,1536]{2,1,0:T(2,128)(2,1)S(1)} %get-tuple-element.49), channel_id=1, replica_groups=mesh['chain_0'=4,'chain_1'=8,'chain_2'=2,'rep'=8] {'chain_2','rep'}, dimensions={0} | all-to-all | bytes 196608 | tf_op jit(solution)/shard_map/all_to_all | solution.py:381
  113.5 1.8 %pull.3 = (f32[8,3072]{1,0:T(8,128)S(1)}, bf16[32,4,640]{2,1,0:T(4,128)(2,1)S(1)}) custom-call(bf16[16,2,1536]{2,1,0:T(2,128)(2,1)S(1)} %all_to_all.67.parts_ref, f32[8,3072]{1,0:T(8,128)S(1)} %get-tuple-element.50.vec_ref, bf16[256,3072]{1,0:T(8,128)(2,1)S(1)} %get-tuple-element.39.st_ref, bf16[128,3072]{1,0:T(8,128)(2,1)S(1)} %get-tuple-element.40.half_ref, ...), custom_call_target="tpu_custom_call" | custom-call | tf_op jit(solution)/shard_map/pull/pallas_call | solution.py:415
  115.3 12.6 %all_to_all.68.refs_0_ = bf16[32,4,640]{2,1,0:T(4,128)(2,1)S(1)} all-to-all(bf16[32,4,640]{2,1,0:T(4,128)(2,1)S(1)} %get-tuple-element.51), channel_id=1, replica_groups=mesh['chain_0'=4,'chain_1'=8,'chain_2'=2,'rep'=8] {'chain_0','chain_1'}, dimensions={0} | all-to-all | bytes 327680 | tf_op jit(solution)/shard_map/all_to_all | solution.py:381
  127.8 0.6 own.3
  128.4 13.1 %all_to_all.69.in_ref = bf16[32,4,640]{2,1,0:T(4,128)(2,1)S(1)} all-to-all(bf16[32,4,640]{2,1,0:T(4,128)(2,1)S(1)} %get-tuple-element.57), channel_id=1, replica_groups=mesh['chain_0'=4,'chain_1'=8,'chain_2'=2,'rep'=8] {'chain_0','chain_1'}, dimensions={0} | all-to-all | bytes 327680 | tf_op jit(solution)/shard_map/all_to_all | solution.py:381
  141.5 1.0 push.5
  142.5 14.1 %all_to_all.70.parts_ref = bf16[16,2,1536]{2,1,0:T(2,128)(2,1)S(1)} all-to-all(bf16[16,2,1536]{2,1,0:T(2,128)(2,1)S(1)} %get-tuple-element.58), channel_id=1, replica_groups=mesh['chain_0'=4,'chain_1'=8,'chain_2'=2,'rep'=8] {'chain_2','rep'}, dimensions={0} | all-to-all | bytes 196608 | tf_op jit(solution)/shard_map/all_to_all | solution.py:381
  156.5 0.2 last_scalars.1
  156.8 12.0 %all_to_all.71 = f32[32,1,128]{2,1,0:T(1,128)S(1)} all-to-all(f32[32,1,128]{2,1,0:T(1,128)S(1)} %bitcast.5), channel_id=1, replica_groups=mesh['chain_0'=4,'chain_1'=8,'chain_2'=2,'rep'=8] {'chain_0','chain_1'}, dimensions={0} | all-to-all | bytes 32768 | tf_op jit(solution)/shard_map/all_to_all | solution.py:381
  168.7 1.2 last.1

commit v7 on v6

--- a/solution.py
+++ b/solution.py
@@ -82,13 +82,19 @@
     return jnp.where(sub == 0, high.astype(F32), jnp.where(sub == 1, low.astype(F32), 0.0)).astype(BF16)
 
 
-def pull(weights, st, half, tt):
-    high, low = two(weights)
-    spins = half.astype(F32)
-    pair = row_pair(high, low)
-    rows = [(spins * high.astype(F32)).astype(BF16), (spins * low.astype(F32)).astype(BF16), pair]
-    grad = by_lanes(jnp.concatenate(rows, axis=0), tt)
-    visible = by_lanes(st, pair)
+def part_of(core):
+    return slice(core * OWN_SLOTS, (core + 1) * OWN_SLOTS)
+
+
+def pull(weights, operands):
+    grad, visible = 0.0, 0.0
+    for core, (st_ref, half_ref, tt_ref) in enumerate(operands):
+        high, low = two(weights[:, part_of(core)])
+        spins = half_ref[...].astype(F32)
+        pair = row_pair(high, low)
+        rows = [(spins * high.astype(F32)).astype(BF16), (spins * low.astype(F32)).astype(BF16), pair]
+        grad = grad + by_lanes(jnp.concatenate(rows, axis=0), tt_ref[...])
+        visible = visible + by_lanes(st_ref[0:SITES, :], pair)
     hidden = grad[2 * HALF : 2 * HALF + 1] + grad[2 * HALF + 1 : 2 * HALF + 2]
     return grad[:HALF] + grad[HALF : 2 * HALF], visible[:, 0:1] + visible[:, 1:2], hidden
 
@@ -140,7 +146,7 @@
 
 
 def share_kernel(
-    count_ref, spins_ref, energy_ref, accepted_ref, weights_ref, bias_ref, out_ref, turned_ref
+    count_ref, spins_ref, energy_ref, accepted_ref, weights_ref, bias_ref, st_ref, turned_ref
 ):
     accepted = accepted_ref[...]
     live = iota((16, OWN_SLOTS), 1) < count_ref[...].reshape(1, 1)
@@ -149,38 +155,39 @@
     table = by_lanes(major, minor)
     mask = jnp.concatenate([table[h : h + 1, :] for h in range(OWN_SLOTS // TAIL)], axis=1)
     energy = (energy_ref[...].astype(F32).reshape(1, OWN_SLOTS) - ENERGY_MID) * mask
-    sites = by_lanes(eye(SITES), spins_ref[...]).astype(BF16)
-    extra = row_pair(energy.astype(BF16), mask.astype(BF16))
-    for core in range(CORES):
-        out_ref[core, 0:SITES, :] = sites
-        out_ref[core, SITES:SIDE, :] = extra
+    st_ref[0:SITES, :] = by_lanes(eye(SITES), spins_ref[...]).astype(BF16)
+    st_ref[SITES:SIDE, :] = row_pair(energy.astype(BF16), mask.astype(BF16))
     bias_row = jnp.broadcast_to(bias_ref[...].astype(F32).reshape(1, HIDDEN), (16, HIDDEN))
     turned_ref[:, 0:SITES] = by_lanes(eye(HIDDEN), weights_ref[...]).astype(BF16)
     turned_ref[:, SITES:SIDE] = by_lanes(eye(HIDDEN), bias_row.astype(BF16)).astype(BF16)
 
 
-def setup_kernel(shared_ref, turned_ref, st_ref, half_ref, tt_ref, vec_ref, out_ref):
-    turned = turned_ref[:, 0:SITES]
-    bias = turned_ref[:, SITES : SITES + 1].astype(F32)
+def acts_kernel(st_ref, turned_ref, half_ref, tt_ref):
+    sites = st_ref[0:SITES, :]
     row, site = iota((HALF, SITES), 0), iota((HALF, SITES), 1)
     mine = jnp.where(site == 8 * (row >> 2) + 4 * lax.axis_index("chain_2") + (row & 3), 1.0, 0.0).astype(BF16)
+    half_ref[...] = dot(mine, sites).astype(BF16)
+    preact = turned_ref[:, SITES : SITES + 1].astype(F32) + dot(turned_ref[:, 0:SITES], sites)
+    tt_ref[...] = jnp.tanh(preact).astype(BF16)
+
+
+def setup_kernel(st0_ref, half0_ref, tt0_ref, st1_ref, turned_ref, half1_ref, tt1_ref, vec_ref, out_ref):
+    acts_kernel(st1_ref, turned_ref, half1_ref, tt1_ref)
     vec_ref[...] = jnp.zeros((8, SLOTS), F32)
-    for core in range(CORES):
-        part = slice(core * OWN_SLOTS, (core + 1) * OWN_SLOTS)
-        sites = shared_ref[core, 0:SITES, :]
-        extra = shared_ref[core, SITES:SIDE, :].astype(F32)
-        st_ref[:, part] = sites
-        half_ref[:, part] = dot(mine, sites).astype(BF16)
-        tt_ref[:, part] = jnp.tanh(bias + dot(turned, sites)).astype(BF16)
-        vec_ref[0:1, part] = extra[1:2, :]
-        vec_ref[1:2, part] = extra[0:1, :]
-    mask, energy = vec_ref[0:1, :], vec_ref[1:2, :]
-    spins = half_ref[...].astype(F32)
-    pair = row_pair(energy.astype(BF16), mask.astype(BF16))
-    rows = [(spins * energy).astype(BF16), (spins * mask).astype(BF16), pair]
-    grad = by_lanes(jnp.concatenate(rows, axis=0), tt_ref[...])
-    visible, hidden = by_lanes(st_ref[...], pair), grad[2 * HALF :]
-    for k, scalars in enumerate(((total(energy),), ())):
+    grad, visible, sums = 0.0, 0.0, 0.0
+    for core, (st_ref, half_ref, tt_ref) in enumerate(((st0_ref, half0_ref, tt0_ref), (st1_ref, half1_ref, tt1_ref))):
+        pair = st_ref[SITES:SIDE, :]
+        extra = pair.astype(F32)
+        energy, mask = extra[0:1, :], extra[1:2, :]
+        vec_ref[0:1, part_of(core)] = mask
+        vec_ref[1:2, part_of(core)] = energy
+        spins = half_ref[...].astype(F32)
+        rows = [(spins * energy).astype(BF16), (spins * mask).astype(BF16), pair]
+        grad = grad + by_lanes(jnp.concatenate(rows, axis=0), tt_ref[...])
+        visible = visible + by_lanes(st_ref[0:SITES, :], pair)
+        sums = sums + total(energy)
+    hidden = grad[2 * HALF :]
+    for k, scalars in enumerate(((sums,), ())):
         tail = tail_of(visible[:, k : k + 1], hidden[k : k + 1], scalars)
         store_rows(out_ref, ROWS * k, grad[HALF * k : HALF * (k + 1)], tail)
 
@@ -219,7 +226,7 @@
     store_copies(copies_ref, res_ref[...])
 
 
-def push_kernel(in_ref, st_ref, half_ref, tt_ref, parts_ref, small_ref, rows_ref, tail_ref):
+def push_kernel(in_ref, st0_ref, half0_ref, tt0_ref, st1_ref, half1_ref, tt1_ref, parts_ref, small_ref, rows_ref, tail_ref):
     for c in range(OWNERS):
         block = in_ref[c].astype(F32)
         rows_ref[ROWS * c : ROWS * (c + 1), :] = block[:, 0:HIDDEN]
@@ -236,15 +243,19 @@
     small_ref[...] = jnp.zeros((8, HIDDEN), F32)
     small_ref[0:1, :] = hidden * float(CORES)
     small_ref[1:2, 0:SITES] = (pair[0:1, :] + pair[1:2, :]) * float(CORES * REPS)
-    side = dot(pair.astype(BF16), st_ref[...])
     rows = jnp.concatenate([rows_ref[...].astype(BF16), row_pair(*two(hidden))], axis=0)
-    mixture = dot(rows, tt_ref[...])
-    side = side + mixture[HALF:, :]
-    values = jnp.sum(mixture[0:HALF, :] * half_ref[...].astype(F32), axis=0, keepdims=True)
-    values = (values + side[0:1, :] + side[1:2, :]) * (1.0 / TOTAL)
-    packed = jnp.concatenate([values[:, 0:OWN_SLOTS], values[:, OWN_SLOTS:]], axis=0).astype(BF16)
-    for p in range(CORES * REPS):
-        parts_ref[p] = packed
+    halves = []
+    for st_ref, half_ref, tt_ref in ((st0_ref, half0_ref, tt0_ref), (st1_ref, half1_ref, tt1_ref)):
+        mixture = dot(rows, tt_ref[...])
+        side = dot(pair.astype(BF16), st_ref[0:SITES, :]) + mixture[HALF:, :]
+        values = jnp.sum(mixture[0:HALF, :] * half_ref[...].astype(F32), axis=0, keepdims=True)
+        halves.append((values + side[0:1, :] + side[1:2, :]) * (1.0 / TOTAL))
+    own = lax.axis_index("chain_2")
+    straight, swapped = jnp.concatenate(halves, axis=0), jnp.concatenate(halves[::-1], axis=0)
+    for core in range(CORES):
+        packed = jnp.where(own == core, straight, swapped).astype(BF16)
+        for y in range(REPS):
+            parts_ref[core * REPS + y] = packed
 
 
 def row_sum(parts_ref, mask):
@@ -267,11 +278,11 @@
     )
 
 
-def pull_kernel(parts_ref, vec_ref, st_ref, half_ref, tt_ref, vec_out_ref, out_ref):
+def pull_kernel(parts_ref, vec_ref, st0_ref, half0_ref, tt0_ref, st1_ref, half1_ref, tt1_ref, vec_out_ref, out_ref):
     values = row_sum(parts_ref, vec_ref[0:1, :])
     vec_out_ref[...] = vec_ref[...]
     vec_out_ref[5:6, :] = values
-    grad, visible, hidden = pull(values, st_ref[...], half_ref[...], tt_ref[...])
+    grad, visible, hidden = pull(values, ((st0_ref, half0_ref, tt0_ref), (st1_ref, half1_ref, tt1_ref)))
     store_rows(out_ref, 0, grad, tail_of(visible, hidden, iteration_scalars(vec_ref, values)))
 
 
@@ -389,22 +400,23 @@
     rows = shape((OWNERS, ROWS, WIDE), BF16)
     own = shape((ROWS, WIDE))
     vec_shape = shape((8, SLOTS))
-    shared, turned = call(
-        share_kernel, [shape((CORES, SIDE, OWN_SLOTS), BF16), shape((HIDDEN, SIDE), BF16)], "share", 6
-    )(counts, *in_hbm(spins, energies, accepted, weights, hidden_bias))
-    spins_and_acts = [shape((n, SLOTS), BF16) for n in (SITES, HALF, HIDDEN)]
-    *operands, vec, blocks = call(
-        setup_kernel,
-        [*spins_and_acts, vec_shape, shape((OWNERS, 2 * ROWS, WIDE), BF16)],
-        "setup", 2,
-    )(exchanged(shared, "chain_2"), turned)
+    st0, turned = call(share_kernel, [shape((SIDE, OWN_SLOTS), BF16), shape((HIDDEN, SIDE), BF16)], "share", 6)(
+        counts, *in_hbm(spins, energies, accepted, weights, hidden_bias)
+    )
+    st1 = lax.ppermute(st0, "chain_2", [(0, 1), (1, 0)])
+    half_and_acts = [shape((n, OWN_SLOTS), BF16) for n in (HALF, HIDDEN)]
+    half0, tt0 = call(acts_kernel, half_and_acts, "acts", 2)(st0, turned)
+    half1, tt1, vec, blocks = call(
+        setup_kernel, [*half_and_acts, vec_shape, shape((OWNERS, 2 * ROWS, WIDE), BF16)], "setup", 5
+    )(st0, half0, tt0, st1, turned)
+    operands = (st0, half0, tt0, st1, half1, tt1)
     res, ones, vec, copies = call(first_own_kernel, [own, own, vec_shape, rows], "first_own", 2)(
         exchanged(blocks, CHIPS), vec
     )
 
     def push(copies):
         parts, small = call(
-            push_kernel, [shape((CORES * REPS, 2, OWN_SLOTS), BF16), shape((8, HIDDEN))], "push", 4,
+            push_kernel, [shape((CORES * REPS, 2, OWN_SLOTS), BF16), shape((8, HIDDEN))], "push", 7,
             scratch=[pltpu.VMEM((HALF, HIDDEN), F32), pltpu.VMEM((SITES, TAIL), F32)],
         )(exchanged(copies, CHIPS), *operands)
         return exchanged(parts, UNITS), small
@@ -412,7 +424,7 @@
     state, smalls, residuals = (), [], [res]
     for iteration in range(2):
         parts, small = push(copies)
-        vec, blocks = call(pull_kernel, [vec_shape, rows], "pull", 5)(parts, vec, *operands)
+        vec, blocks = call(pull_kernel, [vec_shape, rows], "pull", 8)(parts, vec, *operands)
         first = iteration == 0
         sc, vec, res, *state, copies = call(
             lambda *refs, first=first: own_kernel(first, *refs),

time: 171 us -> 170 us (level)
  blocking collectives: 154 us -> 143 us
  starting transfers between devices: 0 us -> 8.74 us
    all_to_all x11 -> x10, blocking collectives: 154 us -> 143 us  [exchanged(): return lax.all_to_all(blocks, axes, split_axis=0, concat_axis=0, tiled=True)]
    ppermute x0 -> x1, starting transfers between devices: none -> 8.74 us  [per_device(): st1 = lax.ppermute(st0, 'chain_2', [(0, 1), (1, 0)])]
    pallas_call x4 -> x5, Pallas kernels: 8.72 us -> 8.79 us  [the longest x2 3.61 us: per_device(): call(pull_kernel, [vec_shape, rows], 'pull', 8)(parts, vec, *operands)]
  transfers between devices with their start and end apart: 0 -> 1, of which waited for: 0 -> 1; matrix products, arithmetic and copies ran while one was open for 0% -> 0% of each run, Pallas kernels for 0% -> 0%
where the time goes in v7:
time: 170 us; the launch traced here: 169 us
  blocking collectives  143 us (84%)
  Pallas kernels  14.6 us (9%)
  starting transfers between devices  8.74 us (5%)
    all_to_all x10, blocking collectives, exchanged(): return lax.all_to_all(blocks, axes, split_axis=0, concat_axis=0, tiled=True)  143 us
    ppermute x1, starting transfers between devices, per_device(): st1 = lax.ppermute(st0, 'chain_2', [(0, 1), (1, 0)])  8.74 us
    pallas_call x2, Pallas kernels, per_device(): call(pull_kernel, [vec_shape, rows], 'pull', 8)(parts, vec, *operands)  3.61 us
  transfers between devices with their start and end apart: 1, of which 1 were waited for; matrix products, arithmetic and copies ran while one was open for 0% of the time, Pallas kernels for 0%

profile of v7, /device:TPU:1, one launch (start us, length us, event | category | flops | bytes accessed | tf_op | source)
XLA Modules:
  0.0 168.6 jit_solution(17825707743098275158)
XLA Ops:
  1.3 2.0 %share.1 = (bf16[272,1536]{1,0:T(8,128)(2,1)S(1)}, bf16[512,272]{1,0:T(8,128)(2,1)S(1)}) custom-call(s32[1]{0:T(128)S(6)} %copy.10.count_ref, bf16[1536,256]{1,0:T(8,128)(2,1)} %spins_ref.1, bf16[1536]{0:T(1024)(128)(2,1)} %energy_ref.1, s32[1,1536]{1,0:T(1,128)} %accepted_ref.1, bf16[256,512]{1,0:T(8,128)(2,1)} %weights_ref.1, bf16[512]{0:T(512)(128)(2,1)} %bias_ref.1), custom_call_target="tpu_custom_call" | custom-call | tf_op jit(solution)/shard_map/share/pallas_call | solution.py:403
  3.3 8.7 %collective-permute-start = (bf16[272,1536]{1,0:T(8,128)(2,1)S(1)}, bf16[272,1536]{1,0:T(8,128)(2,1)S(1)}, u32[]{:S(2)}, u32[]{:S(2)}) collective-permute-start(bf16[272,1536]{1,0:T(8,128)(2,1)S(1)} %get-tuple-element.35.st_ref.st0_ref), channel_id=1, source_target_pairs={{0,8},{8,0},{1,9},{9,1},{2,10},{10,2},{3,11},{11,3},{4,12},{12,4},... | collective-permute-start | bytes 2506760 | tf_op jit(solution)/shard_map/ppermute | solution.py:406
  12.1 0.7 acts.1
  12.8 1.2 collective-permute-done.st1_ref
  14.0 2.4 %setup.1 = (bf16[128,1536]{1,0:T(8,128)(2,1)S(1)}, bf16[512,1536]{1,0:T(8,128)(2,1)S(1)}, f32[8,3072]{1,0:T(8,128)S(1)}, bf16[32,8,640]{2,1,0:T(8,128)(2,1)S(1)}) custom-call(bf16[272,1536]{1,0:T(8,128)(2,1)S(1)} %get-tuple-element.35.st_ref.st0_ref, bf16[128,1536]{1,0:T(8,128)(2,1)S(1)} %get-tuple-element.37.half0_ref, ...), custom_call_target="tpu_custom_call" | custom-call | tf_op jit(solution)/shard_map/setup/pallas_call | solution.py:409
  16.5 17.8 %all_to_all.56.in_ref = bf16[32,8,640]{2,1,0:T(8,128)(2,1)S(1)} all-to-all(bf16[32,8,640]{2,1,0:T(8,128)(2,1)S(1)} %get-tuple-element.39), channel_id=1, replica_groups=mesh['chain_0'=4,'chain_1'=8,'chain_2'=2,'rep'=8] {'chain_0','chain_1'}, dimensions={0} | all-to-all | bytes 655360 | tf_op jit(solution)/shard_map/all_to_all | solution.py:392
  34.3 0.3 first_own.1
  34.6 16.6 %all_to_all.57.in_ref = bf16[32,4,640]{2,1,0:T(4,128)(2,1)S(1)} all-to-all(bf16[32,4,640]{2,1,0:T(4,128)(2,1)S(1)} %get-tuple-element.41), channel_id=1, replica_groups=mesh['chain_0'=4,'chain_1'=8,'chain_2'=2,'rep'=8] {'chain_0','chain_1'}, dimensions={0} | all-to-all | bytes 327680 | tf_op jit(solution)/shard_map/all_to_all | solution.py:392
  51.2 1.0 push.3
  52.2 16.8 %all_to_all.58.parts_ref = bf16[16,2,1536]{2,1,0:T(2,128)(2,1)S(1)} all-to-all(bf16[16,2,1536]{2,1,0:T(2,128)(2,1)S(1)} %get-tuple-element.44), channel_id=1, replica_groups=mesh['chain_0'=4,'chain_1'=8,'chain_2'=2,'rep'=8] {'chain_2','rep'}, dimensions={0} | all-to-all | bytes 196608 | tf_op jit(solution)/shard_map/all_to_all | solution.py:392
  69.0 1.8 %pull.2 = (f32[8,3072]{1,0:T(8,128)S(1)}, bf16[32,4,640]{2,1,0:T(4,128)(2,1)S(1)}) custom-call(bf16[16,2,1536]{2,1,0:T(2,128)(2,1)S(1)} %all_to_all.58.parts_ref, f32[8,3072]{1,0:T(8,128)S(1)} %get-tuple-element.45.vec_ref, bf16[272,1536]{1,0:T(8,128)(2,1)S(1)} %get-tuple-element.35.st_ref.st0_ref, bf16[128,1536]{1,0:T(8,128)(2,1)S(1)} %get-tuple-element.37.half0_ref, ...), custom_call_target="tpu_custom_call" | custom-call | tf_op jit(solution)/shard_map/pull/pallas_call | solution.py:427
  70.8 12.7 %all_to_all.59.refs_0_ = bf16[32,4,640]{2,1,0:T(4,128)(2,1)S(1)} all-to-all(bf16[32,4,640]{2,1,0:T(4,128)(2,1)S(1)} %get-tuple-element.46), channel_id=1, replica_groups=mesh['chain_0'=4,'chain_1'=8,'chain_2'=2,'rep'=8] {'chain_0','chain_1'}, dimensions={0} | all-to-all | bytes 327680 | tf_op jit(solution)/shard_map/all_to_all | solution.py:392
  83.5 0.4 own.2
  83.9 13.1 %all_to_all.60.in_ref = bf16[32,4,640]{2,1,0:T(4,128)(2,1)S(1)} all-to-all(bf16[32,4,640]{2,1,0:T(4,128)(2,1)S(1)} %get-tuple-element.50), channel_id=1, replica_groups=mesh['chain_0'=4,'chain_1'=8,'chain_2'=2,'rep'=8] {'chain_0','chain_1'}, dimensions={0} | all-to-all | bytes 327680 | tf_op jit(solution)/shard_map/all_to_all | solution.py:392
  97.0 1.0 push.4
  98.0 14.1 %all_to_all.61.parts_ref = bf16[16,2,1536]{2,1,0:T(2,128)(2,1)S(1)} all-to-all(bf16[16,2,1536]{2,1,0:T(2,128)(2,1)S(1)} %get-tuple-element.51), channel_id=1, replica_groups=mesh['chain_0'=4,'chain_1'=8,'chain_2'=2,'rep'=8] {'chain_2','rep'}, dimensions={0} | all-to-all | bytes 196608 | tf_op jit(solution)/shard_map/all_to_all | solution.py:392
  112.1 1.8 %pull.3 = (f32[8,3072]{1,0:T(8,128)S(1)}, bf16[32,4,640]{2,1,0:T(4,128)(2,1)S(1)}) custom-call(bf16[16,2,1536]{2,1,0:T(2,128)(2,1)S(1)} %all_to_all.61.parts_ref, f32[8,3072]{1,0:T(8,128)S(1)} %get-tuple-element.52.vec_ref, bf16[272,1536]{1,0:T(8,128)(2,1)S(1)} %get-tuple-element.35.st_ref.st0_ref, bf16[128,1536]{1,0:T(8,128)(2,1)S(1)} %get-tuple-element.37.half0_ref, ...), custom_call_target="tpu_custom_call" | custom-call | tf_op jit(solution)/shard_map/pull/pallas_call | solution.py:427
  113.9 12.6 %all_to_all.62.refs_0_ = bf16[32,4,640]{2,1,0:T(4,128)(2,1)S(1)} all-to-all(bf16[32,4,640]{2,1,0:T(4,128)(2,1)S(1)} %get-tuple-element.53), channel_id=1, replica_groups=mesh['chain_0'=4,'chain_1'=8,'chain_2'=2,'rep'=8] {'chain_0','chain_1'}, dimensions={0} | all-to-all | bytes 327680 | tf_op jit(solution)/shard_map/all_to_all | solution.py:392
  126.4 0.6 own.3
  127.0 13.1 %all_to_all.63.in_ref = bf16[32,4,640]{2,1,0:T(4,128)(2,1)S(1)} all-to-all(bf16[32,4,640]{2,1,0:T(4,128)(2,1)S(1)} %get-tuple-element.59), channel_id=1, replica_groups=mesh['chain_0'=4,'chain_1'=8,'chain_2'=2,'rep'=8] {'chain_0','chain_1'}, dimensions={0} | all-to-all | bytes 327680 | tf_op jit(solution)/shard_map/all_to_all | solution.py:392
  140.1 1.0 push.5
  141.1 14.1 %all_to_all.64.parts_ref = bf16[16,2,1536]{2,1,0:T(2,128)(2,1)S(1)} all-to-all(bf16[16,2,1536]{2,1,0:T(2,128)(2,1)S(1)} %get-tuple-element.60), channel_id=1, replica_groups=mesh['chain_0'=4,'chain_1'=8,'chain_2'=2,'rep'=8] {'chain_2','rep'}, dimensions={0} | all-to-all | bytes 196608 | tf_op jit(solution)/shard_map/all_to_all | solution.py:392
  155.2 0.2 last_scalars.1
  155.4 12.0 %all_to_all.65 = f32[32,1,128]{2,1,0:T(1,128)S(1)} all-to-all(f32[32,1,128]{2,1,0:T(1,128)S(1)} %bitcast.5), channel_id=1, replica_groups=mesh['chain_0'=4,'chain_1'=8,'chain_2'=2,'rep'=8] {'chain_0','chain_1'}, dimensions={0} | all-to-all | bytes 32768 | tf_op jit(solution)/shard_map/all_to_all | solution.py:392
  167.4 1.2 last.1
Async XLA Ops:
  3.3 10.7 %collective-permute-start = (bf16[272,1536]{1,0:T(8,128)(2,1)S(1)}, bf16[272,1536]{1,0:T(8,128)(2,1)S(1)}, u32[]{:S(2)}, u32[]{:S(2)}) collective-permute-start(bf16[272,1536]{1,0:T(8,128)(2,1)S(1)} %get-tuple-element.35.st_ref.st0_ref), channel_id=1, source_target_pairs={{0,8},{8,0},{1,9},{9,1},{2,10},{10,2},{3,11},{11,3},{4,12},{12,4},... | collective-permute-start | bytes 2506760 | tf_op jit(solution)/shard_map/ppermute | solution.py:406

commit v8 on v7

--- a/solution.py
+++ b/solution.py
@@ -131,13 +131,15 @@
     return tail + second
 
 
-def store_copies(out_ref, rows):
+def store_copies(out_ref, rows, ones):
     lane = iota((ROWS, TAIL), 1)
     tail = rows[:, HIDDEN:WIDE]
     tail = jnp.where((lane == 0) | (lane == 2), tail * (1.0 / (CORES * REPS)), jnp.where((lane >= 8) & (lane < 24), tail * (1.0 / CORES), 0.0))
     high = tail.astype(BF16).astype(F32)
     low = tail - high
     packed = high + jnp.where(lane < 8, pltpu.roll(low, 1, 1), jnp.where(lane >= 24, pltpu.roll(low, 16, 1), 0.0))
+    mean = total(rows[:, 0:HIDDEN] * ones[:, 0:HIDDEN]) * (1.0 / (TOTAL * TOTAL))
+    packed = packed + jnp.where(iota((ROWS, TAIL), 0) == 1, scalar_lanes((mean,)), 0.0)
     packed = packed.astype(BF16)
     coupling = rows[:, 0:HIDDEN].astype(BF16)
     for c in range(OWNERS):
@@ -223,7 +225,7 @@
     vec_out_ref[0:1, :] = mask
     vec_out_ref[1:2, :] = raw - mean * mask
     vec_out_ref[2:8, :] = jnp.zeros((6, SLOTS), F32)
-    store_copies(copies_ref, res_ref[...])
+    store_copies(copies_ref, res_ref[...], ones)
 
 
 def push_kernel(in_ref, st0_ref, half0_ref, tt0_ref, st1_ref, half1_ref, tt1_ref, parts_ref, small_ref, rows_ref, tail_ref):
@@ -243,6 +245,7 @@
     small_ref[...] = jnp.zeros((8, HIDDEN), F32)
     small_ref[0:1, :] = hidden * float(CORES)
     small_ref[1:2, 0:SITES] = (pair[0:1, :] + pair[1:2, :]) * float(CORES * REPS)
+    mean = total(jnp.where(((row & 7) == 1) & (lane >= FIRST), tail, 0.0))
     rows = jnp.concatenate([rows_ref[...].astype(BF16), row_pair(*two(hidden))], axis=0)
     halves = []
     for st_ref, half_ref, tt_ref in ((st0_ref, half0_ref, tt0_ref), (st1_ref, half1_ref, tt1_ref)):
@@ -252,17 +255,20 @@
         halves.append((values + side[0:1, :] + side[1:2, :]) * (1.0 / TOTAL))
     own = lax.axis_index("chain_2")
     straight, swapped = jnp.concatenate(halves, axis=0), jnp.concatenate(halves[::-1], axis=0)
+    extra = jnp.where(iota((2, TAIL), 0) == 0, scalar_lanes((mean,)), 0.0).astype(BF16)
     for core in range(CORES):
         packed = jnp.where(own == core, straight, swapped).astype(BF16)
         for y in range(REPS):
-            parts_ref[core * REPS + y] = packed
+            parts_ref[core * REPS + y, :, 0:OWN_SLOTS] = packed
+            parts_ref[core * REPS + y, :, OWN_SLOTS:] = extra
 
 
 def row_sum(parts_ref, mask):
     values = parts_ref[0].astype(F32)
     for p in range(1, CORES * REPS):
         values = values + parts_ref[p].astype(F32)
-    return jnp.concatenate([values[0:1, :], values[1:2, :]], axis=1) * mask
+    mean = total(values[0:1, OWN_SLOTS:])
+    return (jnp.concatenate([values[0:1, 0:OWN_SLOTS], values[1:2, 0:OWN_SLOTS]], axis=1) - mean) * mask
 
 
 def iteration_scalars(vec_ref, values):
@@ -337,7 +343,7 @@
     vec_out[3:4, :] = o_dir
     vec_out[4:5, :] = direction if first else vec_ref[4:5, :]
     vec_out[5:8, :] = jnp.zeros((3, SLOTS), F32)
-    store_copies(copies_ref, res_out[...])
+    store_copies(copies_ref, res_out[...], ones_ref[...])
 
 
 def last_scalars_kernel(parts_ref, vec_ref, out_ref):
@@ -416,7 +422,7 @@
 
     def push(copies):
         parts, small = call(
-            push_kernel, [shape((CORES * REPS, 2, OWN_SLOTS), BF16), shape((8, HIDDEN))], "push", 7,
+            push_kernel, [shape((CORES * REPS, 2, OWN_SLOTS + TAIL), BF16), shape((8, HIDDEN))], "push", 7,
             scratch=[pltpu.VMEM((HALF, HIDDEN), F32), pltpu.VMEM((SITES, TAIL), F32)],
         )(exchanged(copies, CHIPS), *operands)
         return exchanged(parts, UNITS), small

time: 170 us -> 171 us (level)
  no operation moved by 1% of the time
where the time goes in v8:
time: 171 us; the launch traced here: 170 us
  blocking collectives  143 us (84%)
  Pallas kernels  15.2 us (9%)
  starting transfers between devices  8.75 us (5%)
    all_to_all x10, blocking collectives, exchanged(): return lax.all_to_all(blocks, axes, split_axis=0, concat_axis=0, tiled=True)  143 us
    ppermute x1, starting transfers between devices, per_device(): st1 = lax.ppermute(st0, 'chain_2', [(0, 1), (1, 0)])  8.75 us
    pallas_call x2, Pallas kernels, per_device(): call(pull_kernel, [vec_shape, rows], 'pull', 8)(parts, vec, *operands)  3.93 us
  transfers between devices with their start and end apart: 1, of which 1 were waited for; matrix products, arithmetic and copies ran while one was open for 0% of the time, Pallas kernels for 0%

profile of v8, /device:TPU:1, one launch (start us, length us, event | category | flops | bytes accessed | tf_op | source)
XLA Modules:
  0.0 169.5 jit_solution(8434606094224391849)
XLA Ops:
  1.3 2.0 %share.1 = (bf16[272,1536]{1,0:T(8,128)(2,1)S(1)}, bf16[512,272]{1,0:T(8,128)(2,1)S(1)}) custom-call(s32[1]{0:T(128)S(6)} %copy.10.count_ref, bf16[1536,256]{1,0:T(8,128)(2,1)} %spins_ref.1, bf16[1536]{0:T(1024)(128)(2,1)} %energy_ref.1, s32[1,1536]{1,0:T(1,128)} %accepted_ref.1, bf16[256,512]{1,0:T(8,128)(2,1)} %weights_ref.1, bf16[512]{0:T(512)(128)(2,1)} %bias_ref.1), custom_call_target="tpu_custom_call" | custom-call | tf_op jit(solution)/shard_map/share/pallas_call | solution.py:409
  3.3 8.7 %collective-permute-start = (bf16[272,1536]{1,0:T(8,128)(2,1)S(1)}, bf16[272,1536]{1,0:T(8,128)(2,1)S(1)}, u32[]{:S(2)}, u32[]{:S(2)}) collective-permute-start(bf16[272,1536]{1,0:T(8,128)(2,1)S(1)} %get-tuple-element.35.st_ref.st0_ref), channel_id=1, source_target_pairs={{0,8},{8,0},{1,9},{9,1},{2,10},{10,2},{3,11},{11,3},{4,12},{12,4},... | collective-permute-start | bytes 2506760 | tf_op jit(solution)/shard_map/ppermute | solution.py:412
  12.1 0.7 acts.1
  12.8 1.3 collective-permute-done.st1_ref
  14.0 2.4 %setup.1 = (bf16[128,1536]{1,0:T(8,128)(2,1)S(1)}, bf16[512,1536]{1,0:T(8,128)(2,1)S(1)}, f32[8,3072]{1,0:T(8,128)S(1)}, bf16[32,8,640]{2,1,0:T(8,128)(2,1)S(1)}) custom-call(bf16[272,1536]{1,0:T(8,128)(2,1)S(1)} %get-tuple-element.35.st_ref.st0_ref, bf16[128,1536]{1,0:T(8,128)(2,1)S(1)} %get-tuple-element.37.half0_ref, ...), custom_call_target="tpu_custom_call" | custom-call | tf_op jit(solution)/shard_map/setup/pallas_call | solution.py:415
  16.5 17.8 %all_to_all.56.in_ref = bf16[32,8,640]{2,1,0:T(8,128)(2,1)S(1)} all-to-all(bf16[32,8,640]{2,1,0:T(8,128)(2,1)S(1)} %get-tuple-element.39), channel_id=1, replica_groups=mesh['chain_0'=4,'chain_1'=8,'chain_2'=2,'rep'=8] {'chain_0','chain_1'}, dimensions={0} | all-to-all | bytes 655360 | tf_op jit(solution)/shard_map/all_to_all | solution.py:398
  34.3 0.3 first_own.1
  34.6 16.6 %all_to_all.57.in_ref = bf16[32,4,640]{2,1,0:T(4,128)(2,1)S(1)} all-to-all(bf16[32,4,640]{2,1,0:T(4,128)(2,1)S(1)} %get-tuple-element.41), channel_id=1, replica_groups=mesh['chain_0'=4,'chain_1'=8,'chain_2'=2,'rep'=8] {'chain_0','chain_1'}, dimensions={0} | all-to-all | bytes 327680 | tf_op jit(solution)/shard_map/all_to_all | solution.py:398
  51.2 1.0 push.3
  52.2 16.8 %all_to_all.58.parts_ref = bf16[16,2,1664]{2,1,0:T(2,128)(2,1)S(1)} all-to-all(bf16[16,2,1664]{2,1,0:T(2,128)(2,1)S(1)} %get-tuple-element.44), channel_id=1, replica_groups=mesh['chain_0'=4,'chain_1'=8,'chain_2'=2,'rep'=8] {'chain_2','rep'}, dimensions={0} | all-to-all | bytes 212992 | tf_op jit(solution)/shard_map/all_to_all | solution.py:398
  69.1 2.0 %pull.2 = (f32[8,3072]{1,0:T(8,128)S(1)}, bf16[32,4,640]{2,1,0:T(4,128)(2,1)S(1)}) custom-call(bf16[16,2,1664]{2,1,0:T(2,128)(2,1)S(1)} %all_to_all.58.parts_ref, f32[8,3072]{1,0:T(8,128)S(1)} %get-tuple-element.45.vec_ref, bf16[272,1536]{1,0:T(8,128)(2,1)S(1)} %get-tuple-element.35.st_ref.st0_ref, bf16[128,1536]{1,0:T(8,128)(2,1)S(1)} %get-tuple-element.37.half0_ref, ...), custom_call_target="tpu_custom_call" | custom-call | tf_op jit(solution)/shard_map/pull/pallas_call | solution.py:433
  71.0 12.7 %all_to_all.59.refs_0_ = bf16[32,4,640]{2,1,0:T(4,128)(2,1)S(1)} all-to-all(bf16[32,4,640]{2,1,0:T(4,128)(2,1)S(1)} %get-tuple-element.46), channel_id=1, replica_groups=mesh['chain_0'=4,'chain_1'=8,'chain_2'=2,'rep'=8] {'chain_0','chain_1'}, dimensions={0} | all-to-all | bytes 327680 | tf_op jit(solution)/shard_map/all_to_all | solution.py:398
  83.7 0.5 own.2
  84.2 13.1 %all_to_all.60.in_ref = bf16[32,4,640]{2,1,0:T(4,128)(2,1)S(1)} all-to-all(bf16[32,4,640]{2,1,0:T(4,128)(2,1)S(1)} %get-tuple-element.50), channel_id=1, replica_groups=mesh['chain_0'=4,'chain_1'=8,'chain_2'=2,'rep'=8] {'chain_0','chain_1'}, dimensions={0} | all-to-all | bytes 327680 | tf_op jit(solution)/shard_map/all_to_all | solution.py:398
  97.3 1.0 push.4
  98.3 14.2 %all_to_all.61.parts_ref = bf16[16,2,1664]{2,1,0:T(2,128)(2,1)S(1)} all-to-all(bf16[16,2,1664]{2,1,0:T(2,128)(2,1)S(1)} %get-tuple-element.51), channel_id=1, replica_groups=mesh['chain_0'=4,'chain_1'=8,'chain_2'=2,'rep'=8] {'chain_2','rep'}, dimensions={0} | all-to-all | bytes 212992 | tf_op jit(solution)/shard_map/all_to_all | solution.py:398
  112.5 2.0 %pull.3 = (f32[8,3072]{1,0:T(8,128)S(1)}, bf16[32,4,640]{2,1,0:T(4,128)(2,1)S(1)}) custom-call(bf16[16,2,1664]{2,1,0:T(2,128)(2,1)S(1)} %all_to_all.61.parts_ref, f32[8,3072]{1,0:T(8,128)S(1)} %get-tuple-element.52.vec_ref, bf16[272,1536]{1,0:T(8,128)(2,1)S(1)} %get-tuple-element.35.st_ref.st0_ref, bf16[128,1536]{1,0:T(8,128)(2,1)S(1)} %get-tuple-element.37.half0_ref, ...), custom_call_target="tpu_custom_call" | custom-call | tf_op jit(solution)/shard_map/pull/pallas_call | solution.py:433
  114.5 12.6 %all_to_all.62.refs_0_ = bf16[32,4,640]{2,1,0:T(4,128)(2,1)S(1)} all-to-all(bf16[32,4,640]{2,1,0:T(4,128)(2,1)S(1)} %get-tuple-element.53), channel_id=1, replica_groups=mesh['chain_0'=4,'chain_1'=8,'chain_2'=2,'rep'=8] {'chain_0','chain_1'}, dimensions={0} | all-to-all | bytes 327680 | tf_op jit(solution)/shard_map/all_to_all | solution.py:398
  127.0 0.6 own.3
  127.7 13.0 %all_to_all.63.in_ref = bf16[32,4,640]{2,1,0:T(4,128)(2,1)S(1)} all-to-all(bf16[32,4,640]{2,1,0:T(4,128)(2,1)S(1)} %get-tuple-element.59), channel_id=1, replica_groups=mesh['chain_0'=4,'chain_1'=8,'chain_2'=2,'rep'=8] {'chain_0','chain_1'}, dimensions={0} | all-to-all | bytes 327680 | tf_op jit(solution)/shard_map/all_to_all | solution.py:398
  140.7 1.0 push.5
  141.7 14.2 %all_to_all.64.parts_ref = bf16[16,2,1664]{2,1,0:T(2,128)(2,1)S(1)} all-to-all(bf16[16,2,1664]{2,1,0:T(2,128)(2,1)S(1)} %get-tuple-element.60), channel_id=1, replica_groups=mesh['chain_0'=4,'chain_1'=8,'chain_2'=2,'rep'=8] {'chain_2','rep'}, dimensions={0} | all-to-all | bytes 212992 | tf_op jit(solution)/shard_map/all_to_all | solution.py:398
  156.0 0.3 last_scalars.1
  156.3 12.0 %all_to_all.65 = f32[32,1,128]{2,1,0:T(1,128)S(1)} all-to-all(f32[32,1,128]{2,1,0:T(1,128)S(1)} %bitcast.5), channel_id=1, replica_groups=mesh['chain_0'=4,'chain_1'=8,'chain_2'=2,'rep'=8] {'chain_0','chain_1'}, dimensions={0} | all-to-all | bytes 32768 | tf_op jit(solution)/shard_map/all_to_all | solution.py:398
  168.3 1.2 last.1
Async XLA Ops:
  3.3 10.7 %collective-permute-start = (bf16[272,1536]{1,0:T(8,128)(2,1)S(1)}, bf16[272,1536]{1,0:T(8,128)(2,1)S(1)}, u32[]{:S(2)}, u32[]{:S(2)}) collective-permute-start(bf16[272,1536]{1,0:T(8,128)(2,1)S(1)} %get-tuple-element.35.st_ref.st0_ref), channel_id=1, source_target_pairs={{0,8},{8,0},{1,9},{9,1},{2,10},{10,2},{3,11},{11,3},{4,12},{12,4},... | collective-permute-start | bytes 2506760 | tf_op jit(solution)/shard_map/ppermute | solution.py:412

commit v9 on v8

--- a/solution.py
+++ b/solution.py
@@ -252,23 +252,20 @@
         mixture = dot(rows, tt_ref[...])
         side = dot(pair.astype(BF16), st_ref[0:SITES, :]) + mixture[HALF:, :]
         values = jnp.sum(mixture[0:HALF, :] * half_ref[...].astype(F32), axis=0, keepdims=True)
-        halves.append((values + side[0:1, :] + side[1:2, :]) * (1.0 / TOTAL))
+        halves.append((values + side[0:1, :] + side[1:2, :]) * (1.0 / TOTAL) - mean)
     own = lax.axis_index("chain_2")
     straight, swapped = jnp.concatenate(halves, axis=0), jnp.concatenate(halves[::-1], axis=0)
-    extra = jnp.where(iota((2, TAIL), 0) == 0, scalar_lanes((mean,)), 0.0).astype(BF16)
     for core in range(CORES):
         packed = jnp.where(own == core, straight, swapped).astype(BF16)
         for y in range(REPS):
-            parts_ref[core * REPS + y, :, 0:OWN_SLOTS] = packed
-            parts_ref[core * REPS + y, :, OWN_SLOTS:] = extra
+            parts_ref[core * REPS + y] = packed
 
 
 def row_sum(parts_ref, mask):
     values = parts_ref[0].astype(F32)
     for p in range(1, CORES * REPS):
         values = values + parts_ref[p].astype(F32)
-    mean = total(values[0:1, OWN_SLOTS:])
-    return (jnp.concatenate([values[0:1, 0:OWN_SLOTS], values[1:2, 0:OWN_SLOTS]], axis=1) - mean) * mask
+    return jnp.concatenate([values[0:1, :], values[1:2, :]], axis=1) * mask
 
 
 def iteration_scalars(vec_ref, values):
@@ -422,7 +419,7 @@
 
     def push(copies):
         parts, small = call(
-            push_kernel, [shape((CORES * REPS, 2, OWN_SLOTS + TAIL), BF16), shape((8, HIDDEN))], "push", 7,
+            push_kernel, [shape((CORES * REPS, 2, OWN_SLOTS), BF16), shape((8, HIDDEN))], "push", 7,
             scratch=[pltpu.VMEM((HALF, HIDDEN), F32), pltpu.VMEM((SITES, TAIL), F32)],
         )(exchanged(copies, CHIPS), *operands)
         return exchanged(parts, UNITS), small

time: 171 us -> 170 us (level)
  no operation moved by 1% of the time
where the time goes in v9:
time: 170 us; the launch traced here: 169 us
  blocking collectives  143 us (84%)
  Pallas kernels  14.8 us (9%)
  starting transfers between devices  8.75 us (5%)
    all_to_all x10, blocking collectives, exchanged(): return lax.all_to_all(blocks, axes, split_axis=0, concat_axis=0, tiled=True)  143 us
    ppermute x1, starting transfers between devices, per_device(): st1 = lax.ppermute(st0, 'chain_2', [(0, 1), (1, 0)])  8.75 us
    pallas_call x2, Pallas kernels, per_device(): call(pull_kernel, [vec_shape, rows], 'pull', 8)(parts, vec, *operands)  3.61 us
  transfers between devices with their start and end apart: 1, of which 1 were waited for; matrix products, arithmetic and copies ran while one was open for 0% of the time, Pallas kernels for 0%

profile of v9, /device:TPU:1, one launch (start us, length us, event | category | flops | bytes accessed | tf_op | source)
XLA Modules:
  0.0 168.8 jit_solution(13813138194001803704)
XLA Ops:
  1.3 2.0 %share.1 = (bf16[272,1536]{1,0:T(8,128)(2,1)S(1)}, bf16[512,272]{1,0:T(8,128)(2,1)S(1)}) custom-call(s32[1]{0:T(128)S(6)} %copy.10.count_ref, bf16[1536,256]{1,0:T(8,128)(2,1)} %spins_ref.1, bf16[1536]{0:T(1024)(128)(2,1)} %energy_ref.1, s32[1,1536]{1,0:T(1,128)} %accepted_ref.1, bf16[256,512]{1,0:T(8,128)(2,1)} %weights_ref.1, bf16[512]{0:T(512)(128)(2,1)} %bias_ref.1), custom_call_target="tpu_custom_call" | custom-call | tf_op jit(solution)/shard_map/share/pallas_call | solution.py:406
  3.3 8.7 %collective-permute-start = (bf16[272,1536]{1,0:T(8,128)(2,1)S(1)}, bf16[272,1536]{1,0:T(8,128)(2,1)S(1)}, u32[]{:S(2)}, u32[]{:S(2)}) collective-permute-start(bf16[272,1536]{1,0:T(8,128)(2,1)S(1)} %get-tuple-element.35.st_ref.st0_ref), channel_id=1, source_target_pairs={{0,8},{8,0},{1,9},{9,1},{2,10},{10,2},{3,11},{11,3},{4,12},{12,4},... | collective-permute-start | bytes 2506760 | tf_op jit(solution)/shard_map/ppermute | solution.py:409
  12.1 0.7 acts.1
  12.8 1.3 collective-permute-done.st1_ref
  14.0 2.4 %setup.1 = (bf16[128,1536]{1,0:T(8,128)(2,1)S(1)}, bf16[512,1536]{1,0:T(8,128)(2,1)S(1)}, f32[8,3072]{1,0:T(8,128)S(1)}, bf16[32,8,640]{2,1,0:T(8,128)(2,1)S(1)}) custom-call(bf16[272,1536]{1,0:T(8,128)(2,1)S(1)} %get-tuple-element.35.st_ref.st0_ref, bf16[128,1536]{1,0:T(8,128)(2,1)S(1)} %get-tuple-element.37.half0_ref, ...), custom_call_target="tpu_custom_call" | custom-call | tf_op jit(solution)/shard_map/setup/pallas_call | solution.py:412
  16.5 17.8 %all_to_all.56.in_ref = bf16[32,8,640]{2,1,0:T(8,128)(2,1)S(1)} all-to-all(bf16[32,8,640]{2,1,0:T(8,128)(2,1)S(1)} %get-tuple-element.39), channel_id=1, replica_groups=mesh['chain_0'=4,'chain_1'=8,'chain_2'=2,'rep'=8] {'chain_0','chain_1'}, dimensions={0} | all-to-all | bytes 655360 | tf_op jit(solution)/shard_map/all_to_all | solution.py:395
  34.3 0.3 first_own.1
  34.6 16.6 %all_to_all.57.in_ref = bf16[32,4,640]{2,1,0:T(4,128)(2,1)S(1)} all-to-all(bf16[32,4,640]{2,1,0:T(4,128)(2,1)S(1)} %get-tuple-element.41), channel_id=1, replica_groups=mesh['chain_0'=4,'chain_1'=8,'chain_2'=2,'rep'=8] {'chain_0','chain_1'}, dimensions={0} | all-to-all | bytes 327680 | tf_op jit(solution)/shard_map/all_to_all | solution.py:395
  51.2 1.0 push.3
  52.2 16.8 %all_to_all.58.parts_ref = bf16[16,2,1536]{2,1,0:T(2,128)(2,1)S(1)} all-to-all(bf16[16,2,1536]{2,1,0:T(2,128)(2,1)S(1)} %get-tuple-element.44), channel_id=1, replica_groups=mesh['chain_0'=4,'chain_1'=8,'chain_2'=2,'rep'=8] {'chain_2','rep'}, dimensions={0} | all-to-all | bytes 196608 | tf_op jit(solution)/shard_map/all_to_all | solution.py:395
  69.0 1.8 %pull.2 = (f32[8,3072]{1,0:T(8,128)S(1)}, bf16[32,4,640]{2,1,0:T(4,128)(2,1)S(1)}) custom-call(bf16[16,2,1536]{2,1,0:T(2,128)(2,1)S(1)} %all_to_all.58.parts_ref, f32[8,3072]{1,0:T(8,128)S(1)} %get-tuple-element.45.vec_ref, bf16[272,1536]{1,0:T(8,128)(2,1)S(1)} %get-tuple-element.35.st_ref.st0_ref, bf16[128,1536]{1,0:T(8,128)(2,1)S(1)} %get-tuple-element.37.half0_ref, ...), custom_call_target="tpu_custom_call" | custom-call | tf_op jit(solution)/shard_map/pull/pallas_call | solution.py:430
  70.8 12.7 %all_to_all.59.refs_0_ = bf16[32,4,640]{2,1,0:T(4,128)(2,1)S(1)} all-to-all(bf16[32,4,640]{2,1,0:T(4,128)(2,1)S(1)} %get-tuple-element.46), channel_id=1, replica_groups=mesh['chain_0'=4,'chain_1'=8,'chain_2'=2,'rep'=8] {'chain_0','chain_1'}, dimensions={0} | all-to-all | bytes 327680 | tf_op jit(solution)/shard_map/all_to_all | solution.py:395
  83.5 0.5 own.2
  84.0 13.1 %all_to_all.60.in_ref = bf16[32,4,640]{2,1,0:T(4,128)(2,1)S(1)} all-to-all(bf16[32,4,640]{2,1,0:T(4,128)(2,1)S(1)} %get-tuple-element.50), channel_id=1, replica_groups=mesh['chain_0'=4,'chain_1'=8,'chain_2'=2,'rep'=8] {'chain_0','chain_1'}, dimensions={0} | all-to-all | bytes 327680 | tf_op jit(solution)/shard_map/all_to_all | solution.py:395
  97.1 1.0 push.4
  98.1 14.1 %all_to_all.61.parts_ref = bf16[16,2,1536]{2,1,0:T(2,128)(2,1)S(1)} all-to-all(bf16[16,2,1536]{2,1,0:T(2,128)(2,1)S(1)} %get-tuple-element.51), channel_id=1, replica_groups=mesh['chain_0'=4,'chain_1'=8,'chain_2'=2,'rep'=8] {'chain_2','rep'}, dimensions={0} | all-to-all | bytes 196608 | tf_op jit(solution)/shard_map/all_to_all | solution.py:395
  112.2 1.8 %pull.3 = (f32[8,3072]{1,0:T(8,128)S(1)}, bf16[32,4,640]{2,1,0:T(4,128)(2,1)S(1)}) custom-call(bf16[16,2,1536]{2,1,0:T(2,128)(2,1)S(1)} %all_to_all.61.parts_ref, f32[8,3072]{1,0:T(8,128)S(1)} %get-tuple-element.52.vec_ref, bf16[272,1536]{1,0:T(8,128)(2,1)S(1)} %get-tuple-element.35.st_ref.st0_ref, bf16[128,1536]{1,0:T(8,128)(2,1)S(1)} %get-tuple-element.37.half0_ref, ...), custom_call_target="tpu_custom_call" | custom-call | tf_op jit(solution)/shard_map/pull/pallas_call | solution.py:430
  114.0 12.6 %all_to_all.62.refs_0_ = bf16[32,4,640]{2,1,0:T(4,128)(2,1)S(1)} all-to-all(bf16[32,4,640]{2,1,0:T(4,128)(2,1)S(1)} %get-tuple-element.53), channel_id=1, replica_groups=mesh['chain_0'=4,'chain_1'=8,'chain_2'=2,'rep'=8] {'chain_0','chain_1'}, dimensions={0} | all-to-all | bytes 327680 | tf_op jit(solution)/shard_map/all_to_all | solution.py:395
  126.6 0.6 own.3
  127.2 13.0 %all_to_all.63.in_ref = bf16[32,4,640]{2,1,0:T(4,128)(2,1)S(1)} all-to-all(bf16[32,4,640]{2,1,0:T(4,128)(2,1)S(1)} %get-tuple-element.59), channel_id=1, replica_groups=mesh['chain_0'=4,'chain_1'=8,'chain_2'=2,'rep'=8] {'chain_0','chain_1'}, dimensions={0} | all-to-all | bytes 327680 | tf_op jit(solution)/shard_map/all_to_all | solution.py:395
  140.2 1.0 push.5
  141.3 14.1 %all_to_all.64.parts_ref = bf16[16,2,1536]{2,1,0:T(2,128)(2,1)S(1)} all-to-all(bf16[16,2,1536]{2,1,0:T(2,128)(2,1)S(1)} %get-tuple-element.60), channel_id=1, replica_groups=mesh['chain_0'=4,'chain_1'=8,'chain_2'=2,'rep'=8] {'chain_2','rep'}, dimensions={0} | all-to-all | bytes 196608 | tf_op jit(solution)/shard_map/all_to_all | solution.py:395
  155.3 0.2 last_scalars.1
  155.6 12.0 %all_to_all.65 = f32[32,1,128]{2,1,0:T(1,128)S(1)} all-to-all(f32[32,1,128]{2,1,0:T(1,128)S(1)} %bitcast.5), channel_id=1, replica_groups=mesh['chain_0'=4,'chain_1'=8,'chain_2'=2,'rep'=8] {'chain_0','chain_1'}, dimensions={0} | all-to-all | bytes 32768 | tf_op jit(solution)/shard_map/all_to_all | solution.py:395
  167.6 1.2 last.1
Async XLA Ops:
  3.3 10.7 %collective-permute-start = (bf16[272,1536]{1,0:T(8,128)(2,1)S(1)}, bf16[272,1536]{1,0:T(8,128)(2,1)S(1)}, u32[]{:S(2)}, u32[]{:S(2)}) collective-permute-start(bf16[272,1536]{1,0:T(8,128)(2,1)S(1)} %get-tuple-element.35.st_ref.st0_ref), channel_id=1, source_target_pairs={{0,8},{8,0},{1,9},{9,1},{2,10},{10,2},{3,11},{11,3},{4,12},{12,4},... | collective-permute-start | bytes 2506760 | tf_op jit(solution)/shard_map/ppermute | solution.py:409
